TPU v7x, 32 devices: a whole 2x2x4 slice. The times are simulated.
32 devices in a mesh: seq: 8 (over z, x), ctx: 4 (over y, core).
Axes of the slice: x: 2, y: 2, z: 4, core: 2. Of those that a mesh axis runs over, the one named last changes fastest.
Arguments:
- tokens: bfloat16 [8, 1024, 1024], P('seq', 'ctx'), may hold values from -6 to 6
- lengths: int32 [8], P('seq'), may hold values from 256 to 1024, as said below
- cotangent: bfloat16 [8, 1024, 1024], P('seq', 'ctx'), may hold values from -6 to 6
- ln1_gain: bfloat16 [1024], P(('seq', 'ctx')), may hold values from 0.5 to 1.5
- ln1_bias: bfloat16 [1024], P(('seq', 'ctx')), may hold values from -3 to 3
- qkv_weight: bfloat16 [1024, 3072], P(('seq', 'ctx')), may hold values from -0.1875 to 0.1875
- query_bias: bfloat16 [1024], P(('seq', 'ctx')), may hold values from -3 to 3
- value_bias: bfloat16 [1024], P(('seq', 'ctx')), may hold values from -3 to 3
- out_weight: bfloat16 [1024, 1024], P(('seq', 'ctx')), may hold values from -0.375 to 0.375
- out_bias: bfloat16 [1024], P(('seq', 'ctx')), may hold values from -3 to 3
- ln2_gain: bfloat16 [1024], P(('seq', 'ctx')), may hold values from 0.5 to 1.5
- ln2_bias: bfloat16 [1024], P(('seq', 'ctx')), may hold values from -3 to 3
- up_weight: bfloat16 [1024, 4096], P(('seq', 'ctx')), may hold values from -0.1875 to 0.1875
- up_bias: bfloat16 [4096], P(('seq', 'ctx')), may hold values from -3 to 3
- down_weight: bfloat16 [4096, 1024], P(('seq', 'ctx')), may hold values from -0.09375 to 0.09375
- down_bias: bfloat16 [1024], P(('seq', 'ctx')), may hold values from -3 to 3
Outputs:
- output: bfloat16 [8, 1024, 1024], P('seq', 'ctx')
- input_grad: float32 [8, 1024, 1024], P('seq', 'ctx')
- ln1_gain_grad: float32 [1024], P(('seq', 'ctx'))
- ln1_bias_grad: float32 [1024], P(('seq', 'ctx'))
- qkv_weight_grad: float32 [1024, 3072], P(('seq', 'ctx'))
- query_bias_grad: float32 [1024], P(('seq', 'ctx'))
- value_bias_grad: float32 [1024], P(('seq', 'ctx'))
- out_weight_grad: float32 [1024, 1024], P(('seq', 'ctx'))
- out_bias_grad: float32 [1024], P(('seq', 'ctx'))
- ln2_gain_grad: float32 [1024], P(('seq', 'ctx'))
- ln2_bias_grad: float32 [1024], P(('seq', 'ctx'))
- up_weight_grad: float32 [1024, 4096], P(('seq', 'ctx'))
- up_bias_grad: float32 [4096], P(('seq', 'ctx'))
- down_weight_grad: float32 [4096, 1024], P(('seq', 'ctx'))
- down_bias_grad: float32 [1024], P(('seq', 'ctx'))
- stats: float32 [8, 3], P('seq')
Inputs may be any that keep to these rules, and one draw needn't show every extreme that they name: `lengths`: some sequence has length 1024 and another 1024 // 4 in every draw.
All inputs are finite; a program needn't handle non-finite values.
Results may differ from a plain program's by a relative error of at most 0.013.
Values may be sent and summed in bfloat16 or wider, within the bound.
A program may use at most 192 MiB of HBM per device.

v0:
```python
import jax
import jax.numpy as jnp
from jax import lax
from jax.sharding import PartitionSpec as P

HEADS = 16


epsilon = 1e-05


def normalize(inputs, gain, shift):
    average = jnp.mean(inputs, axis=-1, keepdims=True)
    centred = inputs - average
    variance = jnp.mean(centred * centred, axis=-1, keepdims=True)
    return centred * lax.rsqrt(variance + epsilon) * gain + shift


def gelu_tanh(inputs):
    return jax.nn.gelu(inputs, approximate=True)


def inner_rows(left, right):
    return lax.dot_general(
        left, right, (((0,), (0,)), ((), ())), preferred_element_type=jnp.float32
    )


def outer_cols(left, right):
    return lax.dot_general(
        left, right, (((1,), (1,)), ((), ())), preferred_element_type=jnp.float32
    )


def alibi_scores(query_block, key_block, query_pos, key_pos, slope_block):
    raw = jnp.einsum("qhd,khd->hqk", query_block, key_block, preferred_element_type=jnp.float32)
    offset = (key_pos[None, :] - query_pos[:, None]).astype(jnp.float32)
    scores = raw * query_block.shape[-1] ** (-0.5) + slope_block[:, None, None] * offset[None]
    allowed = key_pos[None, :] <= query_pos[:, None]
    return (scores, allowed)


def score_grads(
    query_block,
    key_block,
    value_block,
    grad_block,
    query_pos,
    key_pos,
    slope_block,
    log_block,
    delta_block,
):
    scores, allowed = alibi_scores(query_block, key_block, query_pos, key_pos, slope_block)
    probs = jnp.where(allowed[None], jnp.exp(scores - log_block[..., None]), 0.0)
    grad_probs = jnp.einsum(
        "qhd,khd->hqk", grad_block, value_block, preferred_element_type=jnp.float32
    )
    delta_block = jnp.sum(probs * grad_probs, axis=-1)
    grad_scores = (probs * (grad_probs - delta_block[..., None])).astype(jnp.bfloat16)
    return (probs, grad_scores, delta_block)


def on_device(
    tokens,
    lengths,
    cotangent,
    ln1_gain,
    ln1_bias,
    qkv_weight,
    query_bias,
    value_bias,
    out_weight,
    out_bias,
    ln2_gain,
    ln2_bias,
    up_weight,
    up_bias,
    down_weight,
    down_bias,
):
    shards = (
        ln1_gain,
        ln1_bias,
        qkv_weight,
        query_bias,
        value_bias,
        out_weight,
        out_bias,
        ln2_gain,
        ln2_bias,
        up_weight,
        up_bias,
        down_weight,
        down_bias,
    )
    row_count = tokens.shape[1]
    model_width = tokens.shape[2]
    head_count = HEADS
    head_width = model_width // head_count
    per_block = 2
    block_count = head_count // per_block
    slot_rows = row_count * lax.axis_size("ctx")
    positions = lax.axis_index("ctx") * row_count + jnp.arange(row_count, dtype=jnp.int32)
    length = lengths[0]
    valid_rows = (positions < length).astype(jnp.float32)[:, None]
    slopes = jnp.exp2(-8.0 * (jnp.arange(head_count, dtype=jnp.float32) + 1.0) / head_count)
    key_positions = jnp.arange(slot_rows, dtype=jnp.int32)
    scale = head_width ** (-0.5)
    full_weights = (
        lax.all_gather(shards[0], ("seq", "ctx"), axis=0, tiled=True),
        lax.all_gather(shards[1], ("seq", "ctx"), axis=0, tiled=True),
        lax.all_gather(shards[2], ("seq", "ctx"), axis=0, tiled=True),
        lax.all_gather(shards[3], ("seq", "ctx"), axis=0, tiled=True),
        lax.all_gather(shards[4], ("seq", "ctx"), axis=0, tiled=True),
        lax.all_gather(shards[5], ("seq", "ctx"), axis=0, tiled=True),
        lax.all_gather(shards[6], ("seq", "ctx"), axis=0, tiled=True),
        lax.all_gather(shards[7], ("seq", "ctx"), axis=0, tiled=True),
        lax.all_gather(shards[8], ("seq", "ctx"), axis=0, tiled=True),
        lax.all_gather(shards[9], ("seq", "ctx"), axis=0, tiled=True),
        lax.all_gather(shards[10], ("seq", "ctx"), axis=0, tiled=True),
        lax.all_gather(shards[11], ("seq", "ctx"), axis=0, tiled=True),
        lax.all_gather(shards[12], ("seq", "ctx"), axis=0, tiled=True),
    )
    (
        gain_one,
        shift_one,
        w_qkv,
        bias_query,
        bias_value,
        w_out,
        bias_out,
        gain_two,
        shift_two,
        w_up,
        bias_up,
        w_down,
        bias_down,
    ) = full_weights

    def pick(array, index):
        return lax.dynamic_slice_in_dim(array, index * per_block, per_block, 1)

    def pick_slopes(index):
        return lax.dynamic_slice_in_dim(slopes, index * per_block, per_block, 0)

    def to_blocks(array):
        return array.transpose(1, 0, 2, 3).reshape(array.shape[1], model_width)

    source = tokens[0].astype(jnp.float32)
    normed_one, back_one = jax.vjp(normalize, source, gain_one, shift_one)
    normed_low = normed_one.astype(jnp.bfloat16)
    mixed = jnp.dot(normed_low, w_qkv, preferred_element_type=jnp.float32)
    query = (mixed[:, :model_width] + bias_query).astype(jnp.bfloat16)
    keys = mixed[:, model_width : 2 * model_width].astype(jnp.bfloat16)
    values = (mixed[:, 2 * model_width :] + bias_value).astype(jnp.bfloat16)
    all_keys, all_values = (
        lax.all_gather(keys, "ctx", axis=0, tiled=True),
        lax.all_gather(values, "ctx", axis=0, tiled=True),
    )
    query_heads = query.reshape(row_count, head_count, head_width)
    key_heads = all_keys.reshape(slot_rows, head_count, head_width)
    value_heads = all_values.reshape(slot_rows, head_count, head_width)

    def forward_block(index):
        scores, allowed = alibi_scores(
            pick(query_heads, index),
            pick(key_heads, index),
            positions,
            key_positions,
            pick_slopes(index),
        )
        masked = jnp.where(allowed[None], scores, -1e30)
        highest = jnp.max(masked, axis=-1)
        total = jnp.sum(jnp.exp(masked - highest[..., None]), axis=-1)
        log_total = highest + jnp.log(total)
        probs = jnp.where(allowed[None], jnp.exp(scores - log_total[..., None]), 0.0)
        block_out = jnp.einsum(
            "hqk,khd->qhd",
            probs.astype(jnp.bfloat16),
            pick(value_heads, index),
            preferred_element_type=jnp.float32,
        )
        return (block_out, log_total)

    head_out, log_totals = lax.map(forward_block, jnp.arange(block_count))
    attended = to_blocks(head_out).astype(jnp.bfloat16)
    branch = jnp.dot(attended, w_out, preferred_element_type=jnp.float32) + bias_out
    resid = source + branch
    normed_two, back_two = jax.vjp(normalize, resid, gain_two, shift_two)
    normed_two_low = normed_two.astype(jnp.bfloat16)
    pre_act = jnp.dot(normed_two_low, w_up, preferred_element_type=jnp.float32) + bias_up
    activated, back_act = jax.vjp(gelu_tanh, pre_act)
    activated_low = activated.astype(jnp.bfloat16)
    ffn = jnp.dot(activated_low, w_down, preferred_element_type=jnp.float32) + bias_down
    output = (valid_rows * (resid + ffn)).astype(jnp.bfloat16)[None]
    squares = jnp.stack(
        [
            jnp.sum(valid_rows * branch * branch),
            jnp.sum(valid_rows * resid * resid),
            jnp.sum(valid_rows * ffn * ffn),
        ]
    )
    totals = lax.psum(squares, "ctx")
    stats = jnp.sqrt(totals / (length.astype(jnp.float32) * model_width))[None]
    w_qkv, w_out, w_up, w_down = (
        lax.all_gather(qkv_weight, ("seq", "ctx"), axis=0, tiled=True),
        lax.all_gather(out_weight, ("seq", "ctx"), axis=0, tiled=True),
        lax.all_gather(up_weight, ("seq", "ctx"), axis=0, tiled=True),
        lax.all_gather(down_weight, ("seq", "ctx"), axis=0, tiled=True),
    )
    grad_out = cotangent[0].astype(jnp.float32) * valid_rows
    grad_ffn = grad_out.astype(jnp.bfloat16)
    grad_down_w = inner_rows(activated_low, grad_ffn)
    grad_down_b = jnp.sum(grad_ffn.astype(jnp.float32), axis=0)
    grad_activated = outer_cols(grad_ffn, w_down)
    (grad_pre,) = back_act(grad_activated)
    grad_pre_low = grad_pre.astype(jnp.bfloat16)
    grad_up_w = inner_rows(normed_two_low, grad_pre_low)
    grad_up_b = jnp.sum(grad_pre_low.astype(jnp.float32), axis=0)
    grad_normed_two = outer_cols(grad_pre_low, w_up)
    grad_resid_norm, grad_gain_two, grad_shift_two = back_two(grad_normed_two)
    grad_resid = grad_out + grad_resid_norm
    grad_branch = grad_resid.astype(jnp.bfloat16)
    grad_out_w = inner_rows(attended, grad_branch)
    grad_out_b = jnp.sum(grad_branch.astype(jnp.float32), axis=0)
    grad_attended = outer_cols(grad_branch, w_out).astype(jnp.bfloat16)
    grad_heads = grad_attended.reshape(row_count, head_count, head_width)

    def backward_block(index):
        query_block = pick(query_heads, index)
        key_block = pick(key_heads, index)
        grad_block = pick(grad_heads, index)
        probs, grad_scores, delta_block = score_grads(
            query_block,
            key_block,
            pick(value_heads, index),
            grad_block,
            positions,
            key_positions,
            pick_slopes(index),
            log_totals[index],
            None,
        )
        grad_query_block = (
            jnp.einsum("hqk,khd->qhd", grad_scores, key_block, preferred_element_type=jnp.float32)
            * scale
        )
        grad_key_block = (
            jnp.einsum("hqk,qhd->khd", grad_scores, query_block, preferred_element_type=jnp.float32)
            * scale
        )
        grad_value_block = jnp.einsum(
            "hqk,qhd->khd",
            probs.astype(jnp.bfloat16),
            grad_block,
            preferred_element_type=jnp.float32,
        )
        return (grad_query_block, grad_key_block, grad_value_block)

    query_parts, key_parts, value_parts = lax.map(backward_block, jnp.arange(block_count))
    grad_query_all = to_blocks(query_parts)
    own_keys, own_values = (
        lax.psum_scatter(
            to_blocks(key_parts).astype(jnp.bfloat16), "ctx", scatter_dimension=0, tiled=True
        ).astype(jnp.float32),
        lax.psum_scatter(
            to_blocks(value_parts).astype(jnp.bfloat16), "ctx", scatter_dimension=0, tiled=True
        ).astype(jnp.float32),
    )
    grad_query_low = grad_query_all.astype(jnp.bfloat16)
    grad_key_low = own_keys.astype(jnp.bfloat16)
    grad_value_low = own_values.astype(jnp.bfloat16)
    grad_mixed = jnp.concatenate([grad_query_low, grad_key_low, grad_value_low], axis=1)
    grad_qkv_w = inner_rows(normed_low, grad_mixed)
    grad_query_bias = jnp.sum(grad_query_low.astype(jnp.float32), axis=0)
    grad_value_bias = jnp.sum(grad_value_low.astype(jnp.float32), axis=0)
    grad_normed_one = outer_cols(grad_mixed, w_qkv)
    grad_source_norm, grad_gain_one, grad_shift_one = back_one(grad_normed_one)
    grad_tokens = (grad_resid + grad_source_norm)[None]
    summed = (
        lax.psum_scatter(
            grad_gain_one.astype(jnp.float32), ("seq", "ctx"), scatter_dimension=0, tiled=True
        ),
        lax.psum_scatter(
            grad_shift_one.astype(jnp.float32), ("seq", "ctx"), scatter_dimension=0, tiled=True
        ),
        lax.psum_scatter(grad_qkv_w, ("seq", "ctx"), scatter_dimension=0, tiled=True),
        lax.psum_scatter(grad_query_bias, ("seq", "ctx"), scatter_dimension=0, tiled=True),
        lax.psum_scatter(grad_value_bias, ("seq", "ctx"), scatter_dimension=0, tiled=True),
        lax.psum_scatter(grad_out_w, ("seq", "ctx"), scatter_dimension=0, tiled=True),
        lax.psum_scatter(grad_out_b, ("seq", "ctx"), scatter_dimension=0, tiled=True),
        lax.psum_scatter(
            grad_gain_two.astype(jnp.float32), ("seq", "ctx"), scatter_dimension=0, tiled=True
        ),
        lax.psum_scatter(
            grad_shift_two.astype(jnp.float32), ("seq", "ctx"), scatter_dimension=0, tiled=True
        ),
        lax.psum_scatter(grad_up_w, ("seq", "ctx"), scatter_dimension=0, tiled=True),
        lax.psum_scatter(grad_up_b, ("seq", "ctx"), scatter_dimension=0, tiled=True),
        lax.psum_scatter(grad_down_w, ("seq", "ctx"), scatter_dimension=0, tiled=True),
        lax.psum_scatter(grad_down_b, ("seq", "ctx"), scatter_dimension=0, tiled=True),
    )
    return (output, grad_tokens) + tuple(summed) + (stats,)


def solution(mesh):
    placed = (
        P("seq", "ctx", None),
        P("seq"),
        P("seq", "ctx", None),
        P(("seq", "ctx")),
        P(("seq", "ctx")),
        P(("seq", "ctx"), None),
        P(("seq", "ctx")),
        P(("seq", "ctx")),
        P(("seq", "ctx"), None),
        P(("seq", "ctx")),
        P(("seq", "ctx")),
        P(("seq", "ctx")),
        P(("seq", "ctx"), None),
        P(("seq", "ctx")),
        P(("seq", "ctx"), None),
        P(("seq", "ctx")),
    )
    return jax.shard_map(
        on_device,
        mesh=mesh,
        in_specs=placed,
        out_specs=(
            P("seq", "ctx", None),
            P("seq", "ctx", None),
            P(("seq", "ctx")),
            P(("seq", "ctx")),
            P(("seq", "ctx"), None),
            P(("seq", "ctx")),
            P(("seq", "ctx")),
            P(("seq", "ctx"), None),
            P(("seq", "ctx")),
            P(("seq", "ctx")),
            P(("seq", "ctx")),
            P(("seq", "ctx"), None),
            P(("seq", "ctx")),
            P(("seq", "ctx"), None),
            P(("seq", "ctx")),
            P("seq", None),
        ),
        check_vma=False,
    )
```

profile of v0, /device:TPU:21, one launch (start us, length us, event | category | flops | bytes accessed | tf_op | source)
XLA Modules:
  0.0 1233.2 jit_solution(6141206525194307702)
XLA Ops:
  14.7 39.7 %all-reduce.18 = (bf16[1024]{0:T(1024)(128)(2,1)S(1)}, bf16[1024]{0:T(1024)(128)(2,1)S(1)}, bf16[1024]{0:T(1024)(128)(2,1)S(1)}, bf16[1024]{0:T(1024)(128)(2,1)S...) all-reduce(bf16[1024]{0:T(1024)(128)(2,1)S(1)} %dynamic-update-slic, ...), channel_id=1, replica_groups=mesh['seq'=8,'ctx'=4] {'seq','ctx'}, use_global_device_ids=true, to_apply=%add.1 | all-reduce | flops 8192 | bytes 32768
  56.9 24.3 %all-gather.8.cloned.1.call-done = bf16[1024,3072]{1,0:T(8,128)(2,1)} async-done(((bf16[32,3072]{1,0:T(8,128)(2,1)}), bf16[1024,3072]{1,0:T(8,128)(2,1)}) %all-gather.8.cloned.1.call-update) | async-done | bytes 6291472 | tf_op jit(solution)/shard_map/all_gather | solution.py:113
  81.2 4.9 fusion.81
  88.9 2.1 slice.23
  93.5 30.0 %all-gather = bf16[32,1,128]{2,1,0:T(2,128)(2,1)S(1)} all-gather(bf16[1,1,128]{2,1,0:T(2,128)(2,1)S(1)} %bitcast.158), channel_id=1, replica_groups=mesh['seq'=8,'ctx'=4] {'seq','ctx'}, dimensions={0}, use_global_device_ids=true | all-gather | bytes 8448 | tf_op jit(solution)/shard_map/all_gather | solution.py:121
  123.8 4.0 copy.43
  127.8 6.8 all-gather.12.cloned.1.call-done
  134.5 4.0 copy.45
  138.6 45.2 %while.30 = (s32[]{:T(128)}, bf16[8,256,2,64]{1,3,2,0:T(8,128)(2,1)S(1)}, f32[8,2,256]{2,1,0:T(2,128)S(1)}, s32[8]{0:T(128)S(1)}, bf16[1024,16,64]{0,2,1:T(8,128...) while((s32[]{:T(128)}, ...), condition=%wide.region_5.6_spmd.clone.clone, body=%wide.region_2.5_spmd.clone.clone.sunk | while | flops 140771072 | bytes 10179299 | solution.py:186
  183.8 9.1 all-gather.14.cloned.1.call-done
  192.9 3.3 fusion.88
  196.5 76.3 %all-gather.16.cloned.1.call-done = bf16[1024,4096]{1,0:T(8,128)(2,1)} async-done(((bf16[32,4096]{1,0:T(8,128)(2,1)}), bf16[1024,4096]{1,0:T(8,128)(2,1)}) %all-gather.16.cloned.1.call-update) | async-done | bytes 8388624 | tf_op jit(solution)/shard_map/all_gather | solution.py:120
  272.8 7.8 convolution_add_fusion
  280.6 70.6 %all-gather.18.cloned.1.call-done = bf16[4096,1024]{1,0:T(8,128)(2,1)} async-done(((bf16[128,1024]{1,0:T(8,128)(2,1)}), bf16[4096,1024]{1,0:T(8,128)(2,1)}) %all-gather.18.cloned.1.call-update) | async-done | bytes 8388624 | tf_op jit(solution)/shard_map/all_gather | solution.py:122
  351.2 11.3 convert_reduce_fusion
  362.6 6.5 fusion.90
  370.7 4.9 fusion.59
  380.3 106.9 %while.31 = (s32[]{:T(128)}, bf16[8,256,2,64]{1,3,2,0:T(8,128)(2,1)}, bf16[8,1024,2,64]{1,3,2,0:T(8,128)(2,1)}, bf16[8,1024,2,64]{1,3,2,0:T(8,128)(2,1)}, s32[8]...) while((s32[]{:T(128)}, ...), condition=%wide.region_12.13_spmd.clone.clone, body=%wide.region_10.12_spmd.clone.clone.sunk | while | flops 342261504 | bytes 20593980 | solution.py:261
  385.4 2.1 multiply_reduce_fusion.5
  387.9 2.0 fusion.137
  398.8 2.1 multiply_reduce_fusion.5
  401.3 2.0 fusion.137
  412.1 2.1 multiply_reduce_fusion.5
  425.5 2.1 multiply_reduce_fusion.5
  428.0 2.0 fusion.137
  438.9 2.1 multiply_reduce_fusion.5
  441.4 2.0 fusion.137
  452.3 2.1 multiply_reduce_fusion.5
  454.8 2.0 fusion.137
  465.6 2.1 multiply_reduce_fusion.5
  468.1 2.0 fusion.137
  479.0 2.1 multiply_reduce_fusion.5
  481.5 2.0 fusion.137
  488.3 2.7 fusion.91
  491.1 25.1 %reduce-scatter.9.cloned.1.call-done = bf16[256,1024]{0,1:T(8,128)(2,1)} async-done(((bf16[1024,1024]{0,1:T(8,128)(2,1)}), bf16[256,1024]{0,1:T(8,128)(2,1)}) %reduce-scatter.9.cloned.1.call-update) | async-done | bytes 524304 | tf_op jit(solution)/shard_map/reduce_scatter | solution.py:267
  516.2 33.7 %reduce-scatter.7.cloned.1.call-done = bf16[256,1024]{0,1:T(8,128)(2,1)} async-done(((bf16[1024,1024]{0,1:T(8,128)(2,1)}), bf16[256,1024]{0,1:T(8,128)(2,1)}) %reduce-scatter.7.cloned.1.call-update) | async-done | bytes 524304 | tf_op jit(solution)/shard_map/reduce_scatter | solution.py:264
  549.9 7.7 fusion.66
  558.9 9.8 fusion.84
  569.7 10.8 fusion.74
  580.6 2.1 pad_maximum_fusion.3
  582.6 6.0 psum.7
  589.7 5.1 fusion.85
  596.3 41.3 %all-reduce.17 = (f32[1024]{0:T(1024)S(1)}, f32[1024]{0:T(1024)S(1)}, f32[1024]{0:T(1024)S(1)}, f32[1024]{0:T(1024)S(1)}, f32[1024]{0:T(1024)S(1)}, /*index=5*/f...) all-reduce(bf16[1024]{0:T(1024)(128)(2,1)S(1)} %get-tuple-element.2, ...), channel_id=4, replica_groups=mesh['seq'=8,'ctx'=4] {'seq','ctx'}, use_global_device_ids=true, to_apply=%region_18.19.clone | all-reduce | flops 12288 | bytes 90112
  642.8 2.7 add_bitcast_fusion
  645.5 20.9 %reduce-scatter.13.cloned.1.call-done = f32[32,1024]{1,0:T(8,128)} async-done(((f32[1024,1024]{1,0:T(8,128)}), f32[32,1024]{1,0:T(8,128)}) %reduce-scatter.13.cloned.1.call-update) | async-done | bytes 131088 | tf_op jit(solution)/shard_map/reduce_scatter | solution.py:291
  666.4 184.4 %reduce-scatter.11.cloned.1.call-done = f32[32,3072]{1,0:T(8,128)} async-done(((f32[1024,3072]{1,0:T(8,128)}), f32[32,3072]{1,0:T(8,128)}) %reduce-scatter.11.cloned.1.call-update) | async-done | bytes 393232 | tf_op jit(solution)/shard_map/reduce_scatter | solution.py:288
  850.8 188.2 %reduce-scatter.15.cloned.1.call-done = f32[32,4096]{1,0:T(8,128)} async-done(((f32[1024,4096]{1,0:T(8,128)}), f32[32,4096]{1,0:T(8,128)}) %reduce-scatter.15.cloned.1.call-update) | async-done | bytes 524304 | tf_op jit(solution)/shard_map/reduce_scatter | solution.py:299
  1039.0 187.4 %reduce-scatter.17.cloned.1.call-done = f32[128,1024]{1,0:T(8,128)} async-done(((f32[4096,1024]{1,0:T(8,128)}), f32[128,1024]{1,0:T(8,128)}) %reduce-scatter.17.cloned.1.call-update) | async-done | bytes 524304 | tf_op jit(solution)/shard_map/reduce_scatter | solution.py:301
  (283 shorter events, 126.8 us)
Async XLA Ops:
  7.2 74.1 %all-gather.8.cloned.1.call-start = ((), (), s32[]{:S(2)}) async-start(), calls=%async_computation.6 | async-start | bytes 6488064 | tf_op jit(solution)/shard_map/all_gather | solution.py:113
  7.9 115.9 %all-gather.10.cloned.1.call-start = ((), (), s32[]{:S(2)}) async-start(), calls=%async_computation.7 | async-start | bytes 2621440 | tf_op jit(solution)/shard_map/all_gather | solution.py:159
  86.1 1.7 copy-start.11
  87.8 5.7 copy-start.18
  88.9 45.7 %all-gather.12.cloned.1.call-start = ((), (), s32[]{:S(2)}) async-start(), calls=%async_computation.8 | async-start | bytes 2621440 | tf_op jit(solution)/shard_map/all_gather | solution.py:158
  91.0 101.9 %all-gather.14.cloned.1.call-start = ((), (), s32[]{:S(2)}) async-start(), calls=%async_computation.9 | async-start | bytes 2162688 | tf_op jit(solution)/shard_map/all_gather | solution.py:116
  91.6 181.2 %all-gather.16.cloned.1.call-start = ((), (), s32[]{:S(2)}) async-start(), calls=%async_computation.10 | async-start | bytes 8650752 | tf_op jit(solution)/shard_map/all_gather | solution.py:120
  92.2 259.0 %all-gather.18.cloned.1.call-start = ((), (), s32[]{:S(2)}) async-start(), calls=%async_computation.11 | async-start | bytes 8650752 | tf_op jit(solution)/shard_map/all_gather | solution.py:122
  92.8 423.4 %reduce-scatter.9.cloned.1.call-start = ((), (), s32[]{:S(2)}) async-start(), calls=%async_computation.13 | async-start | bytes 2621440 | tf_op jit(solution)/shard_map/reduce_scatter | solution.py:267
  138.6 54.3 %copy-start = (bf16[1,256,1024]{2,1,0:T(8,128)(2,1)S(1)}, bf16[1,256,1024]{2,1,0:T(8,128)(2,1)}, u32[]{:S(2)}) copy-start(bf16[1,256,1024]{2,1,0:T(8,128)(2,1)} %param.20) | copy-start | bytes 1572868
  183.8 12.7 %copy-start.9 = (bf16[256,16,64]{0,2,1:T(8,128)(2,1)}, bf16[256,16,64]{0,2,1:T(8,128)(2,1)S(1)}, u32[]{:S(2)}) copy-start(bf16[256,16,64]{0,2,1:T(8,128)(2,1)S(1)} %get-tuple-element.619) | copy-start | bytes 1572868
  196.2 179.4 %copy-start.1 = (f32[256,1024]{1,0:T(8,128)}, f32[256,1024]{1,0:T(8,128)S(1)}, u32[]{:S(2)}) copy-start(f32[256,1024]{1,0:T(8,128)S(1)} %get-tuple-element.351) | copy-start | bytes 3145732
  272.8 78.4 %copy-start.7 = (bf16[1,256,1024]{2,1,0:T(8,128)(2,1)S(1)}, bf16[1,256,1024]{2,1,0:T(8,128)(2,1)}, u32[]{:S(2)}) copy-start(bf16[1,256,1024]{2,1,0:T(8,128)(2,1)} %param.22) | copy-start | bytes 1572868
  362.6 6.6 copy-start.16
  362.6 6.6 copy-start.5
  362.6 6.6 copy-start.17
  362.6 8.1 copy-start.19
  375.6 2.0 copy-start.15
  376.0 1.0 copy-start.3
  377.3 3.0 copy-start.12
  487.2 1.0 copy-start.13
  487.3 62.6 %reduce-scatter.7.cloned.1.call-start = ((), (), s32[]{:S(2)}) async-start(), calls=%async_computation.12 | async-start | bytes 2621440 | tf_op jit(solution)/shard_map/reduce_scatter | solution.py:264
  488.0 178.4 %reduce-scatter.13.cloned.1.call-start = ((), (), s32[]{:S(2)}) async-start(), calls=%async_computation.15 | async-start | bytes 4325376 | tf_op jit(solution)/shard_map/reduce_scatter | solution.py:291
  491.0 58.9 %copy-start.6 = (bf16[8,256,2,64]{1,3,2,0:T(8,128)(2,1)S(1)}, bf16[8,256,2,64]{1,3,2,0:T(8,128)(2,1)}, u32[]{:S(2)}) copy-start(bf16[8,256,2,64]{1,3,2,0:T(8,128)(2,1)} %get-tuple-element.146) | copy-start | bytes 1572868
  491.0 359.8 %reduce-scatter.11.cloned.1.call-start = ((), (), s32[]{:S(2)}) async-start(), calls=%async_computation.14 | async-start | bytes 12976128 | tf_op jit(solution)/shard_map/reduce_scatter | solution.py:288
  557.6 1.2 copy-start.2
  557.7 481.3 %reduce-scatter.15.cloned.1.call-start = ((), (), s32[]{:S(2)}) async-start(), calls=%async_computation.16 | async-start | bytes 17301504 | tf_op jit(solution)/shard_map/reduce_scatter | solution.py:299
  568.7 1.0 copy-start.8
  568.7 657.7 %reduce-scatter.17.cloned.1.call-start = ((), (), s32[]{:S(2)}) async-start(), calls=%async_computation.17 | async-start | bytes 17301504 | tf_op jit(solution)/shard_map/reduce_scatter | solution.py:301
  580.5 8.9 copy-start.14
  589.7 53.2 %copy-start.4 = (f32[256,1024]{1,0:T(8,128)S(1)}, f32[256,1024]{1,0:T(8,128)}, u32[]{:S(2)}) copy-start(f32[256,1024]{1,0:T(8,128)} %copy-done.3) | copy-start | bytes 3145732
  594.7 1.0 copy-start.10
Sparse Core Ops, SparseCore 0:
  10.9 70.3 all-gather.7
  89.0 20.7 all-gather.9
  112.0 22.5 all-gather.11
  137.3 55.5 all-gather.13
  195.6 77.1 all-gather.15
  275.5 75.6 all-gather.17
  487.4 28.7 reduce-scatter.8
  518.7 31.1 reduce-scatter.6
  552.7 113.6 reduce-scatter.12
  672.9 177.9 reduce-scatter.10
  853.7 185.2 reduce-scatter.14
  1041.7 184.6 reduce-scatter.16
where the time goes:
time: 1240 us; the launch traced here: 1230 us
  waiting for transfers between devices  830 us (67%)
  matrix products  177 us (14%)
  blocking collectives  117 us (9%)
  local copies, waits for them, and re-layouts  42.4 us (3%)
  loops' own time  26.7 us (2%)
  other arithmetic  24.8 us (2%)
  between operations  15.3 us (1%)
    reduce_scatter x1, waiting for transfers between devices, on_device(): lax.psum_scatter(grad_up_w, ('seq', 'ctx'), scatter_dimension=0, tiled=True)  188 us
    reduce_scatter x1, waiting for transfers between devices, on_device(): lax.psum_scatter(grad_down_w, ('seq', 'ctx'), scatter_dimension=0, tiled=...  187 us
    reduce_scatter x1, waiting for transfers between devices, on_device(): lax.psum_scatter(grad_qkv_w, ('seq', 'ctx'), scatter_dimension=0, tiled=T...  184 us
    unnamed x2, blocking collectives  81 us
    all_gather x1, waiting for transfers between devices, on_device(): lax.all_gather(shards[9], ('seq', 'ctx'), axis=0, tiled=True)  76.3 us
    all_gather x1, waiting for transfers between devices, on_device(): lax.all_gather(shards[11], ('seq', 'ctx'), axis=0, tiled=True)  70.6 us
    reduce_scatter x1, waiting for transfers between devices, on_device(): lax.psum_scatter(to_blocks(key_parts).astype(jnp.bfloat16), 'ctx', scatte...  33.7 us
    dot_general x4, matrix products, inner_rows(): lax.dot_general(left, right, (((0,), (0,)), ((), ())), preferred_element_...  31.1 us
  transfers between devices with their start and end apart: 12, of which 11 were waited for; matrix products, arithmetic and copies ran while one was open for 10% of the time, Pallas kernels for 0%

commit v1 on v0

--- a/solution.py
+++ b/solution.py
@@ -1,7 +1,898 @@
+import itertools
+
 import jax
 import jax.numpy as jnp
 from jax import lax
+from jax.experimental import pallas as pl
+from jax.experimental.pallas import tpu as pltpu
 from jax.sharding import PartitionSpec as P
+
+MESH = pl.DeviceIdType.MESH
+bf16, f32 = jnp.bfloat16, jnp.float32
+LOG2E = 1.4426950408889634
+D = 1024
+R = 256
+S = 1024
+LIMIT = 66_000_000
+NSEM = 200
+
+
+def nn(a, b):
+    return lax.dot_general(a, b, (((1,), (0,)), ((), ())), preferred_element_type=f32)
+
+
+def nt(a, b):
+    return lax.dot_general(a, b, (((1,), (1,)), ((), ())), preferred_element_type=f32)
+
+
+def tn(a, b):
+    return lax.dot_general(a, b, (((0,), (0,)), ((), ())), preferred_element_type=f32)
+
+
+def mul(v, m):
+    return pl.multiple_of(v, m)
+
+
+def loop(n, body, start=0):
+    def step(i, carry):
+        body(i)
+        return carry
+
+    lax.fori_loop(start, n, step, 0)
+
+
+def layer_stats(v):
+    mean = jnp.sum(v, axis=-1, keepdims=True) * (1.0 / D)
+    cen = v - mean
+    var = jnp.sum(cen * cen, axis=-1, keepdims=True) * (1.0 / D)
+    rstd = lax.rsqrt(var + 1e-5)
+    return cen * rstd, rstd
+
+
+def layer_back(g2, gain, z, rstd):
+    g = g2 * gain
+    m1 = jnp.sum(g, axis=-1, keepdims=True) * (1.0 / D)
+    m2 = jnp.sum(g * z, axis=-1, keepdims=True) * (1.0 / D)
+    return rstd * (g - m1 - z * m2)
+
+
+def block_kernel(
+    length_ref, tok, cot, small, qkv_in, out_in, up_in, down_in,
+    o_out, o_grad, o_dqkv, o_dout, o_dup, o_ddown, o_small,
+    wqkv, wout, wup, wdown, smc, smb, vec,
+    n1, n2, gf, gb, act, gpre, qkv, vt, kt, attt, dot_, do_, dmix, linv,
+    ptri, acck, accv,
+    rs_s, rs_r, rs_own, rt_s, rt_r, rt_own, tmp, res,
+    xs, xr_down, xr_up, xr_qkv, xr_out, own_a, own_b, own_out,
+    zs, zso, zr_down, zr_up, zr_qkv, zr_out, fin_up, fin_qkv, fin_out,
+    sg, sgx, sgs, sgz, sgf, sgc, gvec, gmat, stat,
+    lsem, ssem, rsem,
+):
+    seq, ctx = lax.axis_index("seq"), lax.axis_index("ctx")
+    z, x = seq // 2, seq % 2
+    y, k = ctx // 2, ctx % 2
+    ids = itertools.count()
+    lids = itertools.count()
+
+    mate = {"ctx": y * 2 + (k + 1) % 2}
+    ypeer = {"ctx": ((y + 1) % 2) * 2 + k}
+    xpeer = {"seq": z * 2 + (x + 1) % 2}
+
+    def cpeer(d):
+        return {"ctx": (ctx + d) % 4}
+
+    def zpeer(d):
+        return {"seq": ((z + d) % 4) * 2 + x}
+
+    def take(n=1):
+        first = next(ids)
+        for _ in range(n - 1):
+            next(ids)
+        return first
+
+    def rcopy(src, dst, dev, i):
+        return pltpu.make_async_remote_copy(
+            src_ref=src, dst_ref=dst, send_sem=ssem.at[i], recv_sem=rsem.at[i],
+            device_id=dev, device_id_type=MESH)
+
+    def wait_bytes(ref, sem):
+        pltpu.make_async_copy(ref, ref, sem).wait()
+
+    sends = []
+
+    def sent(ref, i, cond=None):
+        sends.append((ref, i, cond))
+
+    def flush():
+        for ref, i, cond in sends:
+            if cond is None:
+                wait_bytes(ref, ssem.at[i])
+            else:
+                @pl.when(cond)
+                def _(ref=ref, i=i):
+                    wait_bytes(ref, ssem.at[i])
+        sends.clear()
+
+    rows = lambda c: pl.ds(mul(c * R, R), R)
+    srow = lambda s: pl.ds(mul(s * 128, 128), 128)
+
+    barrier = pltpu.get_barrier_semaphore()
+    for d in (1, 2, 3):
+        pl.semaphore_signal(barrier, inc=1, device_id=cpeer(d), device_id_type=MESH)
+        pl.semaphore_signal(barrier, inc=1, device_id=zpeer(d), device_id_type=MESH)
+    pl.semaphore_signal(barrier, inc=1, device_id=xpeer, device_id_type=MESH)
+    pl.semaphore_wait(barrier, 7)
+
+    i_smc = take(4)
+    for d in (1, 2, 3):
+        rcopy(small, smc.at[d], cpeer(d), i_smc + d).start()
+        sent(small, i_smc + d)
+    own32 = pl.ds(mul(seq * 128 + ctx * 32, 32), 32)
+
+    def qkv_pieces(c):
+        for j in range(6):
+            yield (pl.ds(mul((j // 2) * D + (c + 4 * (j % 2)) * 128, 128), 128),
+                   pl.ds(j * 128, 128))
+
+    i_qa = take(4)
+    for d in (1, 2, 3):
+        for a, b in qkv_pieces((ctx + d) % 4):
+            rcopy(qkv_in.at[:, a], wqkv.at[own32, b], cpeer(d), i_qa + d).start()
+        sent(wqkv.at[pl.ds(0, 32), :], i_qa + d)
+    l_q = next(lids)
+    for a, b in qkv_pieces(ctx):
+        pltpu.make_async_copy(qkv_in.at[:, a], wqkv.at[own32, b], lsem.at[l_q]).start()
+
+    for d in (1, 2, 3):
+        rcopy(small, smc.at[d], cpeer(d), i_smc + d).wait_recv()
+    rowid = lax.broadcasted_iota(jnp.int32, (16, 128), 0)
+    smb[seq] = small[...] + jnp.where(rowid < 8, smc[1] + smc[2] + smc[3], 0.0)
+
+    def gather_start(buf, block, zi, xi, src=None):
+        for d in (1, 2, 3):
+            own = block(seq) if src is None else src
+            rcopy(own, block(seq), zpeer(d), zi + d).start()
+            sent(own, zi + d)
+        own = block(seq) if src is None else src
+        rcopy(own, block(seq), xpeer, xi).start()
+        sent(own, xi)
+
+    def gather_forward(block, zi, xi, d):
+        b = block(((z - d + 4) % 4) * 2 + x)
+        rcopy(b, b, xpeer, zi + d).wait_recv()
+        rcopy(b, b, xpeer, xi + d).start()
+        sent(b, xi + d)
+
+    def gather_finish(block, xi):
+        for d in range(4):
+            b = block(seq)
+            rcopy(b, b, xpeer, xi + d).wait_recv()
+
+    small_block = lambda s: smb.at[s]
+    i_sz, i_sx = take(4), take(4)
+    gather_start(smb, small_block, i_sz, i_sx)
+
+    for d in (1, 2, 3):
+        wait_bytes(wqkv.at[pl.ds(0, 32), :], rsem.at[i_qa + d])
+    wait_bytes(wqkv.at[pl.ds(0, 32), :], lsem.at[l_q])
+    qkv_block = lambda s: wqkv.at[srow(s), :]
+    i_qz, i_qx = take(4), take(4)
+    gather_start(wqkv, qkv_block, i_qz, i_qx)
+
+    t = seq % 4
+    out32 = pl.ds(mul((seq // 4) * 128 + ctx * 32, 32), 32)
+    i_oa = take()
+    l_o = next(lids)
+
+    @pl.when(ctx != t)
+    def _():
+        rcopy(out_in, wout.at[out32, :], {"ctx": t}, i_oa).start()
+
+    sent(out_in, i_oa, ctx != t)
+
+    @pl.when(ctx == t)
+    def _():
+        pltpu.make_async_copy(out_in, wout.at[out32, :], lsem.at[l_o]).start()
+
+    for d in (1, 2, 3):
+        gather_forward(small_block, i_sz, i_sx, d)
+    gather_finish(small_block, i_sx)
+    for s in range(8):
+        vec[:, s * 128 : (s + 1) * 128] = smb[s]
+
+    length = length_ref[0]
+    my = mul(ctx * R, R)
+
+    def valid_rows(r0, n):
+        pos = lax.broadcasted_iota(jnp.int32, (n, 1), 0) + (ctx * R + r0)
+        return jnp.where(pos < length, 1.0, 0.0).astype(f32)
+
+    def first(i):
+        r0 = mul(i * 64, 64)
+        zz, _ = layer_stats(tok[pl.ds(r0, 64), :].astype(f32))
+        n1[pl.ds(mul(my + r0, 64), 64), :] = (zz * vec[0:1, :] + vec[1:2, :]).astype(bf16)
+        g = cot[pl.ds(r0, 64), :].astype(f32) * valid_rows(r0, 64)
+        gf[pl.ds(mul(my + r0, 64), 64), :] = g.astype(bf16)
+
+    loop(4, first)
+
+    CH = 2
+    RC = R // CH
+
+    def chunk(buf, c, ch):
+        return buf.at[pl.ds(mul(c * R + ch * RC, RC), RC), :]
+
+    def ag_start(buf, i, ch):
+        own = chunk(buf, ctx, ch)
+        rcopy(own, own, ypeer, i + CH + ch).start()
+        rcopy(own, own, mate, i + ch).start()
+        sent(own, i + CH + ch)
+        sent(own, i + ch)
+
+    def ag_forward(buf, i, ch):
+        b = chunk(buf, ((y + 1) % 2) * 2 + k, ch)
+        rcopy(b, b, mate, i + CH + ch).wait_recv()
+        rcopy(b, b, mate, i + 2 * CH + ch).start()
+        sent(buf.at[pl.ds(0, RC), :], i + 2 * CH + ch)
+
+    def ag_wait(buf, i, which):
+        for ch in range(CH):
+            b = chunk(buf, ctx, ch)
+            rcopy(b, b, mate, i + which * CH + ch).wait_recv()
+
+    i_n1 = take(3 * CH)
+    for ch in range(CH):
+        ag_start(n1, i_n1, ch)
+
+    i_ua = take(4)
+    for d in (1, 2, 3):
+        c2 = (ctx + d) % 4
+        for s in range(8):
+            rcopy(up_in.at[:, pl.ds(mul((s * 4 + c2) * 128, 128), 128)],
+                  wup.at[own32, pl.ds(s * 128, 128)], cpeer(d), i_ua + d).start()
+        sent(wup.at[pl.ds(0, 32), :], i_ua + d)
+    l_u = next(lids)
+    for s in range(8):
+        pltpu.make_async_copy(up_in.at[:, pl.ds(mul((s * 4 + ctx) * 128, 128), 128)],
+                              wup.at[own32, pl.ds(s * 128, 128)], lsem.at[l_u]).start()
+    i_gf = take(3 * CH)
+    for ch in range(CH):
+        ag_start(gf, i_gf, ch)
+    l_d = next(lids)
+    down_block = lambda s: wdown.at[srow(s), :]
+    pltpu.make_async_copy(down_in, down_block(seq), lsem.at[l_d]).start()
+
+    i_oz, i_ox = take(4), take(4)
+    out_block = lambda zz: wout.at[pl.ds(mul((zz // 2) * 128, 128), 128), :]
+
+    @pl.when(ctx == t)
+    def _():
+        wait_bytes(wout.at[pl.ds(0, 96), :], rsem.at[i_oa])
+        wait_bytes(wout.at[pl.ds(0, 32), :], lsem.at[l_o])
+        for d in (1, 2, 3):
+            rcopy(out_block(z), out_block(z), zpeer(d), i_oz + d).start()
+        rcopy(out_block(z), out_block(z), xpeer, i_ox).start()
+
+    for d in (1, 2, 3):
+        sent(out_block(z), i_oz + d, ctx == t)
+    sent(out_block(z), i_ox, ctx == t)
+
+    for ch in range(CH):
+        ag_forward(n1, i_n1, ch)
+
+    for d in (1, 2, 3):
+        wait_bytes(wup.at[pl.ds(0, 32), :], rsem.at[i_ua + d])
+    wait_bytes(wup.at[pl.ds(0, 32), :], lsem.at[l_u])
+    up_block = lambda s: wup.at[srow(s), :]
+    i_uz, i_ux = take(4), take(4)
+    gather_start(wup, up_block, i_uz, i_ux)
+    i_dz, i_dx = take(4), take(4)
+    gather_start(wdown, down_block, i_dz, i_dx, src=down_in)
+
+    for d in (1, 2, 3):
+        gather_forward(qkv_block, i_qz, i_qx, d)
+    ag_wait(n1, i_n1, 0)
+    gather_finish(qkv_block, i_qx)
+
+    def project(it):
+        blk = ((y + it // 2) % 2) * 2 + (k + it % 2) % 2
+
+        @pl.when(it == 3)
+        def _():
+            ag_wait(n1, i_n1, 2)
+
+        a = n1[rows(blk), :]
+        for j in range(3):
+            r = nn(a, wqkv[:, j * 256 : (j + 1) * 256])
+            if j != 1:
+                for i in range(2):
+                    b = vec[2 + j // 2 : 3 + j // 2, pl.ds(mul((ctx + 4 * i) * 128, 128), 128)]
+                    qkv[rows(blk), j * 256 + i * 128 : j * 256 + (i + 1) * 128] = (
+                        r[:, i * 128 : (i + 1) * 128] + b).astype(bf16)
+            else:
+                qkv[rows(blk), 256:512] = r.astype(bf16)
+
+    loop(4, project)
+    for ch in range(CH):
+        ag_forward(gf, i_gf, ch)
+
+    mine = x == k
+    for d in (1, 2, 3):
+        zz = (z - d + 4) % 4
+
+        @pl.when(jnp.logical_and(mine, zz % 2 == y))
+        def _(d=d, zz=zz):
+            rcopy(out_block(zz), out_block(zz), xpeer, i_oz + d).wait_recv()
+            rcopy(out_block(zz), out_block(zz), xpeer, i_ox + d).start()
+
+        sent(out_block(zz), i_ox + d, jnp.logical_and(mine, zz % 2 == y))
+
+    def turn(i):
+        c0 = pl.ds(mul(i * 128, 128), 128)
+        vt[c0, :] = qkv[:, pl.ds(mul(512 + i * 128, 128), 128)].T
+        kt[c0, :] = qkv[:, pl.ds(mul(256 + i * 128, 128), 128)].T
+
+    loop(2, turn)
+
+    lane = lax.broadcasted_iota(jnp.int32, (256, 128), 1)
+    krow = lax.broadcasted_iota(jnp.int32, (256, 256), 0)
+    qcol = lax.broadcasted_iota(jnp.int32, (256, 256), 1)
+
+    def tri(kb, qb):
+        return (qb * (qb + 1)) // 2 + kb
+
+    def half(v, j):
+        return jnp.where((lane // 64) == j, v, jnp.zeros_like(v))
+
+    def pair_forward(i):
+        for j in range(2):
+            slope = jnp.exp2(jnp.full((1024, 128), -0.5, f32)
+                             * (2 * ctx + 8 * i + j + 1).astype(f32)) * LOG2E
+            b = slope * lax.broadcasted_iota(jnp.int32, (1024, 128), 0).astype(f32)
+            for kb in range(4):
+                own_b[j * 256 : (j + 1) * 256, kb * 128 : (kb + 1) * 128] = b[kb * 256 : (kb + 1) * 256]
+
+        def queries(qb):
+            q0 = pl.ds(mul(qb * 256, 256), 256)
+            qblk = qkv[q0, pl.ds(mul(i * 128, 128), 128)]
+
+            def scores(kb, best):
+                k0 = pl.ds(mul(kb * 256, 256), 256)
+                kblk = qkv[k0, pl.ds(mul(256 + i * 128, 128), 128)]
+                new = []
+                for j in range(2):
+                    b = own_b[j * 256 : (j + 1) * 256, pl.ds(mul(kb * 128, 128), 128)]
+                    sc = nt(half(kblk, j), qblk) * (0.125 * LOG2E) + jnp.concatenate([b, b], axis=1)
+                    sc = jnp.where(krow + kb * 256 <= qcol + qb * 256, sc, -1e30)
+                    own_a[j * 256 : (j + 1) * 256, k0] = sc
+                    new.append(jnp.maximum(best[j], jnp.max(sc.reshape(32, 8, 256), axis=0)))
+                return tuple(new)
+
+            low = jnp.full((8, 256), -3e38, f32)
+            best = lax.fori_loop(0, qb + 1, scores, (low, low))
+            top = [jnp.max(b, axis=0, keepdims=True) for b in best]
+
+            def weigh(kb, carry):
+                k0 = pl.ds(mul(kb * 256, 256), 256)
+                new = []
+                for j in range(2):
+                    total, acc = carry[2 * j], carry[2 * j + 1]
+                    p = jnp.exp2(own_a[j * 256 : (j + 1) * 256, k0] - top[j])
+                    total = total + jnp.sum(p.reshape(32, 8, 256), axis=0)
+                    p = p.astype(bf16)
+                    ptri[2 * i + j, tri(kb, qb)] = p
+                    v = vt[pl.ds(mul(i * 128 + j * 64, 64), 64), k0]
+                    new += [total, acc + nn(v, p)]
+                return tuple(new)
+
+            zero = (jnp.zeros((8, 256), f32), jnp.zeros((64, 256), f32))
+            out = lax.fori_loop(0, qb + 1, weigh, zero + zero)
+            for j in range(2):
+                inv = 1.0 / jnp.sum(out[2 * j], axis=0, keepdims=True)
+                linv[2 * i + j, :, q0] = jnp.broadcast_to(inv, (8, 256))
+                attt[pl.ds(mul(i * 128 + j * 64, 64), 64), q0] = (out[2 * j + 1] * inv).astype(bf16)
+
+        loop(4, queries)
+
+    loop(2, pair_forward)
+
+    def rs_run(partial, sb, rb, own, i):
+        def step(tt):
+            g, ch, sub = tt // 4, (tt // 2) % 2, tt % 2
+            blk = ((y + 1 - g) % 2) * 2 + (k + 1 - sub) % 2
+            partial(blk, ch, tmp)
+
+            @pl.when(jnp.logical_and(g == 0, sub == 0))
+            def _():
+                sb[0, ch] = tmp[...].astype(bf16)
+                rcopy(sb.at[0, ch], rb.at[0, ch], mate, i + ch).start()
+
+            @pl.when(jnp.logical_and(g == 0, sub == 1))
+            def _():
+                rcopy(sb.at[0, ch], rb.at[0, ch], mate, i + ch).wait_recv()
+                sb[1, ch] = (tmp[...] + rb[0, ch].astype(f32)).astype(bf16)
+                rcopy(sb.at[1, ch], rb.at[1, ch], ypeer, i + CH + ch).start()
+
+            @pl.when(jnp.logical_and(g == 1, sub == 0))
+            def _():
+                sb[2, ch] = tmp[...].astype(bf16)
+                rcopy(sb.at[2, ch], rb.at[2, ch], mate, i + 2 * CH + ch).start()
+
+            @pl.when(jnp.logical_and(g == 1, sub == 1))
+            def _():
+                own[ch] = tmp[...]
+
+        loop(4 * CH, step)
+
+    def rs_wait(sb, rb, i, ch):
+        rcopy(sb.at[2, ch], rb.at[2, ch], mate, i + 2 * CH + ch).wait_recv()
+        rcopy(sb.at[1, ch], rb.at[1, ch], mate, i + CH + ch).wait_recv()
+
+    def rs_sum(rb, own, ch, r):
+        return own[ch, r, :] + rb[2, ch, r, :].astype(f32) + rb[1, ch, r, :].astype(f32)
+
+    def rs_sent(sb, i):
+        for j in range(3):
+            for ch in range(CH):
+                wait_bytes(sb.at[j, ch], ssem.at[i + j * CH + ch])
+
+    for d in range(4):
+        zz = (z - d + 4) % 4
+
+        @pl.when(jnp.logical_and(x != k, zz % 2 == y))
+        def _(d=d):
+            rcopy(out_block(z), out_block(z), xpeer, i_ox + d).wait_recv()
+
+    def branch_part(blk, ch, dst):
+        a = attt[:, pl.ds(mul(blk * R + ch * RC, RC), RC)]
+        dst[...] = tn(a, wout[...])
+
+    i_br = take(3 * CH)
+    rs_run(branch_part, rs_s, rs_r, rs_own, i_br)
+
+    for d in (1, 2, 3):
+        gather_forward(up_block, i_uz, i_ux, d)
+
+    i_n2 = take(3 * CH)
+    stat[...] = jnp.zeros_like(stat)
+    for ch in range(CH):
+        rs_wait(rs_s, rs_r, i_br, ch)
+
+        def second(q, ch=ch):
+            r = pl.ds(mul(q * 32, 32), 32)
+            r1 = pl.ds(mul(ch * RC + q * 32, 32), 32)
+            branch = rs_sum(rs_r, rs_own, ch, r) + vec[4:5, :]
+            resid = tok[r1, :].astype(f32) + branch
+            res[r1, :] = resid
+            zz, _ = layer_stats(resid)
+            n2[pl.ds(mul(my + ch * RC + q * 32, 32), 32), :] = (
+                zz * vec[5:6, :] + vec[6:7, :]).astype(bf16)
+            v = valid_rows(ch * RC + q * 32, 32)
+            stat[0:8, :] += jnp.sum((branch * branch * v).reshape(4, 8, D), axis=0)
+            stat[8:16, :] += jnp.sum((resid * resid * v).reshape(4, 8, D), axis=0)
+
+        loop(RC // 32, second)
+        ag_start(n2, i_n2, ch)
+
+    ag_wait(gf, i_gf, 0)
+    ag_wait(gf, i_gf, 2)
+    for d in (1, 2, 3):
+        gather_forward(down_block, i_dz, i_dx, d)
+    gather_finish(up_block, i_ux)
+
+    def feed(it):
+        blk = ((y + it // 2) % 2) * 2 + (k + it % 2) % 2
+
+        @pl.when(it == 1)
+        def _():
+            ag_wait(n2, i_n2, 0)
+            for ch in range(CH):
+                ag_forward(n2, i_n2, ch)
+            for d in range(4):
+                rcopy(down_block(seq), down_block(seq), xpeer, i_dx + d).wait_recv()
+            wait_bytes(down_in, lsem.at[l_d])
+
+        @pl.when(it == 3)
+        def _():
+            ag_wait(n2, i_n2, 2)
+
+        def cols(n):
+            c0 = pl.ds(mul(n * 512, 512), 512)
+            pre = nn(n2[rows(blk), :], wup[:, c0]) + vec[8:9, c0]
+            sq = pre * pre
+            th = jnp.tanh(0.7978845608028654 * pre * (1.0 + 0.044715 * sq))
+            a1 = 0.5 * (1.0 + th)
+            act[rows(blk), c0] = (pre * a1).astype(bf16)
+            der = a1 + 0.5 * pre * (1.0 - th * th) * (
+                0.7978845608028654 * (1.0 + 0.134145 * sq))
+            gpre[rows(blk), c0] = der.astype(bf16)
+
+        loop(2, cols)
+
+    loop(4, feed)
+    gvec[...] = jnp.zeros_like(gvec)
+
+    def grad_feed(it):
+        r = pl.ds(mul(it * R, R), R)
+
+        def cols(n):
+            c0 = pl.ds(mul(n * 512, 512), 512)
+            ga = nt(gf[r, :], wdown[c0, :])
+            g = (ga * gpre[r, c0].astype(f32)).astype(bf16)
+            gpre[r, c0] = g
+            gvec[2, :, c0] += jnp.sum(g.astype(f32).reshape(R // 8, 8, 512), axis=0)
+
+        loop(2, cols)
+
+    loop(4, grad_feed)
+
+    rs_sent(rs_s, i_br)
+
+    def gn2_part(blk, ch, dst):
+        dst[...] = nt(gpre[pl.ds(mul(blk * R + ch * RC, RC), RC), :], wup[...])
+
+    i_g2 = take(3 * CH)
+    rs_run(gn2_part, rs_s, rs_r, rs_own, i_g2)
+
+    def dw_half(a, b, n, xx, hh):
+        c1 = pl.ds(mul(((2 * hh) * 2 + xx) * 128, 128), 128)
+        c2 = pl.ds(mul(((2 * hh + 1) * 2 + xx) * 128, 128), 128)
+        return tn(jnp.concatenate([a[:, c1], a[:, c2]], axis=1), b[:, 0:n])
+
+    def dw_run(a, b, n, xr, own, i, before=None):
+        def away(hh):
+            xs[pl.ds(mul(hh * 256, 256), 256), 0:n] = dw_half(a, b, n, (x + 1) % 2, hh).astype(bf16)
+            s0 = xs.at[pl.ds(mul(hh * 256, 256), 256), pl.ds(0, n)]
+            rcopy(s0, xr.at[pl.ds(mul(hh * 256, 256), 256), :], xpeer, i + hh).start()
+
+        loop(2, away)
+
+        def keep(hh):
+            own[pl.ds(mul(hh * 256, 256), 256), 0:n] = dw_half(a, b, n, x, hh)
+
+        loop(2, keep)
+
+    def dw_xsent(n, i):
+        for hh in range(2):
+            wait_bytes(xs.at[pl.ds(0, 256), pl.ds(0, n)], ssem.at[i + hh])
+
+    def dw_z(n, xr, own, zr, fin, i, iz):
+        for hh in range(2):
+            wait_bytes(xr.at[pl.ds(0, 256), :], rsem.at[i + hh])
+        for d in (1, 2, 3):
+            blk = srow((z + d) % 4)
+            zs[d - 1, :, 0:n] = (own[blk, 0:n] + xr[blk, :].astype(f32)).astype(bf16)
+            rcopy(zs.at[d - 1, :, pl.ds(0, n)], zr.at[d - 1], zpeer(d), iz + d).start()
+        blk = srow(z)
+        fin[...] = own[blk, 0:n] + xr[blk, :].astype(f32)
+
+    def dw_zsent(n, iz):
+        for d in (1, 2, 3):
+            wait_bytes(zs.at[d - 1, :, pl.ds(0, n)], ssem.at[iz + d])
+
+    def dw_end(zr, fin, iz):
+        for d in (1, 2, 3):
+            wait_bytes(zr.at[d - 1], rsem.at[iz + d])
+        fin[...] += (zr[0].astype(f32) + zr[1].astype(f32)) + zr[2].astype(f32)
+
+    i_dwx, i_dwz = take(2), take(4)
+    dw_run(act, gf, D, xr_down, own_a, i_dwx)
+
+    i_gb = take(3 * CH)
+    for ch in range(CH):
+        rs_wait(rs_s, rs_r, i_g2, ch)
+
+        def third(q, ch=ch):
+            r = pl.ds(mul(q * 32, 32), 32)
+            r1 = pl.ds(mul(ch * RC + q * 32, 32), 32)
+            g2 = rs_sum(rs_r, rs_own, ch, r)
+            zz, rstd = layer_stats(res[r1, :])
+            gout = cot[r1, :].astype(f32) * valid_rows(ch * RC + q * 32, 32)
+            gres = gout + layer_back(g2, vec[5:6, :], zz, rstd)
+            o_grad[r1, :] = gres
+            low = gres.astype(bf16)
+            gb[pl.ds(mul(my + ch * RC + q * 32, 32), 32), :] = low
+            fold = lambda v: jnp.sum(v.reshape(4, 8, D), axis=0)
+            gvec[4] += fold(low.astype(f32))
+            gvec[5] += fold(g2 * zz)
+            gvec[6] += fold(g2)
+            gvec[7] += fold(gout)
+
+        loop(RC // 32, third)
+        ag_start(gb, i_gb, ch)
+
+    dw_xsent(D, i_dwx)
+    i_uwx, i_uwz = take(2), take(4)
+    dw_run(n2, gpre, D, xr_up, own_b, i_uwx)
+    dw_z(D, xr_down, own_a, zr_down, o_ddown, i_dwx, i_dwz)
+    for ch in range(CH):
+        ag_forward(gb, i_gb, ch)
+
+    def ffn_part(blk, ch, dst):
+        dst[...] = nn(act[pl.ds(mul(blk * R + ch * RC, RC), RC), :], wdown[...])
+
+    i_ff = take(3 * CH)
+    rs_run(ffn_part, rt_s, rt_r, rt_own, i_ff)
+
+    ag_wait(gb, i_gb, 0)
+    ag_wait(gb, i_gb, 2)
+
+    def att_grad(i):
+        c0 = pl.ds(mul(i * 256, 256), 256)
+        dot_[:, c0] = nt(wout[...], gb[c0, :]).astype(bf16)
+
+    loop(4, att_grad)
+    own_out[...] = nn(attt[...], gb[...])
+    i_owx, i_owz = take(), take(4)
+
+    dw_xsent(D, i_uwx)
+
+    @pl.when(x != k)
+    def _():
+        xs[0:256, :] = own_out[...].astype(bf16)
+        rcopy(xs.at[pl.ds(0, 256), :], xr_out, xpeer, i_owx).start()
+
+    lane2 = lax.broadcasted_iota(jnp.int32, (1024, 128), 1)
+
+    def pair_backward(i):
+        p0 = pl.ds(mul(i * 128, 128), 128)
+        for j in range(2):
+            r0 = pl.ds(mul(i * 128 + j * 64, 64), 64)
+            li = linv[2 * i + j, 0:1, :]
+            dd = dot_[r0, :].astype(f32) * li
+            delta = jnp.sum(dd * attt[r0, :].astype(f32), axis=0, keepdims=True)
+            linv[2 * i + j, :, :] = jnp.broadcast_to(delta, (8, 1024))
+            dot_[r0, :] = dd.astype(bf16)
+        do_[...] = dot_[p0, :].T
+        acck[...] = jnp.zeros_like(acck)
+        accv[...] = jnp.zeros_like(accv)
+
+        def queries(qb):
+            q0 = pl.ds(mul(qb * 256, 256), 256)
+            qblk = qkv[q0, p0]
+            doblk = do_[q0, :]
+            dt = dot_[p0, q0]
+
+            def keys(kb, carry):
+                k0 = pl.ds(mul(kb * 256, 256), 256)
+                vblk = qkv[k0, pl.ds(mul(512 + i * 128, 128), 128)]
+                new = []
+                for j in range(2):
+                    p = ptri[2 * i + j, tri(kb, qb)]
+                    dp = nn(half(vblk, j), dt) - linv[2 * i + j, 0:1, q0]
+                    ds = (p.astype(f32) * dp).astype(bf16)
+                    accv[j, k0, :] += nn(p, doblk)
+                    acck[j, k0, :] += nn(ds, qblk)
+                    kk = kt[pl.ds(mul(i * 128 + j * 64, 64), 64), k0]
+                    new.append(carry[j] + nn(kk, ds))
+                return tuple(new)
+
+            zero = jnp.zeros((64, 256), f32)
+            dq = lax.fori_loop(0, qb + 1, keys, (zero, zero))
+            dq = jnp.concatenate(dq, axis=0) * 0.125
+            dmix[q0, pl.ds(mul(i * 128, 128), 128)] = dq.T.astype(bf16)
+
+        loop(4, queries)
+        dk = jnp.where(lane2 < 64, acck[0], acck[1]) * 0.125
+        dv = jnp.where(lane2 < 64, accv[0], accv[1])
+        dmix[:, pl.ds(mul(256 + i * 128, 128), 128)] = dk.astype(bf16)
+        dmix[:, pl.ds(mul(512 + i * 128, 128), 128)] = dv.astype(bf16)
+
+    loop(2, pair_backward)
+
+    rs_sent(rs_s, i_g2)
+
+    def gn1_part(blk, ch, dst):
+        dst[...] = nt(dmix[pl.ds(mul(blk * R + ch * RC, RC), RC), :], wqkv[...])
+
+    i_g1 = take(3 * CH)
+    rs_run(gn1_part, rs_s, rs_r, rs_own, i_g1)
+    dw_zsent(D, i_dwz)
+    dw_z(D, xr_up, own_b, zr_up, fin_up, i_uwx, i_uwz)
+
+    @pl.when(x != k)
+    def _():
+        wait_bytes(xs.at[pl.ds(0, 256), :], ssem.at[i_owx])
+
+    i_qwx, i_qwz = take(2), take(4)
+    dw_run(n1, dmix, 768, xr_qkv, own_a, i_qwx)
+
+    for i in range(2):
+        zi = y + 2 * i
+        dz = (zi - z + 4) % 4
+
+        @pl.when(x == k)
+        def _(i=i, zi=zi, dz=dz):
+            if i == 0:
+                wait_bytes(xr_out, rsem.at[i_owx])
+            half_rows = slice(i * 128, (i + 1) * 128)
+            total = own_out[half_rows, :] + xr_out[half_rows, :].astype(f32)
+
+            @pl.when(zi == z)
+            def _():
+                fin_out[...] = total
+
+            @pl.when(zi != z)
+            def _():
+                zso[i] = total.astype(bf16)
+                rcopy(zso.at[i], zr_out.at[dz - 1], {"seq": zi * 2 + x}, i_owz + dz).start()
+
+        sent(zso.at[i], i_owz + dz, jnp.logical_and(x == k, zi != z))
+
+    for ch in range(CH):
+        rs_wait(rs_s, rs_r, i_g1, ch)
+
+        def fourth(q, ch=ch):
+            r = pl.ds(mul(q * 32, 32), 32)
+            r1 = pl.ds(mul(ch * RC + q * 32, 32), 32)
+            g1 = rs_sum(rs_r, rs_own, ch, r)
+            zz, rstd = layer_stats(tok[r1, :].astype(f32))
+            o_grad[r1, :] += layer_back(g1, vec[0:1, :], zz, rstd)
+            fold = lambda v: jnp.sum(v.reshape(4, 8, D), axis=0)
+            gvec[0] += fold(g1 * zz)
+            gvec[1] += fold(g1)
+
+        loop(RC // 32, fourth)
+
+    gmat[...] = jnp.zeros_like(gmat)
+    for r, v in ((0, 0), (1, 1), (4, 4), (5, 5), (6, 6), (7, 7), (8, 2)):
+        gmat[r : r + 1, :] = jnp.sum(gvec[v], axis=0, keepdims=True)
+    for j, r in ((0, 2), (2, 3)):
+        v = dmix[:, j * 256 : (j + 1) * 256].astype(f32)
+        v = jnp.sum(jnp.sum(v.reshape(128, 8, 256), axis=0), axis=0, keepdims=True)
+        for i in range(2):
+            gmat[r : r + 1, pl.ds(mul((ctx + 4 * i) * 128, 128), 128)] = v[:, i * 128 : (i + 1) * 128]
+    for s in range(8):
+        sg[s] = gmat[:, s * 128 : (s + 1) * 128]
+    i_sgx, i_sgz, i_sgc = take(4), take(4), take(4)
+    for j in range(4):
+        src = sg.at[j * 2 + (x + 1) % 2]
+        rcopy(src, sgx.at[j], xpeer, i_sgx + j).start()
+        sent(src, i_sgx + j)
+
+    dw_zsent(D, i_uwz)
+    dw_z(768, xr_qkv, own_a, zr_qkv, fin_qkv, i_qwx, i_qwz)
+    for j in range(4):
+        rcopy(sg.at[j], sgx.at[j], xpeer, i_sgx + j).wait_recv()
+    for d in (1, 2, 3):
+        zz = (z + d) % 4
+        sgs[d - 1] = sg[zz * 2 + x] + sgx[zz]
+        rcopy(sgs.at[d - 1], sgz.at[d - 1], zpeer(d), i_sgz + d).start()
+        sent(sgs.at[d - 1], i_sgz + d)
+
+    dw_end(zr_down, o_ddown, i_dwz)
+    dw_end(zr_up, fin_up, i_uwz)
+    i_uf, i_qf, i_of = take(4), take(4), take(4)
+
+    def up_piece(fin, c, s):
+        return (fin.at[pl.ds(mul(c * 32, 32), 32), pl.ds(s * 128, 128)],
+                o_dup.at[:, pl.ds(mul((s * 4 + ctx) * 128, 128), 128)])
+
+    for d in (1, 2, 3):
+        for s in range(8):
+            a, b = up_piece(fin_up, (ctx + d) % 4, s)
+            rcopy(a, b, cpeer(d), i_uf + d).start()
+        sent(fin_up.at[pl.ds(0, 32), :], i_uf + d)
+    mine32 = pl.ds(mul(ctx * 32, 32), 32)
+    for s in range(8):
+        o_dup[:, pl.ds(mul((s * 4 + ctx) * 128, 128), 128)] = fin_up[mine32, s * 128 : (s + 1) * 128]
+
+    @pl.when(ctx == t)
+    def _():
+        for d in (1, 2, 3):
+            wait_bytes(zr_out.at[d - 1], rsem.at[i_owz + d])
+        fin_out[...] += (zr_out[0].astype(f32) + zr_out[1].astype(f32)) + zr_out[2].astype(f32)
+        for d in (1, 2, 3):
+            src = fin_out.at[pl.ds(mul(((ctx + d) % 4) * 32, 32), 32), :]
+            rcopy(src, o_dout, cpeer(d), i_of + d).start()
+        o_dout[...] = fin_out[mine32, :]
+
+    for d in (1, 2, 3):
+        sent(fin_out.at[pl.ds(0, 32), :], i_of + d, ctx == t)
+
+    for ch in range(CH):
+        rs_wait(rt_s, rt_r, i_ff, ch)
+
+        def last(q, ch=ch):
+            r = pl.ds(mul(q * 32, 32), 32)
+            r1 = pl.ds(mul(ch * RC + q * 32, 32), 32)
+            ffn = rs_sum(rt_r, rt_own, ch, r) + vec[7:8, :]
+            v = valid_rows(ch * RC + q * 32, 32)
+            o_out[r1, :] = (v * (res[r1, :] + ffn)).astype(bf16)
+            stat[16:24, :] += jnp.sum((ffn * ffn * v).reshape(4, 8, D), axis=0)
+
+        loop(RC // 32, last)
+
+    for d in (1, 2, 3):
+        wait_bytes(sgz.at[d - 1], rsem.at[i_sgz + d])
+    sgf[...] = sg[seq] + sgx[z] + (sgz[0] + sgz[1] + sgz[2])
+    for j in range(3):
+        v = jnp.sum(stat[j * 8 : (j + 1) * 8, :], axis=0, keepdims=True)
+        sgf[9 + j : 10 + j, :] = jnp.broadcast_to(jnp.sum(v, axis=1, keepdims=True), (1, 128))
+    for d in (1, 2, 3):
+        rcopy(sgf, sgc.at[d], cpeer(d), i_sgc + d).start()
+        sent(sgf, i_sgc + d)
+
+    dw_end(zr_qkv, fin_qkv, i_qwz)
+    for d in (1, 2, 3):
+        c2 = (ctx + d) % 4
+        for a, b in qkv_pieces(ctx):
+            rcopy(fin_qkv.at[pl.ds(mul(c2 * 32, 32), 32), b], o_dqkv.at[:, a], cpeer(d), i_qf + d).start()
+        sent(fin_qkv.at[pl.ds(0, 32), :], i_qf + d)
+    for a, b in qkv_pieces(ctx):
+        o_dqkv[:, a] = fin_qkv[mine32, b]
+
+    for d in (1, 2, 3):
+        wait_bytes(sgc.at[d], rsem.at[i_sgc + d])
+    o_small[...] = sgf[...] + jnp.where(rowid != 8, sgc[1] + sgc[2] + sgc[3], 0.0)
+
+    @pl.when(ctx != t)
+    def _():
+        wait_bytes(o_dout, rsem.at[i_of + (ctx - t + 4) % 4])
+
+    for d in (1, 2, 3):
+        wait_bytes(fin_up.at[pl.ds(0, 32), :], rsem.at[i_uf + d])
+        wait_bytes(fin_qkv.at[pl.ds(0, 32), :], rsem.at[i_qf + d])
+    dw_zsent(768, i_qwz)
+    dw_xsent(768, i_qwx)
+    rs_sent(rs_s, i_g1)
+    rs_sent(rt_s, i_ff)
+    flush()
+    assert next(ids) <= NSEM, next(ids)
+
+
+def fast(mesh):
+    def scratch():
+        v = lambda dt, *shape: pltpu.VMEM(shape, dt)
+        return [
+            v(bf16, D, 768), v(bf16, 256, D), v(bf16, D, D), v(bf16, D, D),
+            v(f32, 4, 16, 128), v(f32, 8, 16, 128), v(f32, 16, D),
+            v(bf16, S, D), v(bf16, S, D), v(bf16, S, D), v(bf16, S, D), v(bf16, S, D), v(bf16, S, D),
+            v(bf16, S, 768), v(bf16, 256, S), v(bf16, 256, S), v(bf16, 256, S),
+            v(bf16, 256, S), v(bf16, S, 128), v(bf16, S, 768), v(f32, 4, 8, S),
+            v(bf16, 4, 10, 256, 256), v(f32, 2, S, 128), v(f32, 2, S, 128),
+            v(bf16, 3, 2, 128, D), v(bf16, 3, 2, 128, D), v(f32, 2, 128, D),
+            v(bf16, 3, 2, 128, D), v(bf16, 3, 2, 128, D), v(f32, 2, 128, D),
+            v(f32, 128, D), v(f32, R, D),
+            v(bf16, 512, D), v(bf16, 512, D), v(bf16, 512, D), v(bf16, 512, 768), v(bf16, 256, D),
+            v(f32, 512, D), v(f32, 512, D), v(f32, 256, D),
+            v(bf16, 3, 128, D), v(bf16, 2, 128, D),
+            v(bf16, 3, 128, D), v(bf16, 3, 128, D), v(bf16, 3, 128, 768), v(bf16, 3, 128, D),
+            v(f32, 128, D), v(f32, 128, 768), v(f32, 128, D),
+            v(f32, 8, 16, 128), v(f32, 4, 16, 128), v(f32, 3, 16, 128), v(f32, 3, 16, 128),
+            v(f32, 16, 128), v(f32, 4, 16, 128), v(f32, 8, 8, D), v(f32, 16, D), v(f32, 24, D),
+            pltpu.SemaphoreType.DMA((8,)),
+            pltpu.SemaphoreType.DMA((NSEM,)),
+            pltpu.SemaphoreType.DMA((NSEM,)),
+        ]
+
+    def on_device(tokens, lengths, cotangent, g1, b1, wq, qb, vb, wo, ob, g2, b2, wu, ub, wd, db):
+        ctx = lax.axis_index("ctx")
+        vectors = jnp.stack([g1, b1, qb, vb, ob, g2, b2, db]).astype(f32)
+        place = (jnp.arange(128) // 32) == ctx
+        small = jnp.concatenate([
+            jnp.where(place[None], jnp.tile(vectors, (1, 4)), 0.0),
+            ub.astype(f32)[None], jnp.zeros((7, 128), f32)])
+        vm = pl.BlockSpec(memory_space=pltpu.VMEM)
+        sds = jax.ShapeDtypeStruct
+        out, grad, dqkv, dout, dup, ddown, sums = pl.pallas_call(
+            block_kernel,
+            out_shape=(sds((R, D), bf16), sds((R, D), f32), sds((32, 3 * D), f32), sds((32, D), f32),
+                       sds((32, 4 * D), f32), sds((128, D), f32), sds((16, 128), f32)),
+            in_specs=[pl.BlockSpec(memory_space=pltpu.SMEM)] + [vm] * 7,
+            out_specs=tuple([vm] * 7),
+            scratch_shapes=scratch(),
+            compiler_params=pltpu.CompilerParams(
+                collective_id=0, has_side_effects=True, vmem_limit_bytes=LIMIT),
+            name="block",
+        )(lengths, tokens[0], cotangent[0], small, wq, wo, wu, wd)
+        mine = lax.dynamic_slice(sums, (0, ctx * 32), (8, 32))
+        stats = jnp.sqrt(sums[9:12, 0] / (lengths[0].astype(f32) * D))[None]
+        return (out[None], grad[None], mine[0], mine[1], dqkv, mine[2], mine[3], dout, mine[4],
+                mine[5], mine[6], dup, sums[8], ddown, mine[7], stats)
+
+    return on_device
+
 
 HEADS = 16
 
@@ -305,6 +1196,7 @@
 
 
 def solution(mesh):
+    small_slice = mesh.shape["seq"] == 8 and mesh.shape["ctx"] == 4
     placed = (
         P("seq", "ctx", None),
         P("seq"),
@@ -324,7 +1216,7 @@
         P(("seq", "ctx")),
     )
     return jax.shard_map(
-        on_device,
+        fast(mesh) if small_slice else on_device,
         mesh=mesh,
         in_specs=placed,
         out_specs=(

time: 1240 us -> 267 us (0.22)
  waiting for transfers between devices: 830 us -> 0 us
  Pallas kernels: 0 us -> 249 us
  matrix products: 177 us -> 0 us
  blocking collectives: 117 us -> 0 us
  local copies, waits for them, and re-layouts: 42.4 us -> 10.8 us
  loops' own time: 26.7 us -> 0 us
  other arithmetic: 24.8 us -> 2.01 us
  between operations: 15.3 us -> 1.41 us
    reduce_scatter x6 -> x0, waiting for transfers between devices: 640 us -> none  [the longest x1 188 us: on_device(): lax.psum_scatter(grad_up_w, ('seq', 'ctx'), scatter_dimension=0, tiled=True)]
    pallas_call x0 -> x1, Pallas kernels: none -> 249 us  [on_device(): pl.pallas_call(block_kernel, out_shape=(sds((R, D), bf16), sds((R, D), f3...]
    all_gather x6 -> x0, waiting for transfers between devices: 187 us -> none  [the longest x1 76.3 us: on_device(): lax.all_gather(shards[9], ('seq', 'ctx'), axis=0, tiled=True)]
    dot_general x68 -> x0, matrix products: 177 us -> none  [the longest x4 31.1 us: inner_rows(): lax.dot_general(left, right, (((0,), (0,)), ((), ())), preferred_element_...]
    unnamed x2 -> x0, blocking collectives: 81 us -> none
    all_gather x1 -> x0, blocking collectives: 30 us -> none  [on_device(): lax.all_gather(shards[10], ('seq', 'ctx'), axis=0, tiled=True)]
    another operation x2 -> x0, loops' own time: 26.7 us -> none  [the longest x1 21.1 us: on_device(): lax.map(backward_block, jnp.arange(block_count))]
  transfers between devices with their start and end apart: 12 -> 0, of which waited for: 11 -> 0; matrix products, arithmetic and copies ran while one was open for 10% -> 0% of each run, Pallas kernels for 0% -> 0%
where the time goes in v1:
time: 267 us; the launch traced here: 264 us
  Pallas kernels  249 us (93%)
  local copies, waits for them, and re-layouts  10.8 us (4%)
    pallas_call x1, Pallas kernels, on_device(): pl.pallas_call(block_kernel, out_shape=(sds((R, D), bf16), sds((R, D), f3...  249 us
    unnamed x34, local copies, waits for them, and re-layouts  8.06 us

profile of v1, /device:TPU:21, one launch (start us, length us, event | category | flops | bytes accessed | tf_op | source)
XLA Modules:
  0.0 263.6 jit_solution(11452359893150845762)
XLA Ops:
  0.7 0.0 copy-start.12
  0.7 0.0 copy-start.8
  0.7 0.0 copy-start.9
  0.7 0.0 copy-start.10
  0.7 0.0 copy-start.11
  0.7 0.0 copy-start.5
  0.7 0.0 copy-start.6
  0.7 0.0 copy-start.7
  0.8 0.6 copy-done.12
  1.3 0.0 copy-done.8
  1.3 0.0 copy-done.9
  1.4 0.0 copy-done.10
  1.4 0.0 copy-done.11
  1.4 0.0 copy-done.5
  1.4 0.0 copy-done.6
  1.4 0.0 copy-done.7
  1.5 0.1 tile.10
  1.6 0.0 copy-start.13
  1.6 0.1 pad.2.clone
  1.6 0.6 copy-done.13
  2.2 0.7 maximum_maximum_fusion.small
  3.5 249.4 %block.1 = (bf16[256,1024]{1,0:T(8,128)(2,1)}, f32[256,1024]{1,0:T(8,128)}, f32[32,3072]{1,0:T(8,128)}, f32[32,1024]{1,0:T(8,128)}, f32[32,4096]{1,0:T(8,128)}, /*index=5*/f32[128,1024]{1,0:T(8,128)}, f32[16,128]{1,0:T(8,128)}) custom-call(s32[1]{0:T(128)S(6)} %copy.38.length_ref, bf16[256,1024]{1,0:T(8,128)(2,1)} %bitcast.37, bf16[256,1024]{1,0:T(8,128)(2,1)} %bitcast.38, ...), custom_call_target="tpu_custom_call" | custom-call | tf_op jit(solution)/shard_map/block/pallas_call | solution.py:878
  252.9 0.0 copy-start
  253.0 0.8 constant_dynamic-slice_fusion
  253.8 0.5 slice_bitcast_fusion
  254.3 1.3 sqrt_reduce_fusion
  255.6 1.2 slice_bitcast_fusion.1
  256.8 1.9 copy.39
  258.7 0.0 copy-done
  258.7 0.0 copy-start.3
  258.7 1.0 copy.40
  259.7 0.3 copy-done.3
  259.9 0.0 copy-start.4
  259.9 0.0 copy-start.2
  260.0 0.7 copy.41
  260.7 0.2 copy-done.4
  260.9 0.7 copy.42
  261.6 0.0 copy-done.2
  261.6 0.0 copy-start.1
  261.6 0.8 copy.43
  262.4 0.4 copy-done.1
  262.8 0.8 copy.44
  (6 shorter events, 0.1 us)
Async XLA Ops:
  0.7 0.7 copy-start.12
  0.7 0.7 copy-start.8
  0.7 0.7 copy-start.9
  0.7 0.7 copy-start.10
  0.7 0.7 copy-start.11
  0.7 0.7 copy-start.5
  0.7 0.7 copy-start.6
  0.7 0.7 copy-start.7
  1.6 0.7 copy-start.13
  252.9 5.8 %copy-start = (f32[256,1024]{1,0:T(8,128)S(1)}, f32[256,1024]{1,0:T(8,128)}, u32[]{:S(2)}) copy-start(f32[256,1024]{1,0:T(8,128)} %get-tuple-element.24) | copy-start | bytes 3145732
  258.7 1.2 copy-start.3
  259.9 1.0 copy-start.4
  259.9 1.7 copy-start.2
  261.6 1.2 copy-start.1

commit v2 on v1

--- a/solution.py
+++ b/solution.py
@@ -14,7 +14,8 @@
 R = 256
 S = 1024
 LIMIT = 66_000_000
-NSEM = 200
+NSEM = 260
+ORDER = (2, 3, 1)
 
 
 def nn(a, b):
@@ -63,9 +64,9 @@
     n1, n2, gf, gb, act, gpre, qkv, vt, kt, attt, dot_, do_, dmix, linv,
     ptri, acck, accv,
     rs_s, rs_r, rs_own, rt_s, rt_r, rt_own, tmp, res,
-    xs, xr_down, xr_up, xr_qkv, xr_out, own_a, own_b, own_out,
-    zs, zso, zr_down, zr_up, zr_qkv, zr_out, fin_up, fin_qkv, fin_out,
-    sg, sgx, sgs, sgz, sgf, sgc, gvec, gmat, stat,
+    xs_down, xs_up, xr_down, xr_up, xr_qkv, xr_out, own_a, own_b, own_out,
+    zr_down, zr_up, zr_qkv, zr_out, fin_up, fin_qkv, fin_out,
+    sg, sgx, sgs, sgz, sgf, sgc, gvec, gmat, stat, qbias,
     lsem, ssem, rsem,
 ):
     seq, ctx = lax.axis_index("seq"), lax.axis_index("ctx")
@@ -114,7 +115,7 @@
         sends.clear()
 
     rows = lambda c: pl.ds(mul(c * R, R), R)
-    srow = lambda s: pl.ds(mul(s * 128, 128), 128)
+    srow = lambda s: pl.ds(s * 128 if isinstance(s, int) else mul(s * 128, 128), 128)
 
     barrier = pltpu.get_barrier_semaphore()
     for d in (1, 2, 3):
@@ -131,7 +132,7 @@
 
     def qkv_pieces(c):
         for j in range(6):
-            yield (pl.ds(mul((j // 2) * D + (c + 4 * (j % 2)) * 128, 128), 128),
+            yield (pl.ds(mul((j % 3) * D + (c + 4 * (j // 3)) * 128, 128), 128),
                    pl.ds(j * 128, 128))
 
     i_qa = take(4)
@@ -143,42 +144,6 @@
     for a, b in qkv_pieces(ctx):
         pltpu.make_async_copy(qkv_in.at[:, a], wqkv.at[own32, b], lsem.at[l_q]).start()
 
-    for d in (1, 2, 3):
-        rcopy(small, smc.at[d], cpeer(d), i_smc + d).wait_recv()
-    rowid = lax.broadcasted_iota(jnp.int32, (16, 128), 0)
-    smb[seq] = small[...] + jnp.where(rowid < 8, smc[1] + smc[2] + smc[3], 0.0)
-
-    def gather_start(buf, block, zi, xi, src=None):
-        for d in (1, 2, 3):
-            own = block(seq) if src is None else src
-            rcopy(own, block(seq), zpeer(d), zi + d).start()
-            sent(own, zi + d)
-        own = block(seq) if src is None else src
-        rcopy(own, block(seq), xpeer, xi).start()
-        sent(own, xi)
-
-    def gather_forward(block, zi, xi, d):
-        b = block(((z - d + 4) % 4) * 2 + x)
-        rcopy(b, b, xpeer, zi + d).wait_recv()
-        rcopy(b, b, xpeer, xi + d).start()
-        sent(b, xi + d)
-
-    def gather_finish(block, xi):
-        for d in range(4):
-            b = block(seq)
-            rcopy(b, b, xpeer, xi + d).wait_recv()
-
-    small_block = lambda s: smb.at[s]
-    i_sz, i_sx = take(4), take(4)
-    gather_start(smb, small_block, i_sz, i_sx)
-
-    for d in (1, 2, 3):
-        wait_bytes(wqkv.at[pl.ds(0, 32), :], rsem.at[i_qa + d])
-    wait_bytes(wqkv.at[pl.ds(0, 32), :], lsem.at[l_q])
-    qkv_block = lambda s: wqkv.at[srow(s), :]
-    i_qz, i_qx = take(4), take(4)
-    gather_start(wqkv, qkv_block, i_qz, i_qx)
-
     t = seq % 4
     out32 = pl.ds(mul((seq // 4) * 128 + ctx * 32, 32), 32)
     i_oa = take()
@@ -193,56 +158,6 @@
     @pl.when(ctx == t)
     def _():
         pltpu.make_async_copy(out_in, wout.at[out32, :], lsem.at[l_o]).start()
-
-    for d in (1, 2, 3):
-        gather_forward(small_block, i_sz, i_sx, d)
-    gather_finish(small_block, i_sx)
-    for s in range(8):
-        vec[:, s * 128 : (s + 1) * 128] = smb[s]
-
-    length = length_ref[0]
-    my = mul(ctx * R, R)
-
-    def valid_rows(r0, n):
-        pos = lax.broadcasted_iota(jnp.int32, (n, 1), 0) + (ctx * R + r0)
-        return jnp.where(pos < length, 1.0, 0.0).astype(f32)
-
-    def first(i):
-        r0 = mul(i * 64, 64)
-        zz, _ = layer_stats(tok[pl.ds(r0, 64), :].astype(f32))
-        n1[pl.ds(mul(my + r0, 64), 64), :] = (zz * vec[0:1, :] + vec[1:2, :]).astype(bf16)
-        g = cot[pl.ds(r0, 64), :].astype(f32) * valid_rows(r0, 64)
-        gf[pl.ds(mul(my + r0, 64), 64), :] = g.astype(bf16)
-
-    loop(4, first)
-
-    CH = 2
-    RC = R // CH
-
-    def chunk(buf, c, ch):
-        return buf.at[pl.ds(mul(c * R + ch * RC, RC), RC), :]
-
-    def ag_start(buf, i, ch):
-        own = chunk(buf, ctx, ch)
-        rcopy(own, own, ypeer, i + CH + ch).start()
-        rcopy(own, own, mate, i + ch).start()
-        sent(own, i + CH + ch)
-        sent(own, i + ch)
-
-    def ag_forward(buf, i, ch):
-        b = chunk(buf, ((y + 1) % 2) * 2 + k, ch)
-        rcopy(b, b, mate, i + CH + ch).wait_recv()
-        rcopy(b, b, mate, i + 2 * CH + ch).start()
-        sent(buf.at[pl.ds(0, RC), :], i + 2 * CH + ch)
-
-    def ag_wait(buf, i, which):
-        for ch in range(CH):
-            b = chunk(buf, ctx, ch)
-            rcopy(b, b, mate, i + which * CH + ch).wait_recv()
-
-    i_n1 = take(3 * CH)
-    for ch in range(CH):
-        ag_start(n1, i_n1, ch)
 
     i_ua = take(4)
     for d in (1, 2, 3):
@@ -255,13 +170,164 @@
     for s in range(8):
         pltpu.make_async_copy(up_in.at[:, pl.ds(mul((s * 4 + ctx) * 128, 128), 128)],
                               wup.at[own32, pl.ds(s * 128, 128)], lsem.at[l_u]).start()
+
+    for d in (1, 2, 3):
+        rcopy(small, smc.at[d], cpeer(d), i_smc + d).wait_recv()
+    rowid = lax.broadcasted_iota(jnp.int32, (16, 128), 0)
+    smb[seq] = small[...] + jnp.where(rowid < 8, smc[1] + smc[2] + smc[3], 0.0)
+
+    def gather_z(block, zi, src=None):
+        own = block(seq) if src is None else src
+        for d in ORDER:
+            rcopy(own, block(seq), zpeer(d), zi + d).start()
+            sent(own, zi + d)
+
+    def gather_x(block, xi, src=None):
+        own = block(seq) if src is None else src
+        rcopy(own, block(seq), xpeer, xi).start()
+        sent(own, xi)
+
+    def gather_forward(block, zi, xi, d):
+        b = block(((z - d + 4) % 4) * 2 + x)
+        rcopy(b, b, xpeer, zi + d).wait_recv()
+        rcopy(b, b, xpeer, xi + d).start()
+        sent(block(0), xi + d)
+
+    def gather_finish(block, xi):
+        for d in range(4):
+            b = block(seq)
+            rcopy(b, b, xpeer, xi + d).wait_recv()
+
+    def relay_start(block, i, src=None):
+        own = block(seq) if src is None else src
+        for cond, step, first in ((z < 3, 1, i), (z > 0, -1, i + 4)):
+            @pl.when(cond)
+            def _(step=step, first=first):
+                rcopy(own, block(seq), {"seq": (z + step) * 2 + x}, first + 1).start()
+
+            sent(own, first + 1, cond)
+
+    def relay_x(block, i, src=None):
+        own = block(seq) if src is None else src
+        rcopy(own, block(seq), xpeer, i + 8 + z).start()
+        sent(own, i + 8 + z)
+
+    def relay_step(block, i, j):
+        for has, on, step, first in ((z >= j, z < 3, 1, i), (z + j <= 3, z > 0, -1, i + 4)):
+            zz = z - j * step
+
+            @pl.when(has)
+            def _(on=on, step=step, first=first, zz=zz):
+                b = block(zz * 2 + x)
+                rcopy(b, b, xpeer, first + j).wait_recv()
+                if j < 3:
+                    @pl.when(on)
+                    def _():
+                        rcopy(b, b, {"seq": (z + step) * 2 + x}, first + j + 1).start()
+                rcopy(b, b, xpeer, i + 8 + zz).start()
+
+            if j < 3:
+                sent(block(0), first + j + 1, jnp.logical_and(has, on))
+
+    def relay_finish(block, i):
+        for zz in range(4):
+            rcopy(block(0), block(0), xpeer, i + 8 + zz).wait_recv()
+
+    def relay_sent(block, i):
+        for j in (1, 2, 3):
+            for has, zz in ((z >= j, z - j), (z + j <= 3, z + j)):
+                @pl.when(has)
+                def _(zz=zz):
+                    wait_bytes(block(0), ssem.at[i + 8 + zz])
+
+    small_block = lambda s: smb.at[s]
+    i_sz, i_sx = take(4), take(4)
+    gather_z(small_block, i_sz)
+    gather_x(small_block, i_sx)
+
+    for d in (1, 2, 3):
+        wait_bytes(wqkv.at[pl.ds(0, 32), :], rsem.at[i_qa + d])
+    wait_bytes(wqkv.at[pl.ds(0, 32), :], lsem.at[l_q])
+    qkv_block = lambda s: wqkv.at[srow(s), :]
+    i_qr = take(12)
+    relay_start(qkv_block, i_qr)
+    for d in ORDER:
+        gather_forward(small_block, i_sz, i_sx, d)
+    relay_x(qkv_block, i_qr)
+    l_d = next(lids)
+    down_block = lambda s: wdown.at[srow(s), :]
+    i_dr = take(12)
+    relay_x(down_block, i_dr, src=down_in)
+    pltpu.make_async_copy(down_in, down_block(seq), lsem.at[l_d]).start()
+
+    gather_finish(small_block, i_sx)
+    for s in range(8):
+        vec[:, s * 128 : (s + 1) * 128] = smb[s]
+
+    length = length_ref[0]
+    my = mul(ctx * R, R)
+
+    def valid_rows(r0, n):
+        pos = lax.broadcasted_iota(jnp.int32, (n, 1), 0) + (ctx * R + r0)
+        return jnp.where(pos < length, 1.0, 0.0).astype(f32)
+
+    CH = 2
+    RC = R // CH
+
+    def chunk(buf, c, ch):
+        return buf.at[pl.ds(mul(c * R + ch * RC, RC), RC), :]
+
+    def ag_start(buf, i, ch):
+        own = chunk(buf, ctx, ch)
+        rcopy(own, own, ypeer, i + CH + ch).start()
+        rcopy(own, own, mate, i + ch).start()
+        if buf is not gf and buf is not n2:
+            sent(own, i + CH + ch)
+            sent(own, i + ch)
+
+    def ag_forward(buf, i, ch):
+        b = chunk(buf, ((y + 1) % 2) * 2 + k, ch)
+        rcopy(b, b, mate, i + CH + ch).wait_recv()
+        rcopy(b, b, mate, i + 2 * CH + ch).start()
+        if buf is not gf and buf is not n2:
+            sent(buf.at[pl.ds(0, RC), :], i + 2 * CH + ch)
+
+    def ag_wait(buf, i, which):
+        for ch in range(CH):
+            b = chunk(buf, ctx, ch)
+            rcopy(b, b, mate, i + which * CH + ch).wait_recv()
+
+    i_n1 = take(3 * CH)
+    for ch in range(CH):
+        def first(q, ch=ch):
+            r0 = mul(ch * RC + q * 32, 32)
+            zz, _ = layer_stats(tok[pl.ds(r0, 32), :].astype(f32))
+            n1[pl.ds(mul(my + r0, 32), 32), :] = (zz * vec[0:1, :] + vec[1:2, :]).astype(bf16)
+
+        loop(RC // 32, first)
+        ag_start(n1, i_n1, ch)
+
+
+    def mask_rows(q):
+        r0 = mul(q * 32, 32)
+        g = cot[pl.ds(r0, 32), :].astype(f32) * valid_rows(r0, 32)
+        gf[pl.ds(mul(my + r0, 32), 32), :] = g.astype(bf16)
+
+    loop(R // 32, mask_rows)
     i_gf = take(3 * CH)
     for ch in range(CH):
         ag_start(gf, i_gf, ch)
-    l_d = next(lids)
-    down_block = lambda s: wdown.at[srow(s), :]
-    pltpu.make_async_copy(down_in, down_block(seq), lsem.at[l_d]).start()
-
+    for j in range(6):
+        if j % 3 == 1:
+            qbias[:, j * 128 : (j + 1) * 128] = jnp.zeros((8, 128), f32)
+        else:
+            r = 2 + j % 3 // 2
+            b = vec[r : r + 1, pl.ds(mul((ctx + 4 * (j // 3)) * 128, 128), 128)]
+            qbias[:, j * 128 : (j + 1) * 128] = jnp.broadcast_to(b, (8, 128))
+    relay_step(qkv_block, i_qr, 1)
+    relay_step(qkv_block, i_qr, 2)
+    ag_forward(n1, i_n1, 0)
+    relay_step(qkv_block, i_qr, 3)
     i_oz, i_ox = take(4), take(4)
     out_block = lambda zz: wout.at[pl.ds(mul((zz // 2) * 128, 128), 128), :]
 
@@ -277,22 +343,17 @@
         sent(out_block(z), i_oz + d, ctx == t)
     sent(out_block(z), i_ox, ctx == t)
 
-    for ch in range(CH):
-        ag_forward(n1, i_n1, ch)
-
     for d in (1, 2, 3):
         wait_bytes(wup.at[pl.ds(0, 32), :], rsem.at[i_ua + d])
     wait_bytes(wup.at[pl.ds(0, 32), :], lsem.at[l_u])
     up_block = lambda s: wup.at[srow(s), :]
-    i_uz, i_ux = take(4), take(4)
-    gather_start(wup, up_block, i_uz, i_ux)
-    i_dz, i_dx = take(4), take(4)
-    gather_start(wdown, down_block, i_dz, i_dx, src=down_in)
-
-    for d in (1, 2, 3):
-        gather_forward(qkv_block, i_qz, i_qx, d)
+    i_ur = take(12)
+    relay_start(up_block, i_ur)
+    ag_forward(n1, i_n1, 1)
+
     ag_wait(n1, i_n1, 0)
-    gather_finish(qkv_block, i_qx)
+    relay_finish(qkv_block, i_qr)
+    relay_x(up_block, i_ur)
 
     def project(it):
         blk = ((y + it // 2) % 2) * 2 + (k + it % 2) % 2
@@ -301,21 +362,9 @@
         def _():
             ag_wait(n1, i_n1, 2)
 
-        a = n1[rows(blk), :]
-        for j in range(3):
-            r = nn(a, wqkv[:, j * 256 : (j + 1) * 256])
-            if j != 1:
-                for i in range(2):
-                    b = vec[2 + j // 2 : 3 + j // 2, pl.ds(mul((ctx + 4 * i) * 128, 128), 128)]
-                    qkv[rows(blk), j * 256 + i * 128 : j * 256 + (i + 1) * 128] = (
-                        r[:, i * 128 : (i + 1) * 128] + b).astype(bf16)
-            else:
-                qkv[rows(blk), 256:512] = r.astype(bf16)
+        qkv[rows(blk), :] = (nn(n1[rows(blk), :], wqkv[...]) + qbias[0:1, :]).astype(bf16)
 
     loop(4, project)
-    for ch in range(CH):
-        ag_forward(gf, i_gf, ch)
-
     mine = x == k
     for d in (1, 2, 3):
         zz = (z - d + 4) % 4
@@ -327,10 +376,13 @@
 
         sent(out_block(zz), i_ox + d, jnp.logical_and(mine, zz % 2 == y))
 
+    relay_step(up_block, i_ur, 1)
+    relay_start(down_block, i_dr, src=down_in)
+
     def turn(i):
         c0 = pl.ds(mul(i * 128, 128), 128)
-        vt[c0, :] = qkv[:, pl.ds(mul(512 + i * 128, 128), 128)].T
-        kt[c0, :] = qkv[:, pl.ds(mul(256 + i * 128, 128), 128)].T
+        vt[c0, :] = qkv[:, pl.ds(mul(i * 384 + 256, 128), 128)].T
+        kt[c0, :] = qkv[:, pl.ds(mul(i * 384 + 128, 128), 128)].T
 
     loop(2, turn)
 
@@ -354,11 +406,11 @@
 
         def queries(qb):
             q0 = pl.ds(mul(qb * 256, 256), 256)
-            qblk = qkv[q0, pl.ds(mul(i * 128, 128), 128)]
+            qblk = qkv[q0, pl.ds(mul(i * 384, 128), 128)]
 
             def scores(kb, best):
                 k0 = pl.ds(mul(kb * 256, 256), 256)
-                kblk = qkv[k0, pl.ds(mul(256 + i * 128, 128), 128)]
+                kblk = qkv[k0, pl.ds(mul(i * 384 + 128, 128), 128)]
                 new = []
                 for j in range(2):
                     b = own_b[j * 256 : (j + 1) * 256, pl.ds(mul(kb * 128, 128), 128)]
@@ -394,11 +446,15 @@
 
         loop(4, queries)
 
-    loop(2, pair_forward)
-
+    pair_forward(0)
+    for ch in range(CH):
+        ag_forward(gf, i_gf, ch)
+    pair_forward(1)
+
+    relay_step(up_block, i_ur, 2)
     def rs_run(partial, sb, rb, own, i):
         def step(tt):
-            g, ch, sub = tt // 4, (tt // 2) % 2, tt % 2
+            g, ch, sub = tt // 4, tt % 2, (tt // 2) % 2
             blk = ((y + 1 - g) % 2) * 2 + (k + 1 - sub) % 2
             partial(blk, ch, tmp)
 
@@ -449,9 +505,8 @@
 
     i_br = take(3 * CH)
     rs_run(branch_part, rs_s, rs_r, rs_own, i_br)
-
-    for d in (1, 2, 3):
-        gather_forward(up_block, i_uz, i_ux, d)
+    relay_step(up_block, i_ur, 3)
+    relay_step(down_block, i_dr, 1)
 
     i_n2 = take(3 * CH)
     stat[...] = jnp.zeros_like(stat)
@@ -474,11 +529,8 @@
         loop(RC // 32, second)
         ag_start(n2, i_n2, ch)
 
-    ag_wait(gf, i_gf, 0)
-    ag_wait(gf, i_gf, 2)
-    for d in (1, 2, 3):
-        gather_forward(down_block, i_dz, i_dx, d)
-    gather_finish(up_block, i_ux)
+    relay_step(down_block, i_dr, 2)
+    relay_finish(up_block, i_ur)
 
     def feed(it):
         blk = ((y + it // 2) % 2) * 2 + (k + it % 2) % 2
@@ -486,11 +538,12 @@
         @pl.when(it == 1)
         def _():
             ag_wait(n2, i_n2, 0)
-            for ch in range(CH):
-                ag_forward(n2, i_n2, ch)
-            for d in range(4):
-                rcopy(down_block(seq), down_block(seq), xpeer, i_dx + d).wait_recv()
-            wait_bytes(down_in, lsem.at[l_d])
+            ag_forward(n2, i_n2, 0)
+            relay_step(down_block, i_dr, 3)
+
+        @pl.when(it == 2)
+        def _():
+            ag_forward(n2, i_n2, 1)
 
         @pl.when(it == 3)
         def _():
@@ -510,6 +563,60 @@
         loop(2, cols)
 
     loop(4, feed)
+
+    def dw_half(a, b, c0, n, xx, hh):
+        c1 = pl.ds(mul(((2 * hh) * 2 + xx) * 128, 128), 128)
+        c2 = pl.ds(mul(((2 * hh + 1) * 2 + xx) * 128, 128), 128)
+        return tn(jnp.concatenate([a[:, c1], a[:, c2]], axis=1), b[:, c0 : c0 + n])
+
+    def dw_away(a, b, c0, n, xb, xr, i):
+        def away(hh):
+            r = pl.ds(mul(hh * 256, 256), 256)
+            xb[r, c0 : c0 + n] = dw_half(a, b, c0, n, (x + 1) % 2, hh).astype(bf16)
+            rcopy(xb.at[r, pl.ds(c0, n)], xr.at[r, pl.ds(c0, n)], xpeer, i + hh).start()
+            sent(xb.at[pl.ds(0, 256), pl.ds(c0, n)], i + hh)
+
+        for hh in range(2):
+            away(hh)
+
+    def dw_keep(a, b, c0, n, own):
+        def keep(hh):
+            own[pl.ds(mul(hh * 256, 256), 256), c0 : c0 + n] = dw_half(a, b, c0, n, x, hh)
+
+        loop(2, keep)
+
+    def dw_z(hh, c0, n, xr, own, zb, zo, zr, fin, i, iz):
+        wait_bytes(xr.at[pl.ds(0, 256), pl.ds(c0, n)], rsem.at[i + hh])
+        c = slice(c0, c0 + n)
+        for zz in (2 * hh, 2 * hh + 1):
+            r = slice(zz * 128, zz * 128 + 128)
+            ro = slice(zo + zz * 128, zo + zz * 128 + 128)
+            dz = (zz - z + 4) % 4
+
+            @pl.when(zz == z)
+            def _(r=r):
+                fin[:, c] = own[r, c] + xr[r, c].astype(f32)
+
+            @pl.when(zz != z)
+            def _(r=r, ro=ro, zz=zz, dz=dz):
+                zb[ro, c] = (own[r, c] + xr[r, c].astype(f32)).astype(bf16)
+                rcopy(zb.at[ro, c], zr.at[dz - 1, :, c], {"seq": zz * 2 + x}, iz + dz).start()
+
+            sent(zb.at[ro, c], iz + dz, zz != z)
+
+    def dw_end(c0, n, zr, fin, iz):
+        c = slice(c0, c0 + n)
+        for d in (1, 2, 3):
+            wait_bytes(zr.at[d - 1, :, c], rsem.at[iz + d])
+        fin[:, c] += (zr[0, :, c].astype(f32) + zr[1, :, c].astype(f32)) + zr[2, :, c].astype(f32)
+
+    ag_wait(gf, i_gf, 0)
+    ag_wait(gf, i_gf, 2)
+    i_dwx, i_dwz = take(2), take(4)
+    dw_away(act, gf, 0, D, xs_down, xr_down, i_dwx)
+    dw_keep(act, gf, 0, D, own_a)
+    relay_finish(down_block, i_dr)
+    wait_bytes(down_in, lsem.at[l_d])
     gvec[...] = jnp.zeros_like(gvec)
 
     def grad_feed(it):
@@ -534,49 +641,16 @@
     i_g2 = take(3 * CH)
     rs_run(gn2_part, rs_s, rs_r, rs_own, i_g2)
 
-    def dw_half(a, b, n, xx, hh):
-        c1 = pl.ds(mul(((2 * hh) * 2 + xx) * 128, 128), 128)
-        c2 = pl.ds(mul(((2 * hh + 1) * 2 + xx) * 128, 128), 128)
-        return tn(jnp.concatenate([a[:, c1], a[:, c2]], axis=1), b[:, 0:n])
-
-    def dw_run(a, b, n, xr, own, i, before=None):
-        def away(hh):
-            xs[pl.ds(mul(hh * 256, 256), 256), 0:n] = dw_half(a, b, n, (x + 1) % 2, hh).astype(bf16)
-            s0 = xs.at[pl.ds(mul(hh * 256, 256), 256), pl.ds(0, n)]
-            rcopy(s0, xr.at[pl.ds(mul(hh * 256, 256), 256), :], xpeer, i + hh).start()
-
-        loop(2, away)
-
-        def keep(hh):
-            own[pl.ds(mul(hh * 256, 256), 256), 0:n] = dw_half(a, b, n, x, hh)
-
-        loop(2, keep)
-
-    def dw_xsent(n, i):
-        for hh in range(2):
-            wait_bytes(xs.at[pl.ds(0, 256), pl.ds(0, n)], ssem.at[i + hh])
-
-    def dw_z(n, xr, own, zr, fin, i, iz):
-        for hh in range(2):
-            wait_bytes(xr.at[pl.ds(0, 256), :], rsem.at[i + hh])
-        for d in (1, 2, 3):
-            blk = srow((z + d) % 4)
-            zs[d - 1, :, 0:n] = (own[blk, 0:n] + xr[blk, :].astype(f32)).astype(bf16)
-            rcopy(zs.at[d - 1, :, pl.ds(0, n)], zr.at[d - 1], zpeer(d), iz + d).start()
-        blk = srow(z)
-        fin[...] = own[blk, 0:n] + xr[blk, :].astype(f32)
-
-    def dw_zsent(n, iz):
-        for d in (1, 2, 3):
-            wait_bytes(zs.at[d - 1, :, pl.ds(0, n)], ssem.at[iz + d])
-
-    def dw_end(zr, fin, iz):
-        for d in (1, 2, 3):
-            wait_bytes(zr.at[d - 1], rsem.at[iz + d])
-        fin[...] += (zr[0].astype(f32) + zr[1].astype(f32)) + zr[2].astype(f32)
-
-    i_dwx, i_dwz = take(2), take(4)
-    dw_run(act, gf, D, xr_down, own_a, i_dwx)
+    def down_z(hh):
+        dw_z(hh, 0, D, xr_down, own_a, gpre, 0, zr_down, o_ddown, i_dwx, i_dwz)
+
+    def up_z(hh):
+        dw_z(hh, 0, D, xr_up, own_b, gpre, 512, zr_up, fin_up, i_uwx, i_uwz)
+
+    i_uwx, i_uwz = take(2), take(4)
+    dw_away(n2, gpre, 0, D, xs_up, xr_up, i_uwx)
+    dw_keep(n2, gpre, 0, D, own_b)
+    down_z(0)
 
     i_gb = take(3 * CH)
     for ch in range(CH):
@@ -601,18 +675,15 @@
         loop(RC // 32, third)
         ag_start(gb, i_gb, ch)
 
-    dw_xsent(D, i_dwx)
-    i_uwx, i_uwz = take(2), take(4)
-    dw_run(n2, gpre, D, xr_up, own_b, i_uwx)
-    dw_z(D, xr_down, own_a, zr_down, o_ddown, i_dwx, i_dwz)
-    for ch in range(CH):
-        ag_forward(gb, i_gb, ch)
+    down_z(1)
+    ag_forward(gb, i_gb, 0)
 
     def ffn_part(blk, ch, dst):
         dst[...] = nn(act[pl.ds(mul(blk * R + ch * RC, RC), RC), :], wdown[...])
 
     i_ff = take(3 * CH)
     rs_run(ffn_part, rt_s, rt_r, rt_own, i_ff)
+    ag_forward(gb, i_gb, 1)
 
     ag_wait(gb, i_gb, 0)
     ag_wait(gb, i_gb, 2)
@@ -624,13 +695,17 @@
     loop(4, att_grad)
     own_out[...] = nn(attt[...], gb[...])
     i_owx, i_owz = take(), take(4)
-
-    dw_xsent(D, i_uwx)
+    for j in range(3 * CH):
+        wait_bytes(gf.at[pl.ds(0, RC), :], ssem.at[i_gf + j])
+        wait_bytes(n2.at[pl.ds(0, RC), :], ssem.at[i_n2 + j])
+    xs_out = gf.at[pl.ds(512, 256), :]
 
     @pl.when(x != k)
     def _():
-        xs[0:256, :] = own_out[...].astype(bf16)
-        rcopy(xs.at[pl.ds(0, 256), :], xr_out, xpeer, i_owx).start()
+        gf[512:768, :] = own_out[...].astype(bf16)
+        rcopy(xs_out, xr_out, xpeer, i_owx).start()
+
+    sent(xs_out, i_owx, x != k)
 
     lane2 = lax.broadcasted_iota(jnp.int32, (1024, 128), 1)
 
@@ -649,13 +724,13 @@
 
         def queries(qb):
             q0 = pl.ds(mul(qb * 256, 256), 256)
-            qblk = qkv[q0, p0]
+            qblk = qkv[q0, pl.ds(mul(i * 384, 128), 128)]
             doblk = do_[q0, :]
             dt = dot_[p0, q0]
 
             def keys(kb, carry):
                 k0 = pl.ds(mul(kb * 256, 256), 256)
-                vblk = qkv[k0, pl.ds(mul(512 + i * 128, 128), 128)]
+                vblk = qkv[k0, pl.ds(mul(i * 384 + 256, 128), 128)]
                 new = []
                 for j in range(2):
                     p = ptri[2 * i + j, tri(kb, qb)]
@@ -670,15 +745,19 @@
             zero = jnp.zeros((64, 256), f32)
             dq = lax.fori_loop(0, qb + 1, keys, (zero, zero))
             dq = jnp.concatenate(dq, axis=0) * 0.125
-            dmix[q0, pl.ds(mul(i * 128, 128), 128)] = dq.T.astype(bf16)
+            dmix[q0, pl.ds(mul(i * 384, 128), 128)] = dq.T.astype(bf16)
 
         loop(4, queries)
         dk = jnp.where(lane2 < 64, acck[0], acck[1]) * 0.125
         dv = jnp.where(lane2 < 64, accv[0], accv[1])
-        dmix[:, pl.ds(mul(256 + i * 128, 128), 128)] = dk.astype(bf16)
-        dmix[:, pl.ds(mul(512 + i * 128, 128), 128)] = dv.astype(bf16)
-
-    loop(2, pair_backward)
+        dmix[:, pl.ds(mul(i * 384 + 128, 128), 128)] = dk.astype(bf16)
+        dmix[:, pl.ds(mul(i * 384 + 256, 128), 128)] = dv.astype(bf16)
+
+    up_z(0)
+    pair_backward(0)
+    i_qwx, i_qwz = (take(2), take(2)), (take(4), take(4))
+    dw_away(n1, dmix, 0, 384, gf, xr_qkv, i_qwx[0])
+    pair_backward(1)
 
     rs_sent(rs_s, i_g2)
 
@@ -686,16 +765,10 @@
         dst[...] = nt(dmix[pl.ds(mul(blk * R + ch * RC, RC), RC), :], wqkv[...])
 
     i_g1 = take(3 * CH)
+    up_z(1)
     rs_run(gn1_part, rs_s, rs_r, rs_own, i_g1)
-    dw_zsent(D, i_dwz)
-    dw_z(D, xr_up, own_b, zr_up, fin_up, i_uwx, i_uwz)
-
-    @pl.when(x != k)
-    def _():
-        wait_bytes(xs.at[pl.ds(0, 256), :], ssem.at[i_owx])
-
-    i_qwx, i_qwz = take(2), take(4)
-    dw_run(n1, dmix, 768, xr_qkv, own_a, i_qwx)
+    dw_away(n1, dmix, 384, 384, gf, xr_qkv, i_qwx[1])
+    dw_keep(n1, dmix, 0, 768, own_a)
 
     for i in range(2):
         zi = y + 2 * i
@@ -714,10 +787,10 @@
 
             @pl.when(zi != z)
             def _():
-                zso[i] = total.astype(bf16)
-                rcopy(zso.at[i], zr_out.at[dz - 1], {"seq": zi * 2 + x}, i_owz + dz).start()
-
-        sent(zso.at[i], i_owz + dz, jnp.logical_and(x == k, zi != z))
+                n2[512 + i * 128 : 640 + i * 128, :] = total.astype(bf16)
+                rcopy(n2.at[pl.ds(512 + i * 128, 128), :], zr_out.at[dz - 1], {"seq": zi * 2 + x}, i_owz + dz).start()
+
+        sent(n2.at[pl.ds(512, 128), :], i_owz + dz, jnp.logical_and(x == k, zi != z))
 
     for ch in range(CH):
         rs_wait(rs_s, rs_r, i_g1, ch)
@@ -737,11 +810,11 @@
     gmat[...] = jnp.zeros_like(gmat)
     for r, v in ((0, 0), (1, 1), (4, 4), (5, 5), (6, 6), (7, 7), (8, 2)):
         gmat[r : r + 1, :] = jnp.sum(gvec[v], axis=0, keepdims=True)
-    for j, r in ((0, 2), (2, 3)):
-        v = dmix[:, j * 256 : (j + 1) * 256].astype(f32)
-        v = jnp.sum(jnp.sum(v.reshape(128, 8, 256), axis=0), axis=0, keepdims=True)
+    for r, p in ((2, 0), (3, 256)):
         for i in range(2):
-            gmat[r : r + 1, pl.ds(mul((ctx + 4 * i) * 128, 128), 128)] = v[:, i * 128 : (i + 1) * 128]
+            v = dmix[:, i * 384 + p : i * 384 + p + 128].astype(f32)
+            v = jnp.sum(jnp.sum(v.reshape(128, 8, 128), axis=0), axis=0, keepdims=True)
+            gmat[r : r + 1, pl.ds(mul((ctx + 4 * i) * 128, 128), 128)] = v
     for s in range(8):
         sg[s] = gmat[:, s * 128 : (s + 1) * 128]
     i_sgx, i_sgz, i_sgc = take(4), take(4), take(4)
@@ -750,8 +823,9 @@
         rcopy(src, sgx.at[j], xpeer, i_sgx + j).start()
         sent(src, i_sgx + j)
 
-    dw_zsent(D, i_uwz)
-    dw_z(768, xr_qkv, own_a, zr_qkv, fin_qkv, i_qwx, i_qwz)
+    for h in range(2):
+        for hh in range(2):
+            dw_z(hh, h * 384, 384, xr_qkv, own_a, n2, 0, zr_qkv, fin_qkv, i_qwx[h], i_qwz[h])
     for j in range(4):
         rcopy(sg.at[j], sgx.at[j], xpeer, i_sgx + j).wait_recv()
     for d in (1, 2, 3):
@@ -760,8 +834,8 @@
         rcopy(sgs.at[d - 1], sgz.at[d - 1], zpeer(d), i_sgz + d).start()
         sent(sgs.at[d - 1], i_sgz + d)
 
-    dw_end(zr_down, o_ddown, i_dwz)
-    dw_end(zr_up, fin_up, i_uwz)
+    dw_end(0, D, zr_down, o_ddown, i_dwz)
+    dw_end(0, D, zr_up, fin_up, i_uwz)
     i_uf, i_qf, i_of = take(4), take(4), take(4)
 
     def up_piece(fin, c, s):
@@ -813,7 +887,8 @@
         rcopy(sgf, sgc.at[d], cpeer(d), i_sgc + d).start()
         sent(sgf, i_sgc + d)
 
-    dw_end(zr_qkv, fin_qkv, i_qwz)
+    for h in range(2):
+        dw_end(h * 384, 384, zr_qkv, fin_qkv, i_qwz[h])
     for d in (1, 2, 3):
         c2 = (ctx + d) % 4
         for a, b in qkv_pieces(ctx):
@@ -833,10 +908,10 @@
     for d in (1, 2, 3):
         wait_bytes(fin_up.at[pl.ds(0, 32), :], rsem.at[i_uf + d])
         wait_bytes(fin_qkv.at[pl.ds(0, 32), :], rsem.at[i_qf + d])
-    dw_zsent(768, i_qwz)
-    dw_xsent(768, i_qwx)
     rs_sent(rs_s, i_g1)
     rs_sent(rt_s, i_ff)
+    for block, i in ((qkv_block, i_qr), (up_block, i_ur), (down_block, i_dr)):
+        relay_sent(block, i)
     flush()
     assert next(ids) <= NSEM, next(ids)
 
@@ -854,13 +929,12 @@
             v(bf16, 3, 2, 128, D), v(bf16, 3, 2, 128, D), v(f32, 2, 128, D),
             v(bf16, 3, 2, 128, D), v(bf16, 3, 2, 128, D), v(f32, 2, 128, D),
             v(f32, 128, D), v(f32, R, D),
-            v(bf16, 512, D), v(bf16, 512, D), v(bf16, 512, D), v(bf16, 512, 768), v(bf16, 256, D),
+            v(bf16, 512, D), v(bf16, 512, D), v(bf16, 512, D), v(bf16, 512, D), v(bf16, 512, 768), v(bf16, 256, D),
             v(f32, 512, D), v(f32, 512, D), v(f32, 256, D),
-            v(bf16, 3, 128, D), v(bf16, 2, 128, D),
             v(bf16, 3, 128, D), v(bf16, 3, 128, D), v(bf16, 3, 128, 768), v(bf16, 3, 128, D),
             v(f32, 128, D), v(f32, 128, 768), v(f32, 128, D),
             v(f32, 8, 16, 128), v(f32, 4, 16, 128), v(f32, 3, 16, 128), v(f32, 3, 16, 128),
-            v(f32, 16, 128), v(f32, 4, 16, 128), v(f32, 8, 8, D), v(f32, 16, D), v(f32, 24, D),
+            v(f32, 16, 128), v(f32, 4, 16, 128), v(f32, 8, 8, D), v(f32, 16, D), v(f32, 24, D), v(f32, 8, 768),
             pltpu.SemaphoreType.DMA((8,)),
             pltpu.SemaphoreType.DMA((NSEM,)),
             pltpu.SemaphoreType.DMA((NSEM,)),

time: 267 us -> 210 us (0.79); the launches traced: 264 us -> 210 us
  Pallas kernels: 249 us -> 195 us
    pallas_call x1, Pallas kernels: 249 us -> 195 us  [on_device(): pl.pallas_call(block_kernel, out_shape=(sds((R, D), bf16), sds((R, D), f3...]
where the time goes in v2:
time: 210 us
  Pallas kernels  195 us (93%)
  local copies, waits for them, and re-layouts  10.8 us (5%)
    pallas_call x1, Pallas kernels, on_device(): pl.pallas_call(block_kernel, out_shape=(sds((R, D), bf16), sds((R, D), f3...  195 us
    unnamed x34, local copies, waits for them, and re-layouts  8.06 us

profile of v2, /device:TPU:21, one launch (start us, length us, event | category | flops | bytes accessed | tf_op | source)
XLA Modules:
  0.0 209.6 jit_solution(5061865403621458134)
XLA Ops:
  0.7 0.0 copy-start.12
  0.7 0.0 copy-start.8
  0.7 0.0 copy-start.9
  0.7 0.0 copy-start.10
  0.7 0.0 copy-start.11
  0.7 0.0 copy-start.5
  0.7 0.0 copy-start.6
  0.7 0.0 copy-start.7
  0.8 0.6 copy-done.12
  1.3 0.0 copy-done.8
  1.3 0.0 copy-done.9
  1.4 0.0 copy-done.10
  1.4 0.0 copy-done.11
  1.4 0.0 copy-done.5
  1.4 0.0 copy-done.6
  1.4 0.0 copy-done.7
  1.5 0.1 tile.10
  1.6 0.0 copy-start.13
  1.6 0.1 pad.2.clone
  1.6 0.6 copy-done.13
  2.2 0.7 maximum_maximum_fusion.small
  3.5 195.3 %block.1 = (bf16[256,1024]{1,0:T(8,128)(2,1)}, f32[256,1024]{1,0:T(8,128)}, f32[32,3072]{1,0:T(8,128)}, f32[32,1024]{1,0:T(8,128)}, f32[32,4096]{1,0:T(8,128)}, /*index=5*/f32[128,1024]{1,0:T(8,128)}, f32[16,128]{1,0:T(8,128)}) custom-call(s32[1]{0:T(128)S(6)} %copy.38.length_ref, bf16[256,1024]{1,0:T(8,128)(2,1)} %bitcast.37, bf16[256,1024]{1,0:T(8,128)(2,1)} %bitcast.38, ...), custom_call_target="tpu_custom_call" | custom-call | tf_op jit(solution)/shard_map/block/pallas_call | solution.py:952
  198.9 0.0 copy-start
  198.9 0.8 constant_dynamic-slice_fusion
  199.7 0.5 slice_bitcast_fusion
  200.3 1.3 sqrt_reduce_fusion
  201.6 1.2 slice_bitcast_fusion.1
  202.8 1.9 copy.39
  204.7 0.0 copy-done
  204.7 0.0 copy-start.3
  204.7 1.0 copy.40
  205.6 0.3 copy-done.3
  205.9 0.0 copy-start.4
  205.9 0.0 copy-start.2
  205.9 0.7 copy.41
  206.7 0.2 copy-done.4
  206.9 0.7 copy.42
  207.6 0.0 copy-done.2
  207.6 0.0 copy-start.1
  207.6 0.8 copy.43
  208.4 0.4 copy-done.1
  208.8 0.8 copy.44
  (6 shorter events, 0.1 us)
Async XLA Ops:
  0.7 0.7 copy-start.12
  0.7 0.7 copy-start.8
  0.7 0.7 copy-start.9
  0.7 0.7 copy-start.10
  0.7 0.7 copy-start.11
  0.7 0.7 copy-start.5
  0.7 0.7 copy-start.6
  0.7 0.7 copy-start.7
  1.6 0.7 copy-start.13
  198.9 5.8 %copy-start = (f32[256,1024]{1,0:T(8,128)S(1)}, f32[256,1024]{1,0:T(8,128)}, u32[]{:S(2)}) copy-start(f32[256,1024]{1,0:T(8,128)} %get-tuple-element.24) | copy-start | bytes 3145732
  204.7 1.2 copy-start.3
  205.9 1.0 copy-start.4
  205.9 1.7 copy-start.2
  207.6 1.2 copy-start.1

commit v3 on v2

--- a/solution.py
+++ b/solution.py
@@ -66,7 +66,7 @@
     rs_s, rs_r, rs_own, rt_s, rt_r, rt_own, tmp, res,
     xs_down, xs_up, xr_down, xr_up, xr_qkv, xr_out, own_a, own_b, own_out,
     zr_down, zr_up, zr_qkv, zr_out, fin_up, fin_qkv, fin_out,
-    sg, sgx, sgs, sgz, sgf, sgc, gvec, gmat, stat, qbias,
+    st_out, st_grad, fin_down, sg, sgx, sgs, sgz, sgf, sgc, gvec, gmat, stat, qbias,
     lsem, ssem, rsem,
 ):
     seq, ctx = lax.axis_index("seq"), lax.axis_index("ctx")
@@ -326,8 +326,6 @@
             qbias[:, j * 128 : (j + 1) * 128] = jnp.broadcast_to(b, (8, 128))
     relay_step(qkv_block, i_qr, 1)
     relay_step(qkv_block, i_qr, 2)
-    ag_forward(n1, i_n1, 0)
-    relay_step(qkv_block, i_qr, 3)
     i_oz, i_ox = take(4), take(4)
     out_block = lambda zz: wout.at[pl.ds(mul((zz // 2) * 128, 128), 128), :]
 
@@ -343,6 +341,8 @@
         sent(out_block(z), i_oz + d, ctx == t)
     sent(out_block(z), i_ox, ctx == t)
 
+    ag_forward(n1, i_n1, 0)
+    relay_step(qkv_block, i_qr, 3)
     for d in (1, 2, 3):
         wait_bytes(wup.at[pl.ds(0, 32), :], rsem.at[i_ua + d])
     wait_bytes(wup.at[pl.ds(0, 32), :], lsem.at[l_u])
@@ -353,18 +353,6 @@
 
     ag_wait(n1, i_n1, 0)
     relay_finish(qkv_block, i_qr)
-    relay_x(up_block, i_ur)
-
-    def project(it):
-        blk = ((y + it // 2) % 2) * 2 + (k + it % 2) % 2
-
-        @pl.when(it == 3)
-        def _():
-            ag_wait(n1, i_n1, 2)
-
-        qkv[rows(blk), :] = (nn(n1[rows(blk), :], wqkv[...]) + qbias[0:1, :]).astype(bf16)
-
-    loop(4, project)
     mine = x == k
     for d in (1, 2, 3):
         zz = (z - d + 4) % 4
@@ -375,7 +363,18 @@
             rcopy(out_block(zz), out_block(zz), xpeer, i_ox + d).start()
 
         sent(out_block(zz), i_ox + d, jnp.logical_and(mine, zz % 2 == y))
-
+    relay_x(up_block, i_ur)
+
+    def project(it):
+        blk = ((y + it // 2) % 2) * 2 + (k + it % 2) % 2
+
+        @pl.when(it == 3)
+        def _():
+            ag_wait(n1, i_n1, 2)
+
+        qkv[rows(blk), :] = (nn(n1[rows(blk), :], wqkv[...]) + qbias[0:1, :]).astype(bf16)
+
+    loop(4, project)
     relay_step(up_block, i_ur, 1)
     relay_start(down_block, i_dr, src=down_in)
 
@@ -565,8 +564,8 @@
     loop(4, feed)
 
     def dw_half(a, b, c0, n, xx, hh):
-        c1 = pl.ds(mul(((2 * hh) * 2 + xx) * 128, 128), 128)
-        c2 = pl.ds(mul(((2 * hh + 1) * 2 + xx) * 128, 128), 128)
+        c1 = pl.ds(mul((hh * 2 + xx) * 128, 128), 128)
+        c2 = pl.ds(mul(((3 - hh) * 2 + xx) * 128, 128), 128)
         return tn(jnp.concatenate([a[:, c1], a[:, c2]], axis=1), b[:, c0 : c0 + n])
 
     def dw_away(a, b, c0, n, xb, xr, i):
@@ -588,8 +587,8 @@
     def dw_z(hh, c0, n, xr, own, zb, zo, zr, fin, i, iz):
         wait_bytes(xr.at[pl.ds(0, 256), pl.ds(c0, n)], rsem.at[i + hh])
         c = slice(c0, c0 + n)
-        for zz in (2 * hh, 2 * hh + 1):
-            r = slice(zz * 128, zz * 128 + 128)
+        for sub, zz in enumerate((hh, 3 - hh)):
+            r = slice(hh * 256 + sub * 128, hh * 256 + sub * 128 + 128)
             ro = slice(zo + zz * 128, zo + zz * 128 + 128)
             dz = (zz - z + 4) % 4
 
@@ -642,7 +641,7 @@
     rs_run(gn2_part, rs_s, rs_r, rs_own, i_g2)
 
     def down_z(hh):
-        dw_z(hh, 0, D, xr_down, own_a, gpre, 0, zr_down, o_ddown, i_dwx, i_dwz)
+        dw_z(hh, 0, D, xr_down, own_a, gpre, 0, zr_down, fin_down, i_dwx, i_dwz)
 
     def up_z(hh):
         dw_z(hh, 0, D, xr_up, own_b, gpre, 512, zr_up, fin_up, i_uwx, i_uwz)
@@ -663,7 +662,7 @@
             zz, rstd = layer_stats(res[r1, :])
             gout = cot[r1, :].astype(f32) * valid_rows(ch * RC + q * 32, 32)
             gres = gout + layer_back(g2, vec[5:6, :], zz, rstd)
-            o_grad[r1, :] = gres
+            st_grad[r1, :] = gres
             low = gres.astype(bf16)
             gb[pl.ds(mul(my + ch * RC + q * 32, 32), 32), :] = low
             fold = lambda v: jnp.sum(v.reshape(4, 8, D), axis=0)
@@ -770,6 +769,10 @@
     dw_away(n1, dmix, 384, 384, gf, xr_qkv, i_qwx[1])
     dw_keep(n1, dmix, 0, 768, own_a)
 
+    def qkv_z(h):
+        for hh in range(2):
+            dw_z(hh, h * 384, 384, xr_qkv, own_a, n2, 0, zr_qkv, fin_qkv, i_qwx[h], i_qwz[h])
+
     for i in range(2):
         zi = y + 2 * i
         dz = (zi - z + 4) % 4
@@ -792,6 +795,7 @@
 
         sent(n2.at[pl.ds(512, 128), :], i_owz + dz, jnp.logical_and(x == k, zi != z))
 
+    qkv_z(0)
     for ch in range(CH):
         rs_wait(rs_s, rs_r, i_g1, ch)
 
@@ -800,12 +804,14 @@
             r1 = pl.ds(mul(ch * RC + q * 32, 32), 32)
             g1 = rs_sum(rs_r, rs_own, ch, r)
             zz, rstd = layer_stats(tok[r1, :].astype(f32))
-            o_grad[r1, :] += layer_back(g1, vec[0:1, :], zz, rstd)
+            st_grad[r1, :] += layer_back(g1, vec[0:1, :], zz, rstd)
             fold = lambda v: jnp.sum(v.reshape(4, 8, D), axis=0)
             gvec[0] += fold(g1 * zz)
             gvec[1] += fold(g1)
 
         loop(RC // 32, fourth)
+    l_g = next(lids)
+    pltpu.make_async_copy(st_grad, o_grad, lsem.at[l_g]).start()
 
     gmat[...] = jnp.zeros_like(gmat)
     for r, v in ((0, 0), (1, 1), (4, 4), (5, 5), (6, 6), (7, 7), (8, 2)):
@@ -823,9 +829,7 @@
         rcopy(src, sgx.at[j], xpeer, i_sgx + j).start()
         sent(src, i_sgx + j)
 
-    for h in range(2):
-        for hh in range(2):
-            dw_z(hh, h * 384, 384, xr_qkv, own_a, n2, 0, zr_qkv, fin_qkv, i_qwx[h], i_qwz[h])
+    qkv_z(1)
     for j in range(4):
         rcopy(sg.at[j], sgx.at[j], xpeer, i_sgx + j).wait_recv()
     for d in (1, 2, 3):
@@ -834,9 +838,11 @@
         rcopy(sgs.at[d - 1], sgz.at[d - 1], zpeer(d), i_sgz + d).start()
         sent(sgs.at[d - 1], i_sgz + d)
 
-    dw_end(0, D, zr_down, o_ddown, i_dwz)
+    dw_end(0, D, zr_down, fin_down, i_dwz)
+    l_dd = next(lids)
+    pltpu.make_async_copy(fin_down, o_ddown, lsem.at[l_dd]).start()
     dw_end(0, D, zr_up, fin_up, i_uwz)
-    i_uf, i_qf, i_of = take(4), take(4), take(4)
+    i_uf, i_qf, i_of = take(4), (take(4), take(4)), take(4)
 
     def up_piece(fin, c, s):
         return (fin.at[pl.ds(mul(c * 32, 32), 32), pl.ds(s * 128, 128)],
@@ -848,8 +854,12 @@
             rcopy(a, b, cpeer(d), i_uf + d).start()
         sent(fin_up.at[pl.ds(0, 32), :], i_uf + d)
     mine32 = pl.ds(mul(ctx * 32, 32), 32)
+    l_up = next(lids)
     for s in range(8):
-        o_dup[:, pl.ds(mul((s * 4 + ctx) * 128, 128), 128)] = fin_up[mine32, s * 128 : (s + 1) * 128]
+        a, b = up_piece(fin_up, ctx, s)
+        pltpu.make_async_copy(a, b, lsem.at[l_up]).start()
+
+    l_do = next(lids)
 
     @pl.when(ctx == t)
     def _():
@@ -859,7 +869,7 @@
         for d in (1, 2, 3):
             src = fin_out.at[pl.ds(mul(((ctx + d) % 4) * 32, 32), 32), :]
             rcopy(src, o_dout, cpeer(d), i_of + d).start()
-        o_dout[...] = fin_out[mine32, :]
+        pltpu.make_async_copy(fin_out.at[mine32, :], o_dout, lsem.at[l_do]).start()
 
     for d in (1, 2, 3):
         sent(fin_out.at[pl.ds(0, 32), :], i_of + d, ctx == t)
@@ -872,10 +882,12 @@
             r1 = pl.ds(mul(ch * RC + q * 32, 32), 32)
             ffn = rs_sum(rt_r, rt_own, ch, r) + vec[7:8, :]
             v = valid_rows(ch * RC + q * 32, 32)
-            o_out[r1, :] = (v * (res[r1, :] + ffn)).astype(bf16)
+            st_out[r1, :] = (v * (res[r1, :] + ffn)).astype(bf16)
             stat[16:24, :] += jnp.sum((ffn * ffn * v).reshape(4, 8, D), axis=0)
 
         loop(RC // 32, last)
+    l_t = next(lids)
+    pltpu.make_async_copy(st_out, o_out, lsem.at[l_t]).start()
 
     for d in (1, 2, 3):
         wait_bytes(sgz.at[d - 1], rsem.at[i_sgz + d])
@@ -887,15 +899,18 @@
         rcopy(sgf, sgc.at[d], cpeer(d), i_sgc + d).start()
         sent(sgf, i_sgc + d)
 
+    l_dq = []
     for h in range(2):
         dw_end(h * 384, 384, zr_qkv, fin_qkv, i_qwz[h])
-    for d in (1, 2, 3):
-        c2 = (ctx + d) % 4
-        for a, b in qkv_pieces(ctx):
-            rcopy(fin_qkv.at[pl.ds(mul(c2 * 32, 32), 32), b], o_dqkv.at[:, a], cpeer(d), i_qf + d).start()
-        sent(fin_qkv.at[pl.ds(0, 32), :], i_qf + d)
-    for a, b in qkv_pieces(ctx):
-        o_dqkv[:, a] = fin_qkv[mine32, b]
+        pieces = list(qkv_pieces(ctx))[3 * h : 3 * h + 3]
+        for d in (1, 2, 3):
+            c2 = (ctx + d) % 4
+            for a, b in pieces:
+                rcopy(fin_qkv.at[pl.ds(mul(c2 * 32, 32), 32), b], o_dqkv.at[:, a], cpeer(d), i_qf[h] + d).start()
+            sent(fin_qkv.at[pl.ds(0, 32), pl.ds(0, 384)], i_qf[h] + d)
+        l_dq.append(next(lids))
+        for a, b in pieces:
+            pltpu.make_async_copy(fin_qkv.at[mine32, b], o_dqkv.at[:, a], lsem.at[l_dq[h]]).start()
 
     for d in (1, 2, 3):
         wait_bytes(sgc.at[d], rsem.at[i_sgc + d])
@@ -903,17 +918,49 @@
 
     @pl.when(ctx != t)
     def _():
-        wait_bytes(o_dout, rsem.at[i_of + (ctx - t + 4) % 4])
+        wait_bytes(fin_out.at[pl.ds(0, 32), :], rsem.at[i_of + (ctx - t + 4) % 4])
+
+    @pl.when(ctx == t)
+    def _():
+        wait_bytes(fin_out.at[pl.ds(0, 32), :], lsem.at[l_do])
 
     for d in (1, 2, 3):
         wait_bytes(fin_up.at[pl.ds(0, 32), :], rsem.at[i_uf + d])
-        wait_bytes(fin_qkv.at[pl.ds(0, 32), :], rsem.at[i_qf + d])
+        for h in range(2):
+            wait_bytes(fin_qkv.at[pl.ds(0, 32), pl.ds(0, 384)], rsem.at[i_qf[h] + d])
     rs_sent(rs_s, i_g1)
     rs_sent(rt_s, i_ff)
     for block, i in ((qkv_block, i_qr), (up_block, i_ur), (down_block, i_dr)):
         relay_sent(block, i)
     flush()
+    for ref, i in ((st_grad, l_g), (st_out, l_t), (fin_down, l_dd), (fin_up.at[pl.ds(0, 32), :], l_up),
+                   (fin_qkv.at[pl.ds(0, 32), pl.ds(0, 384)], l_dq[0]),
+                   (fin_qkv.at[pl.ds(0, 32), pl.ds(0, 384)], l_dq[1])):
+        wait_bytes(ref, lsem.at[i])
     assert next(ids) <= NSEM, next(ids)
+
+
+def finish_kernel(length_ref, sums, *refs):
+    big, outs, vecs = refs[:6], refs[6:12], refs[12:20]
+    o_ub, o_stats = refs[20:22]
+    stage, s_in, s_out = refs[22:28], refs[28], refs[29]
+    for i in range(6):
+        pltpu.make_async_copy(big[i], stage[i], s_in.at[i]).start()
+    ctx = lax.axis_index("ctx")
+    mine = sums[0:8, 0:32]
+    for c in range(1, 4):
+        mine = jnp.where(ctx == c, sums[0:8, c * 32 : (c + 1) * 32], mine)
+    for r in range(8):
+        vecs[r][...] = mine[r, :]
+    o_ub[...] = sums[8, :]
+    lane = lax.broadcasted_iota(jnp.int32, (1, 128), 1)
+    v = jnp.where(lane == 0, sums[9:10, :], jnp.where(lane == 1, sums[10:11, :], sums[11:12, :]))
+    o_stats[...] = jnp.sqrt(v / (length_ref[0].astype(f32) * D))[:, 0:3]
+    for i in range(6):
+        pltpu.make_async_copy(big[i], stage[i], s_in.at[i]).wait()
+        pltpu.make_async_copy(stage[i], outs[i], s_out.at[i]).start()
+    for i in range(6):
+        pltpu.make_async_copy(stage[i], outs[i], s_out.at[i]).wait()
 
 
 def fast(mesh):
@@ -933,9 +980,10 @@
             v(f32, 512, D), v(f32, 512, D), v(f32, 256, D),
             v(bf16, 3, 128, D), v(bf16, 3, 128, D), v(bf16, 3, 128, 768), v(bf16, 3, 128, D),
             v(f32, 128, D), v(f32, 128, 768), v(f32, 128, D),
+            v(bf16, R, D), v(f32, R, D), v(f32, 128, D),
             v(f32, 8, 16, 128), v(f32, 4, 16, 128), v(f32, 3, 16, 128), v(f32, 3, 16, 128),
             v(f32, 16, 128), v(f32, 4, 16, 128), v(f32, 8, 8, D), v(f32, 16, D), v(f32, 24, D), v(f32, 8, 768),
-            pltpu.SemaphoreType.DMA((8,)),
+            pltpu.SemaphoreType.DMA((16,)),
             pltpu.SemaphoreType.DMA((NSEM,)),
             pltpu.SemaphoreType.DMA((NSEM,)),
         ]
@@ -954,16 +1002,27 @@
             out_shape=(sds((R, D), bf16), sds((R, D), f32), sds((32, 3 * D), f32), sds((32, D), f32),
                        sds((32, 4 * D), f32), sds((128, D), f32), sds((16, 128), f32)),
             in_specs=[pl.BlockSpec(memory_space=pltpu.SMEM)] + [vm] * 7,
-            out_specs=tuple([vm] * 7),
+            out_specs=tuple([pl.BlockSpec(memory_space=pl.ANY)] * 6 + [vm]),
             scratch_shapes=scratch(),
             compiler_params=pltpu.CompilerParams(
                 collective_id=0, has_side_effects=True, vmem_limit_bytes=LIMIT),
             name="block",
         )(lengths, tokens[0], cotangent[0], small, wq, wo, wu, wd)
-        mine = lax.dynamic_slice(sums, (0, ctx * 32), (8, 32))
-        stats = jnp.sqrt(sums[9:12, 0] / (lengths[0].astype(f32) * D))[None]
-        return (out[None], grad[None], mine[0], mine[1], dqkv, mine[2], mine[3], dout, mine[4],
-                mine[5], mine[6], dup, sums[8], ddown, mine[7], stats)
+        anyspec = pl.BlockSpec(memory_space=pl.ANY)
+        big = (out, grad, dqkv, dout, dup, ddown)
+        res = pl.pallas_call(
+            finish_kernel,
+            out_shape=tuple(sds(v.shape, v.dtype) for v in big)
+            + tuple([sds((32,), f32)] * 8) + (sds((128,), f32), sds((1, 3), f32)),
+            in_specs=[pl.BlockSpec(memory_space=pltpu.SMEM), vm] + [anyspec] * 6,
+            out_specs=tuple([anyspec] * 6 + [vm] * 10),
+            scratch_shapes=[pltpu.VMEM(v.shape, v.dtype) for v in big]
+            + [pltpu.SemaphoreType.DMA((6,)), pltpu.SemaphoreType.DMA((6,))],
+            compiler_params=pltpu.CompilerParams(vmem_limit_bytes=8 << 20),
+            name="finish",
+        )(lengths, sums, *big)
+        out, grad, dqkv, dout, dup, ddown, g1, b1, qb, vb, ob, g2, b2, db, ub, stats = res
+        return (out[None], grad[None], g1, b1, dqkv, qb, vb, dout, ob, g2, b2, dup, ub, ddown, db, stats)
 
     return on_device
 

time: 210 us -> 192 us (0.914)
  Pallas kernels: 195 us -> 180 us
  local copies, waits for them, and re-layouts: 10.8 us -> 8.42 us
    pallas_call x1, Pallas kernels: 195 us -> 177 us  [on_device(): pl.pallas_call(block_kernel, out_shape=(sds((R, D), bf16), sds((R, D), f3...]
    pallas_call x0 -> x1, Pallas kernels: none -> 3.19 us  [on_device(): pl.pallas_call(finish_kernel, out_shape=tuple((sds(v.shape, v.dtype) for...]
    unnamed x34 -> x32, local copies, waits for them, and re-layouts: 8.06 us -> 8.22 us
where the time goes in v3:
time: 192 us; the launch traced here: 191 us
  Pallas kernels  180 us (94%)
  local copies, waits for them, and re-layouts  8.42 us (4%)
    pallas_call x1, Pallas kernels, on_device(): pl.pallas_call(block_kernel, out_shape=(sds((R, D), bf16), sds((R, D), f3...  177 us
    unnamed x32, local copies, waits for them, and re-layouts  8.22 us

profile of v3, /device:TPU:21, one launch (start us, length us, event | category | flops | bytes accessed | tf_op | source)
XLA Modules:
  0.0 190.8 jit_solution(16594922644659988283)
XLA Ops:
  1.3 0.0 copy-start.15
  1.3 0.6 copy-done.15
  2.0 0.0 copy-start.14
  2.0 0.0 copy-start.10
  2.0 0.0 copy-start.11
  2.0 0.0 copy-start.12
  2.0 0.0 copy-start.13
  2.0 0.0 copy-start.7
  2.0 0.0 copy-start.8
  2.0 0.0 copy-start.9
  2.0 0.1 pad.2.clone
  2.1 0.5 copy-done.14
  2.6 0.0 copy-done.10
  2.6 0.0 copy-done.11
  2.7 0.0 copy-done.12
  2.7 0.0 copy-done.13
  2.7 0.0 copy-done.7
  2.7 0.0 copy-done.8
  2.7 0.0 copy-done.9
  2.8 0.1 tile.10
  2.9 0.7 maximum_maximum_fusion.small
  3.5 176.9 %block.1 = (bf16[256,1024]{1,0:T(8,128)(2,1)}, f32[256,1024]{1,0:T(8,128)}, f32[32,3072]{1,0:T(8,128)}, f32[32,1024]{1,0:T(8,128)}, f32[32,4096]{1,0:T(8,128)}, /*index=5*/f32[128,1024]{1,0:T(8,128)}, f32[16,128]{1,0:T(8,128)}) custom-call(s32[1]{0:T(128)S(6)} %copy.32.length_ref, bf16[256,1024]{1,0:T(8,128)(2,1)} %bitcast.15, bf16[256,1024]{1,0:T(8,128)(2,1)} %bitcast.16, ...), custom_call_target="tpu_custom_call" | custom-call | tf_op jit(solution)/shard_map/block/pallas_call | solution.py:1000
  180.5 0.0 copy-start.6
  180.5 0.7 copy-done.6
  181.2 0.0 copy-start
  181.2 1.2 copy-done
  182.4 0.0 copy-start.1
  182.4 1.0 copy-done.1
  183.4 0.0 copy-start.2
  183.4 1.0 copy-done.2
  184.5 0.0 copy-start.3
  184.5 1.0 copy-done.3
  185.5 0.0 copy-start.4
  185.5 1.0 copy-done.4
  186.5 0.0 copy-start.5
  186.5 0.9 copy-done.5
  187.4 3.2 %finish.1 = (bf16[256,1024]{1,0:T(8,128)(2,1)}, f32[256,1024]{1,0:T(8,128)}, f32[32,3072]{1,0:T(8,128)}, f32[32,1024]{1,0:T(8,128)}, f32[32,4096]{1,0:T(8,128)},...) custom-call(s32[1]{0:T(128)S(6)} %copy.32.length_ref, ...), custom_call_target="tpu_custom_call" | custom-call | tf_op jit(solution)/shard_map/finish/pallas_call | solution.py:1013
  (6 shorter events, 0.1 us)
Async XLA Ops:
  1.3 0.7 copy-start.15
  2.0 0.7 copy-start.14
  2.0 0.7 copy-start.10
  2.0 0.7 copy-start.11
  2.0 0.7 copy-start.12
  2.0 0.7 copy-start.13
  2.0 0.7 copy-start.7
  2.0 0.7 copy-start.8
  2.0 0.7 copy-start.9
  180.5 0.7 copy-start.6
  181.2 1.2 copy-start
  182.4 1.0 copy-start.1
  183.4 1.0 copy-start.2
  184.5 1.0 copy-start.3
  185.5 1.0 copy-start.4
  186.5 0.9 copy-start.5

commit v4 on v3

--- a/solution.py
+++ b/solution.py
@@ -14,7 +14,7 @@
 R = 256
 S = 1024
 LIMIT = 66_000_000
-NSEM = 260
+NSEM = 170
 ORDER = (2, 3, 1)
 
 
@@ -1018,7 +1018,7 @@
             out_specs=tuple([anyspec] * 6 + [vm] * 10),
             scratch_shapes=[pltpu.VMEM(v.shape, v.dtype) for v in big]
             + [pltpu.SemaphoreType.DMA((6,)), pltpu.SemaphoreType.DMA((6,))],
-            compiler_params=pltpu.CompilerParams(vmem_limit_bytes=8 << 20),
+            compiler_params=pltpu.CompilerParams(vmem_limit_bytes=LIMIT),
             name="finish",
         )(lengths, sums, *big)
         out, grad, dqkv, dout, dup, ddown, g1, b1, qb, vb, ob, g2, b2, db, ub, stats = res

time: 192 us -> 185 us (0.964)
  local copies, waits for them, and re-layouts: 8.42 us -> 1.48 us
    unnamed x32 -> x18, local copies, waits for them, and re-layouts: 8.22 us -> 1.28 us
where the time goes in v4:
time: 185 us; the launch traced here: 183 us
  Pallas kernels  180 us (97%)
    pallas_call x1, Pallas kernels, on_device(): pl.pallas_call(block_kernel, out_shape=(sds((R, D), bf16), sds((R, D), f3...  175 us
    pallas_call x1, Pallas kernels, on_device(): pl.pallas_call(finish_kernel, out_shape=tuple((sds(v.shape, v.dtype) for...  4.25 us

profile of v4, /device:TPU:21, one launch (start us, length us, event | category | flops | bytes accessed | tf_op | source)
XLA Modules:
  0.0 183.3 jit_solution(4172120031620807691)
XLA Ops:
  1.3 0.0 copy-start.8
  1.3 0.6 copy-done.8
  2.0 0.0 copy-start.7
  2.0 0.0 copy-start.3
  2.0 0.0 copy-start.4
  2.0 0.0 copy-start.5
  2.0 0.0 copy-start.6
  2.0 0.0 copy-start
  2.0 0.0 copy-start.1
  2.0 0.0 copy-start.2
  2.0 0.1 pad.2.clone
  2.1 0.5 copy-done.7
  2.6 0.0 copy-done.3
  2.6 0.0 copy-done.4
  2.7 0.0 copy-done.5
  2.7 0.0 copy-done.6
  2.7 0.0 copy-done
  2.7 0.0 copy-done.1
  2.7 0.0 copy-done.2
  2.8 0.1 tile.10
  2.9 0.7 maximum_maximum_fusion.small
  3.5 175.3 %block.1 = (bf16[256,1024]{1,0:T(8,128)(2,1)}, f32[256,1024]{1,0:T(8,128)}, f32[32,3072]{1,0:T(8,128)}, f32[32,1024]{1,0:T(8,128)}, f32[32,4096]{1,0:T(8,128)}, /*index=5*/f32[128,1024]{1,0:T(8,128)}, f32[16,128]{1,0:T(8,128)}) custom-call(s32[1]{0:T(128)S(6)} %copy.32.length_ref, bf16[256,1024]{1,0:T(8,128)(2,1)} %bitcast.15, bf16[256,1024]{1,0:T(8,128)(2,1)} %bitcast.16, ...), custom_call_target="tpu_custom_call" | custom-call | tf_op jit(solution)/shard_map/block/pallas_call | solution.py:1000
  178.8 4.2 %finish.1 = (bf16[256,1024]{1,0:T(8,128)(2,1)}, f32[256,1024]{1,0:T(8,128)}, f32[32,3072]{1,0:T(8,128)}, f32[32,1024]{1,0:T(8,128)}, f32[32,4096]{1,0:T(8,128)},...) custom-call(s32[1]{0:T(128)S(6)} %copy.32.length_ref, ...), custom_call_target="tpu_custom_call" | custom-call | tf_op jit(solution)/shard_map/finish/pallas_call | solution.py:1013
  (6 shorter events, 0.1 us)
Async XLA Ops:
  1.3 0.7 copy-start.8
  2.0 0.7 copy-start.7
  2.0 0.7 copy-start.3
  2.0 0.7 copy-start.4
  2.0 0.7 copy-start.5
  2.0 0.7 copy-start.6
  2.0 0.7 copy-start
  2.0 0.7 copy-start.1
  2.0 0.7 copy-start.2

commit v5 on v4

--- a/solution.py
+++ b/solution.py
@@ -14,7 +14,7 @@
 R = 256
 S = 1024
 LIMIT = 66_000_000
-NSEM = 170
+NRECV, NSEND, NLOCAL = 103, 52, 11
 ORDER = (2, 3, 1)
 
 
@@ -72,7 +72,7 @@
     seq, ctx = lax.axis_index("seq"), lax.axis_index("ctx")
     z, x = seq // 2, seq % 2
     y, k = ctx // 2, ctx % 2
-    ids = itertools.count()
+    rids, sids = itertools.count(), itertools.count()
     lids = itertools.count()
 
     mate = {"ctx": y * 2 + (k + 1) % 2}
@@ -85,15 +85,21 @@
     def zpeer(d):
         return {"seq": ((z + d) % 4) * 2 + x}
 
-    def take(n=1):
-        first = next(ids)
+    def take(count, n=1):
+        first = next(count)
         for _ in range(n - 1):
-            next(ids)
+            next(count)
         return first
 
-    def rcopy(src, dst, dev, i):
+    def rtake(n=1):
+        return take(rids, n)
+
+    def stake(n=1):
+        return take(sids, n)
+
+    def rcopy(src, dst, dev, i, s):
         return pltpu.make_async_remote_copy(
-            src_ref=src, dst_ref=dst, send_sem=ssem.at[i], recv_sem=rsem.at[i],
+            src_ref=src, dst_ref=dst, send_sem=ssem.at[s], recv_sem=rsem.at[i],
             device_id=dev, device_id_type=MESH)
 
     def wait_bytes(ref, sem):
@@ -124,10 +130,10 @@
     pl.semaphore_signal(barrier, inc=1, device_id=xpeer, device_id_type=MESH)
     pl.semaphore_wait(barrier, 7)
 
-    i_smc = take(4)
+    i_smc, s_smc = rtake(), stake()
     for d in (1, 2, 3):
-        rcopy(small, smc.at[d], cpeer(d), i_smc + d).start()
-        sent(small, i_smc + d)
+        rcopy(small, smc.at[d], cpeer(d), i_smc, s_smc).start()
+    sent(smc.at[pl.ds(1, 3)], s_smc)
     own32 = pl.ds(mul(seq * 128 + ctx * 32, 32), 32)
 
     def qkv_pieces(c):
@@ -135,132 +141,106 @@
             yield (pl.ds(mul((j % 3) * D + (c + 4 * (j // 3)) * 128, 128), 128),
                    pl.ds(j * 128, 128))
 
-    i_qa = take(4)
+    i_qa, s_qa = rtake(), stake()
     for d in (1, 2, 3):
         for a, b in qkv_pieces((ctx + d) % 4):
-            rcopy(qkv_in.at[:, a], wqkv.at[own32, b], cpeer(d), i_qa + d).start()
-        sent(wqkv.at[pl.ds(0, 32), :], i_qa + d)
+            rcopy(qkv_in.at[:, a], wqkv.at[own32, b], cpeer(d), i_qa, s_qa).start()
+    sent(wqkv.at[pl.ds(0, 96), :], s_qa)
     l_q = next(lids)
     for a, b in qkv_pieces(ctx):
         pltpu.make_async_copy(qkv_in.at[:, a], wqkv.at[own32, b], lsem.at[l_q]).start()
 
     t = seq % 4
     out32 = pl.ds(mul((seq // 4) * 128 + ctx * 32, 32), 32)
-    i_oa = take()
+    i_oa, s_oa = rtake(), stake()
     l_o = next(lids)
 
     @pl.when(ctx != t)
     def _():
-        rcopy(out_in, wout.at[out32, :], {"ctx": t}, i_oa).start()
-
-    sent(out_in, i_oa, ctx != t)
+        rcopy(out_in, wout.at[out32, :], {"ctx": t}, i_oa, s_oa).start()
+
+    sent(wout.at[pl.ds(0, 32), :], s_oa, ctx != t)
 
     @pl.when(ctx == t)
     def _():
         pltpu.make_async_copy(out_in, wout.at[out32, :], lsem.at[l_o]).start()
 
-    i_ua = take(4)
+    i_ua, s_ua = rtake(), stake()
     for d in (1, 2, 3):
         c2 = (ctx + d) % 4
         for s in range(8):
             rcopy(up_in.at[:, pl.ds(mul((s * 4 + c2) * 128, 128), 128)],
-                  wup.at[own32, pl.ds(s * 128, 128)], cpeer(d), i_ua + d).start()
-        sent(wup.at[pl.ds(0, 32), :], i_ua + d)
+                  wup.at[own32, pl.ds(s * 128, 128)], cpeer(d), i_ua, s_ua).start()
+    sent(wup.at[pl.ds(0, 96), :], s_ua)
     l_u = next(lids)
     for s in range(8):
         pltpu.make_async_copy(up_in.at[:, pl.ds(mul((s * 4 + ctx) * 128, 128), 128)],
                               wup.at[own32, pl.ds(s * 128, 128)], lsem.at[l_u]).start()
 
-    for d in (1, 2, 3):
-        rcopy(small, smc.at[d], cpeer(d), i_smc + d).wait_recv()
+    wait_bytes(smc.at[pl.ds(1, 3)], rsem.at[i_smc])
     rowid = lax.broadcasted_iota(jnp.int32, (16, 128), 0)
     smb[seq] = small[...] + jnp.where(rowid < 8, smc[1] + smc[2] + smc[3], 0.0)
 
-    def gather_z(block, zi, src=None):
+    def relay_start(block, i, s, src=None):
         own = block(seq) if src is None else src
-        for d in ORDER:
-            rcopy(own, block(seq), zpeer(d), zi + d).start()
-            sent(own, zi + d)
-
-    def gather_x(block, xi, src=None):
+        for cond, step, first, sz in ((z < 3, 1, i, s), (z > 0, -1, i + 4, s + 1)):
+            @pl.when(cond)
+            def _(step=step, first=first, sz=sz):
+                rcopy(own, block(seq), {"seq": (z + step) * 2 + x}, first + 1, sz).start()
+
+    def relay_x(block, i, s, src=None):
         own = block(seq) if src is None else src
-        rcopy(own, block(seq), xpeer, xi).start()
-        sent(own, xi)
-
-    def gather_forward(block, zi, xi, d):
-        b = block(((z - d + 4) % 4) * 2 + x)
-        rcopy(b, b, xpeer, zi + d).wait_recv()
-        rcopy(b, b, xpeer, xi + d).start()
-        sent(block(0), xi + d)
-
-    def gather_finish(block, xi):
-        for d in range(4):
-            b = block(seq)
-            rcopy(b, b, xpeer, xi + d).wait_recv()
-
-    def relay_start(block, i, src=None):
-        own = block(seq) if src is None else src
-        for cond, step, first in ((z < 3, 1, i), (z > 0, -1, i + 4)):
-            @pl.when(cond)
-            def _(step=step, first=first):
-                rcopy(own, block(seq), {"seq": (z + step) * 2 + x}, first + 1).start()
-
-            sent(own, first + 1, cond)
-
-    def relay_x(block, i, src=None):
-        own = block(seq) if src is None else src
-        rcopy(own, block(seq), xpeer, i + 8 + z).start()
-        sent(own, i + 8 + z)
-
-    def relay_step(block, i, j):
-        for has, on, step, first in ((z >= j, z < 3, 1, i), (z + j <= 3, z > 0, -1, i + 4)):
+        rcopy(own, block(seq), xpeer, i, s + 2).start()
+
+    def relay_step(block, i, s, j):
+        for has, on, step, first, sz in ((z >= j, z < 3, 1, i, s), (z + j <= 3, z > 0, -1, i + 4, s + 1)):
             zz = z - j * step
 
             @pl.when(has)
-            def _(on=on, step=step, first=first, zz=zz):
+            def _(on=on, step=step, first=first, zz=zz, sz=sz):
                 b = block(zz * 2 + x)
-                rcopy(b, b, xpeer, first + j).wait_recv()
+                wait_bytes(b, rsem.at[first + j])
                 if j < 3:
                     @pl.when(on)
                     def _():
-                        rcopy(b, b, {"seq": (z + step) * 2 + x}, first + j + 1).start()
-                rcopy(b, b, xpeer, i + 8 + zz).start()
-
-            if j < 3:
-                sent(block(0), first + j + 1, jnp.logical_and(has, on))
-
-    def relay_finish(block, i):
-        for zz in range(4):
-            rcopy(block(0), block(0), xpeer, i + 8 + zz).wait_recv()
-
-    def relay_sent(block, i):
-        for j in (1, 2, 3):
-            for has, zz in ((z >= j, z - j), (z + j <= 3, z + j)):
-                @pl.when(has)
-                def _(zz=zz):
-                    wait_bytes(block(0), ssem.at[i + 8 + zz])
-
-    small_block = lambda s: smb.at[s]
-    i_sz, i_sx = take(4), take(4)
-    gather_z(small_block, i_sz)
-    gather_x(small_block, i_sx)
-
-    for d in (1, 2, 3):
-        wait_bytes(wqkv.at[pl.ds(0, 32), :], rsem.at[i_qa + d])
+                        rcopy(b, b, {"seq": (z + step) * 2 + x}, first + j + 1, sz).start()
+                rcopy(b, b, xpeer, i, s + 2).start()
+
+    def relay_finish(w, i):
+        wait_bytes(w.at[pl.ds(0, 512), :], rsem.at[i])
+
+    def relay_sent(w, s):
+        for n in (1, 2, 3):
+            sent(w.at[pl.ds(0, n * 128), :], s, z == n - 1)
+            sent(w.at[pl.ds(0, n * 128), :], s + 1, z == 4 - n)
+        sent(w.at[pl.ds(0, 512), :], s + 2)
+
+    i_sz, i_sx, s_sz, s_sx = rtake(3), rtake(), stake(), stake()
+    for d in ORDER:
+        rcopy(smb.at[seq], smb.at[seq], zpeer(d), i_sz + d - 1, s_sz).start()
+    rcopy(smb.at[seq], smb.at[seq], xpeer, i_sx, s_sx).start()
+    sent(smb.at[pl.ds(0, 3)], s_sz)
+    sent(smb.at[pl.ds(0, 4)], s_sx)
+
+    wait_bytes(wqkv.at[pl.ds(0, 96), :], rsem.at[i_qa])
     wait_bytes(wqkv.at[pl.ds(0, 32), :], lsem.at[l_q])
     qkv_block = lambda s: wqkv.at[srow(s), :]
-    i_qr = take(12)
-    relay_start(qkv_block, i_qr)
+    i_qr, s_qr = rtake(8), stake(3)
+    relay_start(qkv_block, i_qr, s_qr)
+    relay_sent(wqkv, s_qr)
     for d in ORDER:
-        gather_forward(small_block, i_sz, i_sx, d)
-    relay_x(qkv_block, i_qr)
+        b = smb.at[((z - d + 4) % 4) * 2 + x]
+        wait_bytes(b, rsem.at[i_sz + d - 1])
+        rcopy(b, b, xpeer, i_sx, s_sx).start()
+    relay_x(qkv_block, i_qr, s_qr)
     l_d = next(lids)
     down_block = lambda s: wdown.at[srow(s), :]
-    i_dr = take(12)
-    relay_x(down_block, i_dr, src=down_in)
+    i_dr, s_dr = rtake(8), stake(3)
+    relay_x(down_block, i_dr, s_dr, src=down_in)
+    relay_sent(wdown, s_dr)
     pltpu.make_async_copy(down_in, down_block(seq), lsem.at[l_d]).start()
 
-    gather_finish(small_block, i_sx)
+    wait_bytes(smb.at[pl.ds(0, 4)], rsem.at[i_sx])
     for s in range(8):
         vec[:, s * 128 : (s + 1) * 128] = smb[s]
 
@@ -277,27 +257,25 @@
     def chunk(buf, c, ch):
         return buf.at[pl.ds(mul(c * R + ch * RC, RC), RC), :]
 
-    def ag_start(buf, i, ch):
+    def ag_start(buf, i, s, ch):
         own = chunk(buf, ctx, ch)
-        rcopy(own, own, ypeer, i + CH + ch).start()
-        rcopy(own, own, mate, i + ch).start()
-        if buf is not gf and buf is not n2:
-            sent(own, i + CH + ch)
-            sent(own, i + ch)
-
-    def ag_forward(buf, i, ch):
+        rcopy(own, own, ypeer, i + 1 + ch, s + ch).start()
+        rcopy(own, own, mate, i, s + ch).start()
+
+    def ag_forward(buf, i, s, ch):
         b = chunk(buf, ((y + 1) % 2) * 2 + k, ch)
-        rcopy(b, b, mate, i + CH + ch).wait_recv()
-        rcopy(b, b, mate, i + 2 * CH + ch).start()
-        if buf is not gf and buf is not n2:
-            sent(buf.at[pl.ds(0, RC), :], i + 2 * CH + ch)
+        wait_bytes(b, rsem.at[i + 1 + ch])
+        rcopy(b, b, mate, i + 3, s + ch).start()
 
     def ag_wait(buf, i, which):
-        for ch in range(CH):
-            b = chunk(buf, ctx, ch)
-            rcopy(b, b, mate, i + which * CH + ch).wait_recv()
-
-    i_n1 = take(3 * CH)
+        wait_bytes(buf.at[pl.ds(0, R), :], rsem.at[i + which])
+
+    def ag_bytes(buf):
+        return buf.at[pl.ds(0, 3 * RC), :]
+
+    i_n1, s_n1 = rtake(4), stake(2)
+    for ch in range(CH):
+        sent(ag_bytes(n1), s_n1 + ch)
     for ch in range(CH):
         def first(q, ch=ch):
             r0 = mul(ch * RC + q * 32, 32)
@@ -305,7 +283,7 @@
             n1[pl.ds(mul(my + r0, 32), 32), :] = (zz * vec[0:1, :] + vec[1:2, :]).astype(bf16)
 
         loop(RC // 32, first)
-        ag_start(n1, i_n1, ch)
+        ag_start(n1, i_n1, s_n1, ch)
 
 
     def mask_rows(q):
@@ -314,9 +292,9 @@
         gf[pl.ds(mul(my + r0, 32), 32), :] = g.astype(bf16)
 
     loop(R // 32, mask_rows)
-    i_gf = take(3 * CH)
+    i_gf, s_gf = rtake(4), stake(2)
     for ch in range(CH):
-        ag_start(gf, i_gf, ch)
+        ag_start(gf, i_gf, s_gf, ch)
     for j in range(6):
         if j % 3 == 1:
             qbias[:, j * 128 : (j + 1) * 128] = jnp.zeros((8, 128), f32)
@@ -324,9 +302,9 @@
             r = 2 + j % 3 // 2
             b = vec[r : r + 1, pl.ds(mul((ctx + 4 * (j // 3)) * 128, 128), 128)]
             qbias[:, j * 128 : (j + 1) * 128] = jnp.broadcast_to(b, (8, 128))
-    relay_step(qkv_block, i_qr, 1)
-    relay_step(qkv_block, i_qr, 2)
-    i_oz, i_ox = take(4), take(4)
+    relay_step(qkv_block, i_qr, s_qr, 1)
+    relay_step(qkv_block, i_qr, s_qr, 2)
+    i_oz, i_ox, s_oz, s_ox = rtake(3), rtake(), stake(), stake()
     out_block = lambda zz: wout.at[pl.ds(mul((zz // 2) * 128, 128), 128), :]
 
     @pl.when(ctx == t)
@@ -334,49 +312,47 @@
         wait_bytes(wout.at[pl.ds(0, 96), :], rsem.at[i_oa])
         wait_bytes(wout.at[pl.ds(0, 32), :], lsem.at[l_o])
         for d in (1, 2, 3):
-            rcopy(out_block(z), out_block(z), zpeer(d), i_oz + d).start()
-        rcopy(out_block(z), out_block(z), xpeer, i_ox).start()
-
-    for d in (1, 2, 3):
-        sent(out_block(z), i_oz + d, ctx == t)
-    sent(out_block(z), i_ox, ctx == t)
-
-    ag_forward(n1, i_n1, 0)
-    relay_step(qkv_block, i_qr, 3)
-    for d in (1, 2, 3):
-        wait_bytes(wup.at[pl.ds(0, 32), :], rsem.at[i_ua + d])
+            rcopy(out_block(z), out_block(z), zpeer(d), i_oz + d - 1, s_oz).start()
+        rcopy(out_block(z), out_block(z), xpeer, i_ox, s_ox).start()
+
+    sent(n1.at[pl.ds(0, 384), :], s_oz, ctx == t)
+    sent(wout, s_ox, x == k)
+    ag_forward(n1, i_n1, s_n1, 0)
+    relay_step(qkv_block, i_qr, s_qr, 3)
+
+    wait_bytes(wup.at[pl.ds(0, 96), :], rsem.at[i_ua])
     wait_bytes(wup.at[pl.ds(0, 32), :], lsem.at[l_u])
     up_block = lambda s: wup.at[srow(s), :]
-    i_ur = take(12)
-    relay_start(up_block, i_ur)
-    ag_forward(n1, i_n1, 1)
+    i_ur, s_ur = rtake(8), stake(3)
+    relay_start(up_block, i_ur, s_ur)
+    relay_sent(wup, s_ur)
+    ag_forward(n1, i_n1, s_n1, 1)
 
     ag_wait(n1, i_n1, 0)
-    relay_finish(qkv_block, i_qr)
+    relay_finish(wqkv, i_qr)
     mine = x == k
     for d in (1, 2, 3):
         zz = (z - d + 4) % 4
 
         @pl.when(jnp.logical_and(mine, zz % 2 == y))
         def _(d=d, zz=zz):
-            rcopy(out_block(zz), out_block(zz), xpeer, i_oz + d).wait_recv()
-            rcopy(out_block(zz), out_block(zz), xpeer, i_ox + d).start()
-
-        sent(out_block(zz), i_ox + d, jnp.logical_and(mine, zz % 2 == y))
-    relay_x(up_block, i_ur)
+            wait_bytes(out_block(zz), rsem.at[i_oz + d - 1])
+            rcopy(out_block(zz), out_block(zz), xpeer, i_ox, s_ox).start()
+
+    relay_x(up_block, i_ur, s_ur)
 
     def project(it):
         blk = ((y + it // 2) % 2) * 2 + (k + it % 2) % 2
 
         @pl.when(it == 3)
         def _():
-            ag_wait(n1, i_n1, 2)
+            ag_wait(n1, i_n1, 3)
 
         qkv[rows(blk), :] = (nn(n1[rows(blk), :], wqkv[...]) + qbias[0:1, :]).astype(bf16)
 
     loop(4, project)
-    relay_step(up_block, i_ur, 1)
-    relay_start(down_block, i_dr, src=down_in)
+    relay_step(up_block, i_ur, s_ur, 1)
+    relay_start(down_block, i_dr, s_dr, src=down_in)
 
     def turn(i):
         c0 = pl.ds(mul(i * 128, 128), 128)
@@ -447,11 +423,11 @@
 
     pair_forward(0)
     for ch in range(CH):
-        ag_forward(gf, i_gf, ch)
+        ag_forward(gf, i_gf, s_gf, ch)
     pair_forward(1)
 
-    relay_step(up_block, i_ur, 2)
-    def rs_run(partial, sb, rb, own, i):
+    relay_step(up_block, i_ur, s_ur, 2)
+    def rs_run(partial, sb, rb, own, i, s):
         def step(tt):
             g, ch, sub = tt // 4, tt % 2, (tt // 2) % 2
             blk = ((y + 1 - g) % 2) * 2 + (k + 1 - sub) % 2
@@ -460,18 +436,18 @@
             @pl.when(jnp.logical_and(g == 0, sub == 0))
             def _():
                 sb[0, ch] = tmp[...].astype(bf16)
-                rcopy(sb.at[0, ch], rb.at[0, ch], mate, i + ch).start()
+                rcopy(sb.at[0, ch], rb.at[0, ch], mate, i + ch, s + ch).start()
 
             @pl.when(jnp.logical_and(g == 0, sub == 1))
             def _():
-                rcopy(sb.at[0, ch], rb.at[0, ch], mate, i + ch).wait_recv()
+                wait_bytes(rb.at[0, ch], rsem.at[i + ch])
                 sb[1, ch] = (tmp[...] + rb[0, ch].astype(f32)).astype(bf16)
-                rcopy(sb.at[1, ch], rb.at[1, ch], ypeer, i + CH + ch).start()
+                rcopy(sb.at[1, ch], rb.at[1, ch], ypeer, i + CH + ch, s + ch).start()
 
             @pl.when(jnp.logical_and(g == 1, sub == 0))
             def _():
                 sb[2, ch] = tmp[...].astype(bf16)
-                rcopy(sb.at[2, ch], rb.at[2, ch], mate, i + 2 * CH + ch).start()
+                rcopy(sb.at[2, ch], rb.at[2, ch], mate, i + 2 * CH + ch, s + ch).start()
 
             @pl.when(jnp.logical_and(g == 1, sub == 1))
             def _():
@@ -480,34 +456,30 @@
         loop(4 * CH, step)
 
     def rs_wait(sb, rb, i, ch):
-        rcopy(sb.at[2, ch], rb.at[2, ch], mate, i + 2 * CH + ch).wait_recv()
-        rcopy(sb.at[1, ch], rb.at[1, ch], mate, i + CH + ch).wait_recv()
+        wait_bytes(rb.at[2, ch], rsem.at[i + 2 * CH + ch])
+        wait_bytes(rb.at[1, ch], rsem.at[i + CH + ch])
 
     def rs_sum(rb, own, ch, r):
         return own[ch, r, :] + rb[2, ch, r, :].astype(f32) + rb[1, ch, r, :].astype(f32)
 
-    def rs_sent(sb, i):
-        for j in range(3):
-            for ch in range(CH):
-                wait_bytes(sb.at[j, ch], ssem.at[i + j * CH + ch])
-
-    for d in range(4):
-        zz = (z - d + 4) % 4
-
-        @pl.when(jnp.logical_and(x != k, zz % 2 == y))
-        def _(d=d):
-            rcopy(out_block(z), out_block(z), xpeer, i_ox + d).wait_recv()
+    def rs_sent(sb, s):
+        for ch in range(CH):
+            wait_bytes(sb.at[:, ch], ssem.at[s + ch])
+
+    @pl.when(x != k)
+    def _():
+        wait_bytes(wout, rsem.at[i_ox])
 
     def branch_part(blk, ch, dst):
         a = attt[:, pl.ds(mul(blk * R + ch * RC, RC), RC)]
         dst[...] = tn(a, wout[...])
 
-    i_br = take(3 * CH)
-    rs_run(branch_part, rs_s, rs_r, rs_own, i_br)
-    relay_step(up_block, i_ur, 3)
-    relay_step(down_block, i_dr, 1)
-
-    i_n2 = take(3 * CH)
+    i_br, s_br = rtake(3 * CH), stake(CH)
+    rs_run(branch_part, rs_s, rs_r, rs_own, i_br, s_br)
+    relay_step(up_block, i_ur, s_ur, 3)
+    relay_step(down_block, i_dr, s_dr, 1)
+
+    i_n2, s_n2 = rtake(4), stake(2)
     stat[...] = jnp.zeros_like(stat)
     for ch in range(CH):
         rs_wait(rs_s, rs_r, i_br, ch)
@@ -526,10 +498,10 @@
             stat[8:16, :] += jnp.sum((resid * resid * v).reshape(4, 8, D), axis=0)
 
         loop(RC // 32, second)
-        ag_start(n2, i_n2, ch)
-
-    relay_step(down_block, i_dr, 2)
-    relay_finish(up_block, i_ur)
+        ag_start(n2, i_n2, s_n2, ch)
+
+    relay_step(down_block, i_dr, s_dr, 2)
+    relay_finish(wup, i_ur)
 
     def feed(it):
         blk = ((y + it // 2) % 2) * 2 + (k + it % 2) % 2
@@ -537,16 +509,16 @@
         @pl.when(it == 1)
         def _():
             ag_wait(n2, i_n2, 0)
-            ag_forward(n2, i_n2, 0)
-            relay_step(down_block, i_dr, 3)
+            ag_forward(n2, i_n2, s_n2, 0)
+            relay_step(down_block, i_dr, s_dr, 3)
 
         @pl.when(it == 2)
         def _():
-            ag_forward(n2, i_n2, 1)
+            ag_forward(n2, i_n2, s_n2, 1)
 
         @pl.when(it == 3)
         def _():
-            ag_wait(n2, i_n2, 2)
+            ag_wait(n2, i_n2, 3)
 
         def cols(n):
             c0 = pl.ds(mul(n * 512, 512), 512)
@@ -568,15 +540,15 @@
         c2 = pl.ds(mul(((3 - hh) * 2 + xx) * 128, 128), 128)
         return tn(jnp.concatenate([a[:, c1], a[:, c2]], axis=1), b[:, c0 : c0 + n])
 
-    def dw_away(a, b, c0, n, xb, xr, i):
-        def away(hh):
-            r = pl.ds(mul(hh * 256, 256), 256)
+    def dw_away(a, b, c0, n, xb, xr, i, s, parts):
+        w = n // parts
+        for hh in range(2):
+            r = pl.ds(hh * 256, 256)
             xb[r, c0 : c0 + n] = dw_half(a, b, c0, n, (x + 1) % 2, hh).astype(bf16)
-            rcopy(xb.at[r, pl.ds(c0, n)], xr.at[r, pl.ds(c0, n)], xpeer, i + hh).start()
-            sent(xb.at[pl.ds(0, 256), pl.ds(c0, n)], i + hh)
-
-        for hh in range(2):
-            away(hh)
+            for p in range(parts):
+                c = pl.ds(c0 + p * w, w)
+                rcopy(xb.at[r, c], xr.at[r, c], xpeer, i + hh * parts + p, s).start()
+        sent(xb.at[pl.ds(0, 512), pl.ds(c0, n)], s)
 
     def dw_keep(a, b, c0, n, own):
         def keep(hh):
@@ -584,12 +556,13 @@
 
         loop(2, keep)
 
-    def dw_z(hh, c0, n, xr, own, zb, zo, zr, fin, i, iz):
-        wait_bytes(xr.at[pl.ds(0, 256), pl.ds(c0, n)], rsem.at[i + hh])
+    def dw_z(hh, c0, n, xr, own, zb, zr0, zc, zr, fin, i, iz, sz):
+        wait_bytes(xr.at[pl.ds(0, 256), pl.ds(c0, n)], rsem.at[i])
         c = slice(c0, c0 + n)
-        for sub, zz in enumerate((hh, 3 - hh)):
-            r = slice(hh * 256 + sub * 128, hh * 256 + sub * 128 + 128)
-            ro = slice(zo + zz * 128, zo + zz * 128 + 128)
+        cz = slice(zc, zc + n)
+        for part, zz in enumerate((hh, 3 - hh)):
+            r = slice(hh * 256 + part * 128, hh * 256 + part * 128 + 128)
+            ro = slice(zr0 + zz * 128, zr0 + zz * 128 + 128)
             dz = (zz - z + 4) % 4
 
             @pl.when(zz == z)
@@ -598,24 +571,21 @@
 
             @pl.when(zz != z)
             def _(r=r, ro=ro, zz=zz, dz=dz):
-                zb[ro, c] = (own[r, c] + xr[r, c].astype(f32)).astype(bf16)
-                rcopy(zb.at[ro, c], zr.at[dz - 1, :, c], {"seq": zz * 2 + x}, iz + dz).start()
-
-            sent(zb.at[ro, c], iz + dz, zz != z)
+                zb[ro, cz] = (own[r, c] + xr[r, c].astype(f32)).astype(bf16)
+                rcopy(zb.at[ro, cz], zr.at[dz - 1, :, c], {"seq": zz * 2 + x}, iz, sz).start()
 
     def dw_end(c0, n, zr, fin, iz):
         c = slice(c0, c0 + n)
-        for d in (1, 2, 3):
-            wait_bytes(zr.at[d - 1, :, c], rsem.at[iz + d])
+        wait_bytes(zr.at[:, :, pl.ds(c0, n)], rsem.at[iz])
         fin[:, c] += (zr[0, :, c].astype(f32) + zr[1, :, c].astype(f32)) + zr[2, :, c].astype(f32)
 
     ag_wait(gf, i_gf, 0)
-    ag_wait(gf, i_gf, 2)
-    i_dwx, i_dwz = take(2), take(4)
-    dw_away(act, gf, 0, D, xs_down, xr_down, i_dwx)
+    ag_wait(gf, i_gf, 3)
+    i_dwx, i_dwz, s_dwx, s_dwz = rtake(4), rtake(2), stake(), stake(2)
+    dw_away(act, gf, 0, D, xs_down, xr_down, i_dwx, s_dwx, 2)
     dw_keep(act, gf, 0, D, own_a)
-    relay_finish(down_block, i_dr)
-    wait_bytes(down_in, lsem.at[l_d])
+    relay_finish(wdown, i_dr)
+    wait_bytes(wdown.at[pl.ds(0, 128), :], lsem.at[l_d])
     gvec[...] = jnp.zeros_like(gvec)
 
     def grad_feed(it):
@@ -632,26 +602,36 @@
 
     loop(4, grad_feed)
 
-    rs_sent(rs_s, i_br)
+    def down_z(hh, p):
+        dw_z(hh, p * 512, 512, xr_down, own_a, dmix, p * 512, 0, zr_down, fin_down,
+             i_dwx + hh * 2 + p, i_dwz + p, s_dwz + p)
+
+    down_z(0, 0)
+
+    rs_sent(rs_s, s_br)
 
     def gn2_part(blk, ch, dst):
         dst[...] = nt(gpre[pl.ds(mul(blk * R + ch * RC, RC), RC), :], wup[...])
 
-    i_g2 = take(3 * CH)
-    rs_run(gn2_part, rs_s, rs_r, rs_own, i_g2)
-
-    def down_z(hh):
-        dw_z(hh, 0, D, xr_down, own_a, gpre, 0, zr_down, fin_down, i_dwx, i_dwz)
-
-    def up_z(hh):
-        dw_z(hh, 0, D, xr_up, own_b, gpre, 512, zr_up, fin_up, i_uwx, i_uwz)
-
-    i_uwx, i_uwz = take(2), take(4)
-    dw_away(n2, gpre, 0, D, xs_up, xr_up, i_uwx)
+    i_g2, s_g2 = rtake(3 * CH), stake(CH)
+    rs_run(gn2_part, rs_s, rs_r, rs_own, i_g2, s_g2)
+
+    down_z(0, 1)
+    i_uwx, i_uwz, s_uwx, s_uwz = rtake(4), rtake(2), stake(), stake(2)
+    dw_away(n2, gpre, 0, D, xs_up, xr_up, i_uwx, s_uwx, 2)
     dw_keep(n2, gpre, 0, D, own_b)
-    down_z(0)
-
-    i_gb = take(3 * CH)
+
+    def up_z(hh, p):
+        dw_z(hh, p * 512, 512, xr_up, own_b, gpre, 0, p * 512, zr_up, fin_up,
+             i_uwx + hh * 2 + p, i_uwz + p, s_uwz + p)
+
+    for p in range(2):
+        sent(gpre.at[pl.ds(0, 384), pl.ds(0, 512)], s_uwz + p)
+    down_z(1, 0)
+
+    i_gb, s_gb = rtake(4), stake(2)
+    for ch in range(CH):
+        sent(ag_bytes(gb), s_gb + ch)
     for ch in range(CH):
         rs_wait(rs_s, rs_r, i_g2, ch)
 
@@ -672,20 +652,21 @@
             gvec[7] += fold(gout)
 
         loop(RC // 32, third)
-        ag_start(gb, i_gb, ch)
-
-    down_z(1)
-    ag_forward(gb, i_gb, 0)
+        ag_start(gb, i_gb, s_gb, ch)
+
+    down_z(1, 1)
+    ag_forward(gb, i_gb, s_gb, 0)
 
     def ffn_part(blk, ch, dst):
         dst[...] = nn(act[pl.ds(mul(blk * R + ch * RC, RC), RC), :], wdown[...])
 
-    i_ff = take(3 * CH)
-    rs_run(ffn_part, rt_s, rt_r, rt_own, i_ff)
-    ag_forward(gb, i_gb, 1)
+    i_ff, s_ff = rtake(3 * CH), stake(CH)
+    rs_run(ffn_part, rt_s, rt_r, rt_own, i_ff, s_ff)
+    up_z(0, 0)
+    ag_forward(gb, i_gb, s_gb, 1)
 
     ag_wait(gb, i_gb, 0)
-    ag_wait(gb, i_gb, 2)
+    ag_wait(gb, i_gb, 3)
 
     def att_grad(i):
         c0 = pl.ds(mul(i * 256, 256), 256)
@@ -693,18 +674,20 @@
 
     loop(4, att_grad)
     own_out[...] = nn(attt[...], gb[...])
-    i_owx, i_owz = take(), take(4)
-    for j in range(3 * CH):
-        wait_bytes(gf.at[pl.ds(0, RC), :], ssem.at[i_gf + j])
-        wait_bytes(n2.at[pl.ds(0, RC), :], ssem.at[i_n2 + j])
+    i_owx, i_owz, s_owx, s_owz = rtake(), rtake(), stake(), stake()
+    for ch in range(CH):
+        wait_bytes(ag_bytes(gf), ssem.at[s_gf + ch])
+        wait_bytes(ag_bytes(n2), ssem.at[s_n2 + ch])
     xs_out = gf.at[pl.ds(512, 256), :]
 
     @pl.when(x != k)
     def _():
         gf[512:768, :] = own_out[...].astype(bf16)
-        rcopy(xs_out, xr_out, xpeer, i_owx).start()
-
-    sent(xs_out, i_owx, x != k)
+        rcopy(xs_out, xr_out, xpeer, i_owx, s_owx).start()
+
+    sent(xs_out, s_owx, x != k)
+    sent(n2.at[pl.ds(0, 128), :], s_owz, jnp.logical_and(x == k, z % 2 == y))
+    sent(n2.at[pl.ds(0, 256), :], s_owz, jnp.logical_and(x == k, z % 2 != y))
 
     lane2 = lax.broadcasted_iota(jnp.int32, (1024, 128), 1)
 
@@ -752,26 +735,31 @@
         dmix[:, pl.ds(mul(i * 384 + 128, 128), 128)] = dk.astype(bf16)
         dmix[:, pl.ds(mul(i * 384 + 256, 128), 128)] = dv.astype(bf16)
 
-    up_z(0)
+    up_z(0, 1)
+    for p in range(2):
+        wait_bytes(dmix.at[pl.ds(0, 384), pl.ds(0, 512)], ssem.at[s_dwz + p])
     pair_backward(0)
-    i_qwx, i_qwz = (take(2), take(2)), (take(4), take(4))
-    dw_away(n1, dmix, 0, 384, gf, xr_qkv, i_qwx[0])
+    i_qwx, i_qwz, s_qwx, s_qwz = (rtake(2), rtake(2)), rtake(2), stake(2), stake(2)
+    up_z(1, 0)
+    dw_away(n1, dmix, 0, 384, gf, xr_qkv, i_qwx[0], s_qwx, 1)
     pair_backward(1)
 
-    rs_sent(rs_s, i_g2)
+    rs_sent(rs_s, s_g2)
 
     def gn1_part(blk, ch, dst):
         dst[...] = nt(dmix[pl.ds(mul(blk * R + ch * RC, RC), RC), :], wqkv[...])
 
-    i_g1 = take(3 * CH)
-    up_z(1)
-    rs_run(gn1_part, rs_s, rs_r, rs_own, i_g1)
-    dw_away(n1, dmix, 384, 384, gf, xr_qkv, i_qwx[1])
+    i_g1, s_g1 = rtake(3 * CH), stake(CH)
+    up_z(1, 1)
+    rs_run(gn1_part, rs_s, rs_r, rs_own, i_g1, s_g1)
+    dw_away(n1, dmix, 384, 384, gf, xr_qkv, i_qwx[1], s_qwx + 1, 1)
     dw_keep(n1, dmix, 0, 768, own_a)
 
     def qkv_z(h):
         for hh in range(2):
-            dw_z(hh, h * 384, 384, xr_qkv, own_a, n2, 0, zr_qkv, fin_qkv, i_qwx[h], i_qwz[h])
+            dw_z(hh, h * 384, 384, xr_qkv, own_a, n2, 0, h * 384, zr_qkv, fin_qkv,
+                 i_qwx[h] + hh, i_qwz + h, s_qwz + h)
+        sent(n2.at[pl.ds(0, 384), pl.ds(0, 384)], s_qwz + h)
 
     for i in range(2):
         zi = y + 2 * i
@@ -791,9 +779,7 @@
             @pl.when(zi != z)
             def _():
                 n2[512 + i * 128 : 640 + i * 128, :] = total.astype(bf16)
-                rcopy(n2.at[pl.ds(512 + i * 128, 128), :], zr_out.at[dz - 1], {"seq": zi * 2 + x}, i_owz + dz).start()
-
-        sent(n2.at[pl.ds(512, 128), :], i_owz + dz, jnp.logical_and(x == k, zi != z))
+                rcopy(n2.at[pl.ds(512 + i * 128, 128), :], zr_out.at[dz - 1], {"seq": zi * 2 + x}, i_owz, s_owz).start()
 
     qkv_z(0)
     for ch in range(CH):
@@ -823,26 +809,27 @@
             gmat[r : r + 1, pl.ds(mul((ctx + 4 * i) * 128, 128), 128)] = v
     for s in range(8):
         sg[s] = gmat[:, s * 128 : (s + 1) * 128]
-    i_sgx, i_sgz, i_sgc = take(4), take(4), take(4)
+    i_sgx, i_sgz, i_sgc, s_sgx, s_sgz, s_sgc = rtake(), rtake(), rtake(), stake(), stake(), stake()
     for j in range(4):
         src = sg.at[j * 2 + (x + 1) % 2]
-        rcopy(src, sgx.at[j], xpeer, i_sgx + j).start()
-        sent(src, i_sgx + j)
+        rcopy(src, sgx.at[j], xpeer, i_sgx, s_sgx).start()
+    sent(sgx, s_sgx)
 
     qkv_z(1)
-    for j in range(4):
-        rcopy(sg.at[j], sgx.at[j], xpeer, i_sgx + j).wait_recv()
+    wait_bytes(sgx, rsem.at[i_sgx])
     for d in (1, 2, 3):
         zz = (z + d) % 4
         sgs[d - 1] = sg[zz * 2 + x] + sgx[zz]
-        rcopy(sgs.at[d - 1], sgz.at[d - 1], zpeer(d), i_sgz + d).start()
-        sent(sgs.at[d - 1], i_sgz + d)
-
-    dw_end(0, D, zr_down, fin_down, i_dwz)
+        rcopy(sgs.at[d - 1], sgz.at[d - 1], zpeer(d), i_sgz, s_sgz).start()
+    sent(sgs, s_sgz)
+
+    for p in range(2):
+        dw_end(p * 512, 512, zr_down, fin_down, i_dwz + p)
     l_dd = next(lids)
     pltpu.make_async_copy(fin_down, o_ddown, lsem.at[l_dd]).start()
-    dw_end(0, D, zr_up, fin_up, i_uwz)
-    i_uf, i_qf, i_of = take(4), (take(4), take(4)), take(4)
+    for p in range(2):
+        dw_end(p * 512, 512, zr_up, fin_up, i_uwz + p)
+    i_uf, i_qf, i_of, s_uf, s_qf, s_of = rtake(), rtake(2), rtake(), stake(), stake(2), stake()
 
     def up_piece(fin, c, s):
         return (fin.at[pl.ds(mul(c * 32, 32), 32), pl.ds(s * 128, 128)],
@@ -851,8 +838,8 @@
     for d in (1, 2, 3):
         for s in range(8):
             a, b = up_piece(fin_up, (ctx + d) % 4, s)
-            rcopy(a, b, cpeer(d), i_uf + d).start()
-        sent(fin_up.at[pl.ds(0, 32), :], i_uf + d)
+            rcopy(a, b, cpeer(d), i_uf, s_uf).start()
+    sent(fin_up.at[pl.ds(0, 96), :], s_uf)
     mine32 = pl.ds(mul(ctx * 32, 32), 32)
     l_up = next(lids)
     for s in range(8):
@@ -863,16 +850,14 @@
 
     @pl.when(ctx == t)
     def _():
-        for d in (1, 2, 3):
-            wait_bytes(zr_out.at[d - 1], rsem.at[i_owz + d])
+        wait_bytes(zr_out, rsem.at[i_owz])
         fin_out[...] += (zr_out[0].astype(f32) + zr_out[1].astype(f32)) + zr_out[2].astype(f32)
         for d in (1, 2, 3):
             src = fin_out.at[pl.ds(mul(((ctx + d) % 4) * 32, 32), 32), :]
-            rcopy(src, o_dout, cpeer(d), i_of + d).start()
+            rcopy(src, o_dout, cpeer(d), i_of, s_of).start()
         pltpu.make_async_copy(fin_out.at[mine32, :], o_dout, lsem.at[l_do]).start()
 
-    for d in (1, 2, 3):
-        sent(fin_out.at[pl.ds(0, 32), :], i_of + d, ctx == t)
+    sent(fin_out.at[pl.ds(0, 96), :], s_of, ctx == t)
 
     for ch in range(CH):
         rs_wait(rt_s, rt_r, i_ff, ch)
@@ -889,55 +874,50 @@
     l_t = next(lids)
     pltpu.make_async_copy(st_out, o_out, lsem.at[l_t]).start()
 
-    for d in (1, 2, 3):
-        wait_bytes(sgz.at[d - 1], rsem.at[i_sgz + d])
+    wait_bytes(sgz, rsem.at[i_sgz])
     sgf[...] = sg[seq] + sgx[z] + (sgz[0] + sgz[1] + sgz[2])
     for j in range(3):
         v = jnp.sum(stat[j * 8 : (j + 1) * 8, :], axis=0, keepdims=True)
         sgf[9 + j : 10 + j, :] = jnp.broadcast_to(jnp.sum(v, axis=1, keepdims=True), (1, 128))
     for d in (1, 2, 3):
-        rcopy(sgf, sgc.at[d], cpeer(d), i_sgc + d).start()
-        sent(sgf, i_sgc + d)
+        rcopy(sgf, sgc.at[d], cpeer(d), i_sgc, s_sgc).start()
+    sent(sgc.at[pl.ds(1, 3)], s_sgc)
 
     l_dq = []
     for h in range(2):
-        dw_end(h * 384, 384, zr_qkv, fin_qkv, i_qwz[h])
+        dw_end(h * 384, 384, zr_qkv, fin_qkv, i_qwz + h)
         pieces = list(qkv_pieces(ctx))[3 * h : 3 * h + 3]
         for d in (1, 2, 3):
             c2 = (ctx + d) % 4
             for a, b in pieces:
-                rcopy(fin_qkv.at[pl.ds(mul(c2 * 32, 32), 32), b], o_dqkv.at[:, a], cpeer(d), i_qf[h] + d).start()
-            sent(fin_qkv.at[pl.ds(0, 32), pl.ds(0, 384)], i_qf[h] + d)
+                rcopy(fin_qkv.at[pl.ds(mul(c2 * 32, 32), 32), b], o_dqkv.at[:, a], cpeer(d), i_qf + h, s_qf + h).start()
+        sent(fin_qkv.at[pl.ds(0, 96), pl.ds(0, 384)], s_qf + h)
         l_dq.append(next(lids))
         for a, b in pieces:
             pltpu.make_async_copy(fin_qkv.at[mine32, b], o_dqkv.at[:, a], lsem.at[l_dq[h]]).start()
 
-    for d in (1, 2, 3):
-        wait_bytes(sgc.at[d], rsem.at[i_sgc + d])
+    wait_bytes(sgc.at[pl.ds(1, 3)], rsem.at[i_sgc])
     o_small[...] = sgf[...] + jnp.where(rowid != 8, sgc[1] + sgc[2] + sgc[3], 0.0)
 
     @pl.when(ctx != t)
     def _():
-        wait_bytes(fin_out.at[pl.ds(0, 32), :], rsem.at[i_of + (ctx - t + 4) % 4])
+        wait_bytes(fin_out.at[pl.ds(0, 32), :], rsem.at[i_of])
 
     @pl.when(ctx == t)
     def _():
         wait_bytes(fin_out.at[pl.ds(0, 32), :], lsem.at[l_do])
 
-    for d in (1, 2, 3):
-        wait_bytes(fin_up.at[pl.ds(0, 32), :], rsem.at[i_uf + d])
-        for h in range(2):
-            wait_bytes(fin_qkv.at[pl.ds(0, 32), pl.ds(0, 384)], rsem.at[i_qf[h] + d])
-    rs_sent(rs_s, i_g1)
-    rs_sent(rt_s, i_ff)
-    for block, i in ((qkv_block, i_qr), (up_block, i_ur), (down_block, i_dr)):
-        relay_sent(block, i)
+    wait_bytes(fin_up.at[pl.ds(0, 96), :], rsem.at[i_uf])
+    for h in range(2):
+        wait_bytes(fin_qkv.at[pl.ds(0, 96), pl.ds(0, 384)], rsem.at[i_qf + h])
+    rs_sent(rs_s, s_g1)
+    rs_sent(rt_s, s_ff)
     flush()
     for ref, i in ((st_grad, l_g), (st_out, l_t), (fin_down, l_dd), (fin_up.at[pl.ds(0, 32), :], l_up),
                    (fin_qkv.at[pl.ds(0, 32), pl.ds(0, 384)], l_dq[0]),
                    (fin_qkv.at[pl.ds(0, 32), pl.ds(0, 384)], l_dq[1])):
         wait_bytes(ref, lsem.at[i])
-    assert next(ids) <= NSEM, next(ids)
+    assert next(rids) == NRECV and next(sids) == NSEND and next(lids) == NLOCAL
 
 
 def finish_kernel(length_ref, sums, *refs):
@@ -983,9 +963,9 @@
             v(bf16, R, D), v(f32, R, D), v(f32, 128, D),
             v(f32, 8, 16, 128), v(f32, 4, 16, 128), v(f32, 3, 16, 128), v(f32, 3, 16, 128),
             v(f32, 16, 128), v(f32, 4, 16, 128), v(f32, 8, 8, D), v(f32, 16, D), v(f32, 24, D), v(f32, 8, 768),
-            pltpu.SemaphoreType.DMA((16,)),
-            pltpu.SemaphoreType.DMA((NSEM,)),
-            pltpu.SemaphoreType.DMA((NSEM,)),
+            pltpu.SemaphoreType.DMA((NLOCAL,)),
+            pltpu.SemaphoreType.DMA((NSEND,)),
+            pltpu.SemaphoreType.DMA((NRECV,)),
         ]
 
     def on_device(tokens, lengths, cotangent, g1, b1, wq, qb, vb, wo, ob, g2, b2, wu, ub, wd, db):
@@ -1001,7 +981,7 @@
             block_kernel,
             out_shape=(sds((R, D), bf16), sds((R, D), f32), sds((32, 3 * D), f32), sds((32, D), f32),
                        sds((32, 4 * D), f32), sds((128, D), f32), sds((16, 128), f32)),
-            in_specs=[pl.BlockSpec(memory_space=pltpu.SMEM)] + [vm] * 7,
+            in_specs=[pl.BlockSpec(memory_space=pltpu.SMEM)] + [vm] * 3 + [pl.BlockSpec(memory_space=pl.ANY)] * 4,
             out_specs=tuple([pl.BlockSpec(memory_space=pl.ANY)] * 6 + [vm]),
             scratch_shapes=scratch(),
             compiler_params=pltpu.CompilerParams(

time: 185 us -> 181 us (0.978)
  Pallas kernels: 180 us -> 175 us
    pallas_call x1, Pallas kernels: 175 us -> 170 us  [on_device(): pl.pallas_call(block_kernel, out_shape=(sds((R, D), bf16), sds((R, D), f3...]
where the time goes in v5:
time: 181 us; the launch traced here: 178 us
  Pallas kernels  175 us (97%)
    pallas_call x1, Pallas kernels, on_device(): pl.pallas_call(block_kernel, out_shape=(sds((R, D), bf16), sds((R, D), f3...  170 us
    pallas_call x1, Pallas kernels, on_device(): pl.pallas_call(finish_kernel, out_shape=tuple((sds(v.shape, v.dtype) for...  4.25 us

profile of v5, /device:TPU:21, one launch (start us, length us, event | category | flops | bytes accessed | tf_op | source)
XLA Modules:
  0.0 178.3 jit_solution(16782292288694784384)
XLA Ops:
  1.3 0.0 copy-start.8
  1.3 0.6 copy-done.8
  2.0 0.0 copy-start.7
  2.0 0.0 copy-start.3
  2.0 0.0 copy-start.4
  2.0 0.0 copy-start.5
  2.0 0.0 copy-start.6
  2.0 0.0 copy-start
  2.0 0.0 copy-start.1
  2.0 0.0 copy-start.2
  2.0 0.1 pad.2.clone
  2.1 0.5 copy-done.7
  2.6 0.0 copy-done.3
  2.6 0.0 copy-done.4
  2.7 0.0 copy-done.5
  2.7 0.0 copy-done.6
  2.7 0.0 copy-done
  2.7 0.0 copy-done.1
  2.7 0.0 copy-done.2
  2.8 0.1 tile.10
  2.9 0.7 maximum_maximum_fusion.small
  3.5 170.4 %block.1 = (bf16[256,1024]{1,0:T(8,128)(2,1)}, f32[256,1024]{1,0:T(8,128)}, f32[32,3072]{1,0:T(8,128)}, f32[32,1024]{1,0:T(8,128)}, f32[32,4096]{1,0:T(8,128)}, /*index=5*/f32[128,1024]{1,0:T(8,128)}, f32[16,128]{1,0:T(8,128)}) custom-call(s32[1]{0:T(128)S(6)} %copy.32.length_ref, bf16[256,1024]{1,0:T(8,128)(2,1)} %bitcast.15, bf16[256,1024]{1,0:T(8,128)(2,1)} %bitcast.16, ...), custom_call_target="tpu_custom_call" | custom-call | tf_op jit(solution)/shard_map/block/pallas_call | solution.py:980
  173.9 4.2 %finish.1 = (bf16[256,1024]{1,0:T(8,128)(2,1)}, f32[256,1024]{1,0:T(8,128)}, f32[32,3072]{1,0:T(8,128)}, f32[32,1024]{1,0:T(8,128)}, f32[32,4096]{1,0:T(8,128)},...) custom-call(s32[1]{0:T(128)S(6)} %copy.32.length_ref, ...), custom_call_target="tpu_custom_call" | custom-call | tf_op jit(solution)/shard_map/finish/pallas_call | solution.py:993
  (6 shorter events, 0.1 us)
Async XLA Ops:
  1.3 0.7 copy-start.8
  2.0 0.7 copy-start.7
  2.0 0.7 copy-start.3
  2.0 0.7 copy-start.4
  2.0 0.7 copy-start.5
  2.0 0.7 copy-start.6
  2.0 0.7 copy-start
  2.0 0.7 copy-start.1
  2.0 0.7 copy-start.2

commit v6 on v5

--- a/solution.py
+++ b/solution.py
@@ -383,20 +383,21 @@
             q0 = pl.ds(mul(qb * 256, 256), 256)
             qblk = qkv[q0, pl.ds(mul(i * 384, 128), 128)]
 
-            def scores(kb, best):
+            def scores(kb, best, diagonal=False):
                 k0 = pl.ds(mul(kb * 256, 256), 256)
                 kblk = qkv[k0, pl.ds(mul(i * 384 + 128, 128), 128)]
                 new = []
                 for j in range(2):
                     b = own_b[j * 256 : (j + 1) * 256, pl.ds(mul(kb * 128, 128), 128)]
                     sc = nt(half(kblk, j), qblk) * (0.125 * LOG2E) + jnp.concatenate([b, b], axis=1)
-                    sc = jnp.where(krow + kb * 256 <= qcol + qb * 256, sc, -1e30)
+                    if diagonal:
+                        sc = jnp.where(krow <= qcol, sc, -1e30)
                     own_a[j * 256 : (j + 1) * 256, k0] = sc
                     new.append(jnp.maximum(best[j], jnp.max(sc.reshape(32, 8, 256), axis=0)))
                 return tuple(new)
 
             low = jnp.full((8, 256), -3e38, f32)
-            best = lax.fori_loop(0, qb + 1, scores, (low, low))
+            best = scores(qb, lax.fori_loop(0, qb, scores, (low, low)), diagonal=True)
             top = [jnp.max(b, axis=0, keepdims=True) for b in best]
 
             def weigh(kb, carry):
@@ -874,15 +875,6 @@
     l_t = next(lids)
     pltpu.make_async_copy(st_out, o_out, lsem.at[l_t]).start()
 
-    wait_bytes(sgz, rsem.at[i_sgz])
-    sgf[...] = sg[seq] + sgx[z] + (sgz[0] + sgz[1] + sgz[2])
-    for j in range(3):
-        v = jnp.sum(stat[j * 8 : (j + 1) * 8, :], axis=0, keepdims=True)
-        sgf[9 + j : 10 + j, :] = jnp.broadcast_to(jnp.sum(v, axis=1, keepdims=True), (1, 128))
-    for d in (1, 2, 3):
-        rcopy(sgf, sgc.at[d], cpeer(d), i_sgc, s_sgc).start()
-    sent(sgc.at[pl.ds(1, 3)], s_sgc)
-
     l_dq = []
     for h in range(2):
         dw_end(h * 384, 384, zr_qkv, fin_qkv, i_qwz + h)
@@ -895,6 +887,15 @@
         l_dq.append(next(lids))
         for a, b in pieces:
             pltpu.make_async_copy(fin_qkv.at[mine32, b], o_dqkv.at[:, a], lsem.at[l_dq[h]]).start()
+
+    wait_bytes(sgz, rsem.at[i_sgz])
+    sgf[...] = sg[seq] + sgx[z] + (sgz[0] + sgz[1] + sgz[2])
+    for j in range(3):
+        v = jnp.sum(stat[j * 8 : (j + 1) * 8, :], axis=0, keepdims=True)
+        sgf[9 + j : 10 + j, :] = jnp.broadcast_to(jnp.sum(v, axis=1, keepdims=True), (1, 128))
+    for d in (1, 2, 3):
+        rcopy(sgf, sgc.at[d], cpeer(d), i_sgc, s_sgc).start()
+    sent(sgc.at[pl.ds(1, 3)], s_sgc)
 
     wait_bytes(sgc.at[pl.ds(1, 3)], rsem.at[i_sgc])
     o_small[...] = sgf[...] + jnp.where(rowid != 8, sgc[1] + sgc[2] + sgc[3], 0.0)

time: 181 us -> 180 us (level)
  no operation moved by 1% of the time
where the time goes in v6:
time: 180 us; the launch traced here: 177 us
  Pallas kernels  174 us (97%)
    pallas_call x1, Pallas kernels, on_device(): pl.pallas_call(block_kernel, out_shape=(sds((R, D), bf16), sds((R, D), f3...  169 us
    pallas_call x1, Pallas kernels, on_device(): pl.pallas_call(finish_kernel, out_shape=tuple((sds(v.shape, v.dtype) for...  4.25 us

profile of v6, /device:TPU:21, one launch (start us, length us, event | category | flops | bytes accessed | tf_op | source)
XLA Modules:
  0.0 177.3 jit_solution(16983813008456434566)
XLA Ops:
  1.3 0.0 copy-start.8
  1.3 0.6 copy-done.8
  2.0 0.0 copy-start.7
  2.0 0.0 copy-start.3
  2.0 0.0 copy-start.4
  2.0 0.0 copy-start.5
  2.0 0.0 copy-start.6
  2.0 0.0 copy-start
  2.0 0.0 copy-start.1
  2.0 0.0 copy-start.2
  2.0 0.1 pad.2.clone
  2.1 0.5 copy-done.7
  2.6 0.0 copy-done.3
  2.6 0.0 copy-done.4
  2.7 0.0 copy-done.5
  2.7 0.0 copy-done.6
  2.7 0.0 copy-done
  2.7 0.0 copy-done.1
  2.7 0.0 copy-done.2
  2.8 0.1 tile.10
  2.9 0.7 maximum_maximum_fusion.small
  3.5 169.3 %block.1 = (bf16[256,1024]{1,0:T(8,128)(2,1)}, f32[256,1024]{1,0:T(8,128)}, f32[32,3072]{1,0:T(8,128)}, f32[32,1024]{1,0:T(8,128)}, f32[32,4096]{1,0:T(8,128)}, /*index=5*/f32[128,1024]{1,0:T(8,128)}, f32[16,128]{1,0:T(8,128)}) custom-call(s32[1]{0:T(128)S(6)} %copy.32.length_ref, bf16[256,1024]{1,0:T(8,128)(2,1)} %bitcast.15, bf16[256,1024]{1,0:T(8,128)(2,1)} %bitcast.16, ...), custom_call_target="tpu_custom_call" | custom-call | tf_op jit(solution)/shard_map/block/pallas_call | solution.py:981
  172.9 4.2 %finish.1 = (bf16[256,1024]{1,0:T(8,128)(2,1)}, f32[256,1024]{1,0:T(8,128)}, f32[32,3072]{1,0:T(8,128)}, f32[32,1024]{1,0:T(8,128)}, f32[32,4096]{1,0:T(8,128)},...) custom-call(s32[1]{0:T(128)S(6)} %copy.32.length_ref, ...), custom_call_target="tpu_custom_call" | custom-call | tf_op jit(solution)/shard_map/finish/pallas_call | solution.py:994
  (6 shorter events, 0.1 us)
Async XLA Ops:
  1.3 0.7 copy-start.8
  2.0 0.7 copy-start.7
  2.0 0.7 copy-start.3
  2.0 0.7 copy-start.4
  2.0 0.7 copy-start.5
  2.0 0.7 copy-start.6
  2.0 0.7 copy-start
  2.0 0.7 copy-start.1
  2.0 0.7 copy-start.2
